TPU v7x, 32 devices: a whole 2x2x4 slice. The times are simulated.
32 devices in a mesh: ang: 4 (over y, x), gy: 2 (over core), gx: 4 (over z).
Axes of the slice: x: 2, y: 2, z: 4, core: 2. Of those that a mesh axis runs over, the one named last changes fastest.
Arguments:
- spectrum_data: bfloat16 [2, 16, 16, 2048], P(None, None, 'gy', 'ang'), may hold values from -6 to 6
- offsets: int32 [2048], P('ang'), may hold values from 0 to 1020
- view_index: int32 [2048], P('ang'), may hold values from 0 to 1499
- kernel: float32 [4, 2048], P(None, 'ang'), may hold values from 0.25 to 1
- view_weight: float32 [1500], replicated, may hold values from 0.5 to 2
- volume: float32 [16, 16, 4096], P('ang', 'gy', 'gx'), may hold values from -6 to 6
- multiplier: float32 [16, 16, 4096], P('ang', 'gy', 'gx'), may hold values from -4 to 4
Outputs:
- denoised: float32 [16, 16, 4096], P('ang', 'gy', 'gx')
Inputs may be any that keep to these rules, and one draw needn't show every extreme that they name: `offsets`: each offset is a cell of its sample's block of 1024 frequencies with the three cells after it in the block too.
All inputs are finite; a program needn't handle non-finite values.
Results may differ from a plain program's by a relative error of at most 0.0032.
Values sent between devices are 32-bit elements; how exact they have to be, the bound alone decides.
No kernel may reach another device: no remote copies, remote signals or barrier semaphores. Data moves between devices by JAX's collectives and lax.ppermute only.
A program may use at most 64 MiB of HBM per device.

v0:
```python
import math

import jax
import jax.numpy as jnp
from jax import lax
from jax.sharding import PartitionSpec as P

NX = 4096
TV_STEPS = 4


smooth_weight = 0.5
dual_step = 1.0 / 12.0


def passed_along(block, axis, distance):
    devices = range(lax.axis_size(axis))
    route = [(i - distance, i) for i in devices if i - distance in devices]
    return lax.ppermute(block, axis, route)


def wave_table(freq_first, freq_count, cell_first, cell_count):
    freq_ids = freq_first + jnp.arange(freq_count, dtype=jnp.int32)
    cell_ids = cell_first + jnp.arange(cell_count, dtype=jnp.int32)
    phase_cells = freq_ids[:, None] * cell_ids[None, :] % NX
    phase_angle = phase_cells.astype(jnp.float32) * (2.0 * math.pi / NX)
    return jnp.concatenate([jnp.cos(phase_angle), -jnp.sin(phase_angle)], axis=0).astype(
        jnp.bfloat16
    )


def spread_block(offsets, view_index, kernel, view_weight, block_size):
    cell_ids = jnp.arange(block_size, dtype=jnp.int32)
    spread_sum = jnp.zeros((offsets.shape[0], block_size), jnp.float32)
    for tap_index in range(kernel.shape[0]):
        spread_sum = spread_sum + jnp.where(
            cell_ids[None, :] == (offsets + tap_index)[:, None],
            kernel[tap_index][:, None],
            jnp.float32(0.0),
        )
    view_ids = jnp.arange(view_weight.shape[0], dtype=jnp.int32)
    weights = jnp.sum(
        jnp.where(view_index[:, None] == view_ids[None, :], view_weight[None, :], jnp.float32(0.0)),
        axis=1,
    )
    return (weights[:, None] * spread_sum).astype(jnp.bfloat16)


def per_device(spectrum_data, offsets, view_index, kernel, view_weight, volume, multiplier):
    block_size = NX // lax.axis_size("ang")
    planes, line_count, columns = volume.shape
    spread = spread_block(offsets, view_index, kernel, view_weight, block_size)
    wave_rows = wave_table(
        lax.axis_index("ang") * block_size, block_size, lax.axis_index("gx") * columns, columns
    )
    row_count = spectrum_data.shape[1]
    flat_rows = row_count * line_count
    gridded = jnp.dot(
        spectrum_data.reshape(2 * flat_rows, spectrum_data.shape[3]),
        spread,
        preferred_element_type=jnp.float32,
    ).astype(jnp.bfloat16)
    joined = jnp.concatenate([gridded[:flat_rows], gridded[flat_rows:]], axis=1)
    full_term = jnp.dot(joined, wave_rows, preferred_element_type=jnp.float32).reshape(
        row_count, line_count, columns
    )
    column_part = lax.psum_scatter(full_term, "ang", scatter_dimension=2, tiled=True)
    back = lax.all_to_all(column_part, "ang", split_axis=0, concat_axis=2, tiled=True)
    back = back * NX ** (-0.5)
    source = volume - back + multiplier
    scaled = source / smooth_weight
    plane_end = (
        lax.axis_index("ang") * planes + jnp.arange(planes, dtype=jnp.int32)
        == planes * lax.axis_size("ang") - 1
    )
    row_end = (
        lax.axis_index("gy") * line_count + jnp.arange(line_count, dtype=jnp.int32)
        == line_count * lax.axis_size("gy") - 1
    )
    cell_end = (
        lax.axis_index("gx") * columns + jnp.arange(columns, dtype=jnp.int32)
        == columns * lax.axis_size("gx") - 1
    )
    flow_field = jnp.zeros((3, planes, line_count, columns), jnp.float32)
    for repeat in range(TV_STEPS + 1):
        lower_plane = passed_along(flow_field[0, -1:], "ang", 1)
        lower_row = passed_along(flow_field[1, :, -1:], "gy", 1)
        lower_cell = passed_along(flow_field[2, :, :, -1:], "gx", 1)
        plane_part = flow_field[0] - jnp.concatenate([lower_plane, flow_field[0, :-1]], axis=0)
        row_part = flow_field[1] - jnp.concatenate([lower_row, flow_field[1, :, :-1]], axis=1)
        cell_part = flow_field[2] - jnp.concatenate([lower_cell, flow_field[2, :, :, :-1]], axis=2)
        local_div = plane_part + row_part + cell_part
        if repeat == TV_STEPS:
            return source - smooth_weight * local_div
        target = local_div - scaled
        upper_plane = passed_along(target[:1], "ang", -1)
        upper_row = passed_along(target[:, :1], "gy", -1)
        upper_cell = passed_along(target[:, :, :1], "gx", -1)
        slope_plane = jnp.where(
            plane_end[:, None, None],
            jnp.float32(0.0),
            jnp.concatenate([target[1:], upper_plane], axis=0) - target,
        )
        slope_row = jnp.where(
            row_end[None, :, None],
            jnp.float32(0.0),
            jnp.concatenate([target[:, 1:], upper_row], axis=1) - target,
        )
        slope_cell = jnp.where(
            cell_end[None, None, :],
            jnp.float32(0.0),
            jnp.concatenate([target[:, :, 1:], upper_cell], axis=2) - target,
        )
        slope_norm = jnp.sqrt(
            slope_plane * slope_plane + slope_row * slope_row + slope_cell * slope_cell
        )
        flow_field = (flow_field + dual_step * jnp.stack([slope_plane, slope_row, slope_cell])) / (
            1.0 + dual_step * slope_norm
        )
    return source


def solution(mesh):
    placed = (
        P(None, None, "gy", "ang"),
        P("ang"),
        P("ang"),
        P(None, "ang"),
        P(),
        P("ang", "gy", "gx"),
        P("ang", "gy", "gx"),
    )
    return jax.shard_map(
        per_device, mesh=mesh, in_specs=placed, out_specs=P("ang", "gy", "gx"), check_vma=False
    )
```

profile of v0, /device:TPU:0, one launch (start us, length us, event | category | flops | bytes accessed | tf_op | source)
XLA Modules:
  0.0 158.7 jit_solution(11166117643686291913)
XLA Ops:
  9.2 2.2 %fusion.10 = bf16[256,1024]{0,1:T(8,128)(2,1)S(1)} fusion(bf16[256,512]{1,0:T(8,128)(2,1)S(1)} %bitcast.172, f32[512]{0:T(512)S(1)} %bitcast.181, s32[512]{0:T(512)S(1)} %get-tuple-element.32, f32[512]{0:T(512)S(1)} %bitcast.182, s32[512]{0:T(512)S(1)} %get-tuple-element.33, f32[512]{0:T(512)S(1)} %bitcast.180, s32[512]{0:T(512)S(1)} %get-tuple-element.31, ...), kind=kOutput, calls=%fused_computation.23 | convolution fusion | flops 275513344 | bytes 804864 | tf_op jit(solution)/shard_map/dot_general | solution.py:58
  11.5 17.4 %cosine_convert_fusion = (bf16[1024,1024]{1,0:T(8,128)(2,1)S(1)}, bf16[1024,1024]{1,0:T(8,128)(2,1)S(1)}) fusion(s32[1024]{0:T(1024)S(1)} %get-tuple-element.34, s32[1024]{0:T(1024)S(1)} %get-tuple-element.35), kind=kLoop, calls=%fused_computation.13 | loop fusion | flops 17825792 | bytes 4202496 | tf_op jit(solution)/shard_map/convert
  29.0 1.6 fusion.7
  30.6 4.9 %collective-permute-start = (f32[1,8,1024]{2,1,0:T(8,128)S(1)}, f32[1,8,1024]{2,1,0:T(8,128)S(1)}, u32[]{:S(2)}, u32[]{:S(2)}) collective-permute-start(f32[1,8,1024]{2,1,0:T(8,128)S(1)} %squeeze.120), channel_id=1, source_target_pairs={{0,8},{8,16},{16,24},{1,9},{9,17},{17,25},{2,10},{10,18},{18,26},{... | collective-permute-start | bytes 98312 | tf_op jit(solution)/shard_map/ppermute | solution.py:19
  35.5 1.5 collective-permute-start.1
  37.0 3.5 %collective-permute-start.2 = (f32[4,8,1]{2,1,0:T(8,128)S(1)}, f32[4,8,1]{2,1,0:T(8,128)S(1)}, u32[]{:S(2)}, u32[]{:S(2)}) collective-permute-start(f32[4,8,1]{2,1,0:T(8,128)S(1)} %squeeze.122), channel_id=1, source_target_pairs={{0,1},{1,2},{2,3},{4,5},{5,6},{6,7},{8,9},{9,10},{10,11},{12,13},{... | collective-permute-start | bytes 392 | tf_op jit(solution)/shard_map/ppermute | solution.py:19
  40.5 18.1 %reduce-scatter.2.cloned.1.call-done = f32[16,8,256]{2,1,0:T(8,128)} async-done(((f32[16,8,1024]{2,1,0:T(8,128)}), f32[16,8,256]{2,1,0:T(8,128)}) %reduce-scatter.2.cloned.1.call-update) | async-done | bytes 131088 | tf_op jit(solution)/shard_map/reduce_scatter | solution.py:67
  58.6 3.3 %all-to-all-start = ((f32[16,8,256]{2,1,0:T(8,128)}), f32[16,8,256]{2,1,0:T(8,128)S(1)}, u32[]{:S(2)}, u32[]{:S(2)}) async-start(f32[16,8,256]{2,1,0:T(8,128)} %reduce-scatter.2.cloned.1.call-done), calls=%async_computation.1 | async-start | bytes 262144 | tf_op jit(solution)/shard_map/all_to_all | solution.py:68
  61.9 5.0 %all-to-all-done = f32[16,8,256]{2,1,0:T(8,128)S(1)} async-done(((f32[16,8,256]{2,1,0:T(8,128)}), f32[16,8,256]{2,1,0:T(8,128)S(1)}, u32[]{:S(2)}, u32[]{:S(2)}) %all-to-all-start) | async-done | bytes 131104 | tf_op jit(solution)/shard_map/all_to_all | solution.py:68
  67.1 1.3 collective-permute-start.3
  68.4 1.3 collective-permute-start.4
  69.7 1.3 collective-permute-start.5
  71.1 4.2 %collective-permute-done.5 = f32[4,8,1]{2,1,0:T(8,128)S(1)} collective-permute-done((f32[4,8,1]{2,1,0:T(8,128)S(1)}, f32[4,8,1]{2,1,0:T(8,128)S(1)}, u32[]{:S(2)}, u32[]{:S(2)}) %collective-permute-start.5) | collective-permute-done | bytes 160 | tf_op jit(solution)/shard_map/ppermute | solution.py:19
  75.8 4.5 %collective-permute-start.6 = (f32[1,8,1024]{2,1,0:T(8,128)S(1)}, f32[1,8,1024]{2,1,0:T(8,128)S(1)}, u32[]{:S(2)}, u32[]{:S(2)}) collective-permute-start(f32[1,8,1024]{2,1,0:T(8,128)S(1)} %slice_bitcast_fusion.27), channel_id=1, source_target_pairs={{0,8},{8,16},{16,24},{1,9},{9,17},{17,25},{2,10},{10,18},{18,26},{... | collective-permute-start | bytes 98312 | tf_op jit(solution)/shard_map/ppermute | solution.py:19
  80.4 1.7 %collective-permute-start.7 = (f32[4,1,1024]{2,1,0:T(1,128)S(1)}, f32[4,1,1024]{2,1,0:T(1,128)S(1)}, u32[]{:S(2)}, u32[]{:S(2)}) collective-permute-start(f32[4,1,1024]{2,1,0:T(1,128)S(1)} %slice_bitcast_fusion.31), channel_id=1, source_target_pairs={{0,4},{1,5},{2,6},{3,7},{8,12},{9,13},{10,14},{11,15},{16,20},{17,... | collective-permute-start | bytes 49160 | tf_op jit(solution)/shard_map/ppermute | solution.py:19
  82.1 3.4 %collective-permute-start.8 = (f32[4,8,1]{1,0,2:T(4,128)S(1)}, f32[4,8,1]{1,0,2:T(4,128)S(1)}, u32[]{:S(2)}, u32[]{:S(2)}) collective-permute-start(f32[4,8,1]{1,0,2:T(4,128)S(1)} %bitcast.175), channel_id=1, source_target_pairs={{0,1},{1,2},{2,3},{4,5},{5,6},{6,7},{8,9},{9,10},{10,11},{12,13},{... | collective-permute-start | bytes 392 | tf_op jit(solution)/shard_map/ppermute | solution.py:19
  87.0 1.3 collective-permute-start.9
  88.3 1.3 collective-permute-start.10
  91.1 4.5 %collective-permute-done.11 = f32[4,8,1]{2,1,0:T(8,128)S(1)} collective-permute-done((f32[4,8,1]{2,1,0:T(8,128)S(1)}, f32[4,8,1]{2,1,0:T(8,128)S(1)}, u32[]{:S(2)}, u32[]{:S(2)}) %collective-permute-start.11) | collective-permute-done | bytes 160 | tf_op jit(solution)/shard_map/ppermute | solution.py:19
  96.1 4.5 %collective-permute-start.12 = (f32[1,8,1024]{2,1,0:T(8,128)S(1)}, f32[1,8,1024]{2,1,0:T(8,128)S(1)}, u32[]{:S(2)}, u32[]{:S(2)}) collective-permute-start(f32[1,8,1024]{2,1,0:T(8,128)S(1)} %slice_bitcast_fusion.26), channel_id=1, source_target_pairs={{0,8},{8,16},{16,24},{1,9},{9,17},{17,25},{2,10},{10,18},{18,26},{... | collective-permute-start | bytes 98312 | tf_op jit(solution)/shard_map/ppermute | solution.py:19
  100.6 1.9 %collective-permute-start.13 = (f32[4,1,1024]{2,1,0:T(1,128)S(1)}, f32[4,1,1024]{2,1,0:T(1,128)S(1)}, u32[]{:S(2)}, u32[]{:S(2)}) collective-permute-start(f32[4,1,1024]{2,1,0:T(1,128)S(1)} %slice_bitcast_fusion.30), channel_id=1, source_target_pairs={{0,4},{1,5},{2,6},{3,7},{8,12},{9,13},{10,14},{11,15},{16,20},{17,... | collective-permute-start | bytes 49160 | tf_op jit(solution)/shard_map/ppermute | solution.py:19
  102.5 3.8 %collective-permute-start.14 = (f32[4,8,1]{1,0,2:T(4,128)S(1)}, f32[4,8,1]{1,0,2:T(4,128)S(1)}, u32[]{:S(2)}, u32[]{:S(2)}) collective-permute-start(f32[4,8,1]{1,0,2:T(4,128)S(1)} %bitcast.176), channel_id=1, source_target_pairs={{0,1},{1,2},{2,3},{4,5},{5,6},{6,7},{8,9},{9,10},{10,11},{12,13},{... | collective-permute-start | bytes 392 | tf_op jit(solution)/shard_map/ppermute | solution.py:19
  111.9 4.5 %collective-permute-done.17 = f32[4,8,1]{2,1,0:T(8,128)S(1)} collective-permute-done((f32[4,8,1]{2,1,0:T(8,128)S(1)}, f32[4,8,1]{2,1,0:T(8,128)S(1)}, u32[]{:S(2)}, u32[]{:S(2)}) %collective-permute-start.17) | collective-permute-done | bytes 160 | tf_op jit(solution)/shard_map/ppermute | solution.py:19
  116.9 5.2 %collective-permute-start.18 = (f32[1,8,1024]{2,1,0:T(8,128)S(1)}, f32[1,8,1024]{2,1,0:T(8,128)S(1)}, u32[]{:S(2)}, u32[]{:S(2)}) collective-permute-start(f32[1,8,1024]{2,1,0:T(8,128)S(1)} %slice_bitcast_fusion.25), channel_id=1, source_target_pairs={{0,8},{8,16},{16,24},{1,9},{9,17},{17,25},{2,10},{10,18},{18,26},{... | collective-permute-start | bytes 98312 | tf_op jit(solution)/shard_map/ppermute | solution.py:19
  122.2 1.9 %collective-permute-start.19 = (f32[4,1,1024]{2,1,0:T(1,128)S(1)}, f32[4,1,1024]{2,1,0:T(1,128)S(1)}, u32[]{:S(2)}, u32[]{:S(2)}) collective-permute-start(f32[4,1,1024]{2,1,0:T(1,128)S(1)} %slice_bitcast_fusion.29), channel_id=1, source_target_pairs={{0,4},{1,5},{2,6},{3,7},{8,12},{9,13},{10,14},{11,15},{16,20},{17,... | collective-permute-start | bytes 49160 | tf_op jit(solution)/shard_map/ppermute | solution.py:19
  124.1 3.8 %collective-permute-start.20 = (f32[4,8,1]{1,0,2:T(4,128)S(1)}, f32[4,8,1]{1,0,2:T(4,128)S(1)}, u32[]{:S(2)}, u32[]{:S(2)}) collective-permute-start(f32[4,8,1]{1,0,2:T(4,128)S(1)} %bitcast.177), channel_id=1, source_target_pairs={{0,1},{1,2},{2,3},{4,5},{5,6},{6,7},{8,9},{9,10},{10,11},{12,13},{... | collective-permute-start | bytes 392 | tf_op jit(solution)/shard_map/ppermute | solution.py:19
  129.4 1.3 collective-permute-start.21
  130.7 1.3 collective-permute-start.22
  133.5 4.5 %collective-permute-done.23 = f32[4,8,1]{2,1,0:T(8,128)S(1)} collective-permute-done((f32[4,8,1]{2,1,0:T(8,128)S(1)}, f32[4,8,1]{2,1,0:T(8,128)S(1)}, u32[]{:S(2)}, u32[]{:S(2)}) %collective-permute-start.23) | collective-permute-done | bytes 160 | tf_op jit(solution)/shard_map/ppermute | solution.py:19
  138.6 5.4 %collective-permute-start.24 = (f32[1,8,1024]{2,1,0:T(8,128)S(1)}, f32[1,8,1024]{2,1,0:T(8,128)S(1)}, u32[]{:S(2)}, u32[]{:S(2)}) collective-permute-start(f32[1,8,1024]{2,1,0:T(8,128)S(1)} %slice_bitcast_fusion.24), channel_id=1, source_target_pairs={{0,8},{8,16},{16,24},{1,9},{9,17},{17,25},{2,10},{10,18},{18,26},{... | collective-permute-start | bytes 98312 | tf_op jit(solution)/shard_map/ppermute | solution.py:19
  144.0 1.9 %collective-permute-start.25 = (f32[4,1,1024]{2,1,0:T(1,128)S(1)}, f32[4,1,1024]{2,1,0:T(1,128)S(1)}, u32[]{:S(2)}, u32[]{:S(2)}) collective-permute-start(f32[4,1,1024]{2,1,0:T(1,128)S(1)} %slice_bitcast_fusion.28), channel_id=1, source_target_pairs={{0,4},{1,5},{2,6},{3,7},{8,12},{9,13},{10,14},{11,15},{16,20},{17,... | collective-permute-start | bytes 49160 | tf_op jit(solution)/shard_map/ppermute | solution.py:19
  145.9 3.8 %collective-permute-start.26 = (f32[4,8,1]{1,0,2:T(4,128)S(1)}, f32[4,8,1]{1,0,2:T(4,128)S(1)}, u32[]{:S(2)}, u32[]{:S(2)}) collective-permute-start(f32[4,8,1]{1,0,2:T(4,128)S(1)} %bitcast.178), channel_id=1, source_target_pairs={{0,1},{1,2},{2,3},{4,5},{5,6},{6,7},{8,9},{9,10},{10,11},{12,13},{... | collective-permute-start | bytes 392 | tf_op jit(solution)/shard_map/ppermute | solution.py:19
  (114 shorter events, 18.4 us)
Async XLA Ops:
  6.5 2.7 %copy-start = (bf16[2,16,8,512]{3,2,1,0:T(8,128)(2,1)S(1)}, bf16[2,16,8,512]{3,2,1,0:T(8,128)(2,1)}, u32[]{:S(2)}) copy-start(bf16[2,16,8,512]{3,2,1,0:T(8,128)(2,1)} %param.7) | copy-start | bytes 786436
  6.5 52.1 %reduce-scatter.2.cloned.1.call-start = ((), (), s32[]{:S(2)}) async-start(), calls=%async_computation.2 | async-start | bytes 655360 | tf_op jit(solution)/shard_map/reduce_scatter | solution.py:67
  29.0 38.0 %copy-start.1 = (f32[4,8,1024]{2,1,0:T(8,128)S(1)}, f32[4,8,1024]{2,1,0:T(8,128)}, u32[]{:S(2)}) copy-start(f32[4,8,1024]{2,1,0:T(8,128)} %param.13) | copy-start | bytes 393220
  29.0 38.0 %copy-start.2 = (f32[4,8,1024]{2,1,0:T(8,128)S(1)}, f32[4,8,1024]{2,1,0:T(8,128)}, u32[]{:S(2)}) copy-start(f32[4,8,1024]{2,1,0:T(8,128)} %param.12) | copy-start | bytes 393220
  30.6 36.4 %collective-permute-start = (f32[1,8,1024]{2,1,0:T(8,128)S(1)}, f32[1,8,1024]{2,1,0:T(8,128)S(1)}, u32[]{:S(2)}, u32[]{:S(2)}) collective-permute-start(f32[1,8,1024]{2,1,0:T(8,128)S(1)} %squeeze.120), channel_id=1, source_target_pairs={{0,8},{8,16},{16,24},{1,9},{9,17},{17,25},{2,10},{10,18},{18,26},{... | collective-permute-start | bytes 98312 | tf_op jit(solution)/shard_map/ppermute | solution.py:19
  35.5 31.4 %collective-permute-start.1 = (f32[4,1,1024]{2,1,0:T(1,128)S(1)}, f32[4,1,1024]{2,1,0:T(1,128)S(1)}, u32[]{:S(2)}, u32[]{:S(2)}) collective-permute-start(f32[4,1,1024]{2,1,0:T(1,128)S(1)} %squeeze.121), channel_id=1, source_target_pairs={{0,4},{1,5},{2,6},{3,7},{8,12},{9,13},{10,14},{11,15},{16,20},{17,... | collective-permute-start | bytes 49160 | tf_op jit(solution)/shard_map/ppermute | solution.py:19
  37.0 29.9 %collective-permute-start.2 = (f32[4,8,1]{2,1,0:T(8,128)S(1)}, f32[4,8,1]{2,1,0:T(8,128)S(1)}, u32[]{:S(2)}, u32[]{:S(2)}) collective-permute-start(f32[4,8,1]{2,1,0:T(8,128)S(1)} %squeeze.122), channel_id=1, source_target_pairs={{0,1},{1,2},{2,3},{4,5},{5,6},{6,7},{8,9},{9,10},{10,11},{12,13},{... | collective-permute-start | bytes 392 | tf_op jit(solution)/shard_map/ppermute | solution.py:19
  58.6 8.3 %all-to-all-start = ((f32[16,8,256]{2,1,0:T(8,128)}), f32[16,8,256]{2,1,0:T(8,128)S(1)}, u32[]{:S(2)}, u32[]{:S(2)}) async-start(f32[16,8,256]{2,1,0:T(8,128)} %reduce-scatter.2.cloned.1.call-done), calls=%async_computation.1 | async-start | bytes 262144 | tf_op jit(solution)/shard_map/all_to_all | solution.py:68
  67.1 8.3 %collective-permute-start.3 = (f32[1,8,1024]{2,1,0:T(8,128)S(1)}, f32[1,8,1024]{2,1,0:T(8,128)S(1)}, u32[]{:S(2)}, u32[]{:S(2)}) collective-permute-start(f32[1,8,1024]{2,1,0:T(8,128)S(1)} %slice.267), channel_id=1, source_target_pairs={{8,0},{16,8},{24,16},{9,1},{17,9},{25,17},{10,2},{18,10},{26,18},{... | collective-permute-start | bytes 98312 | tf_op jit(solution)/shard_map/ppermute | solution.py:19
  68.4 7.0 %collective-permute-start.4 = (f32[4,1,1024]{2,1,0:T(1,128)S(1)}, f32[4,1,1024]{2,1,0:T(1,128)S(1)}, u32[]{:S(2)}, u32[]{:S(2)}) collective-permute-start(f32[4,1,1024]{2,1,0:T(1,128)S(1)} %slice.269), channel_id=1, source_target_pairs={{4,0},{5,1},{6,2},{7,3},{12,8},{13,9},{14,10},{15,11},{20,16},{21,... | collective-permute-start | bytes 49160 | tf_op jit(solution)/shard_map/ppermute | solution.py:19
  69.7 5.7 %collective-permute-start.5 = (f32[4,8,1]{2,1,0:T(8,128)S(1)}, f32[4,8,1]{2,1,0:T(8,128)S(1)}, u32[]{:S(2)}, u32[]{:S(2)}) collective-permute-start(f32[4,8,1]{2,1,0:T(8,128)S(1)} %slice.271), channel_id=1, source_target_pairs={{1,0},{2,1},{3,2},{5,4},{6,5},{7,6},{9,8},{10,9},{11,10},{13,12},{... | collective-permute-start | bytes 392 | tf_op jit(solution)/shard_map/ppermute | solution.py:19
  75.8 11.1 %collective-permute-start.6 = (f32[1,8,1024]{2,1,0:T(8,128)S(1)}, f32[1,8,1024]{2,1,0:T(8,128)S(1)}, u32[]{:S(2)}, u32[]{:S(2)}) collective-permute-start(f32[1,8,1024]{2,1,0:T(8,128)S(1)} %slice_bitcast_fusion.27), channel_id=1, source_target_pairs={{0,8},{8,16},{16,24},{1,9},{9,17},{17,25},{2,10},{10,18},{18,26},{... | collective-permute-start | bytes 98312 | tf_op jit(solution)/shard_map/ppermute | solution.py:19
  80.4 6.5 %collective-permute-start.7 = (f32[4,1,1024]{2,1,0:T(1,128)S(1)}, f32[4,1,1024]{2,1,0:T(1,128)S(1)}, u32[]{:S(2)}, u32[]{:S(2)}) collective-permute-start(f32[4,1,1024]{2,1,0:T(1,128)S(1)} %slice_bitcast_fusion.31), channel_id=1, source_target_pairs={{0,4},{1,5},{2,6},{3,7},{8,12},{9,13},{10,14},{11,15},{16,20},{17,... | collective-permute-start | bytes 49160 | tf_op jit(solution)/shard_map/ppermute | solution.py:19
  82.1 4.7 %collective-permute-start.8 = (f32[4,8,1]{1,0,2:T(4,128)S(1)}, f32[4,8,1]{1,0,2:T(4,128)S(1)}, u32[]{:S(2)}, u32[]{:S(2)}) collective-permute-start(f32[4,8,1]{1,0,2:T(4,128)S(1)} %bitcast.175), channel_id=1, source_target_pairs={{0,1},{1,2},{2,3},{4,5},{5,6},{6,7},{8,9},{9,10},{10,11},{12,13},{... | collective-permute-start | bytes 392 | tf_op jit(solution)/shard_map/ppermute | solution.py:19
  87.0 8.6 %collective-permute-start.9 = (f32[1,8,1024]{2,1,0:T(8,128)S(1)}, f32[1,8,1024]{2,1,0:T(8,128)S(1)}, u32[]{:S(2)}, u32[]{:S(2)}) collective-permute-start(f32[1,8,1024]{2,1,0:T(8,128)S(1)} %slice.282), channel_id=1, source_target_pairs={{8,0},{16,8},{24,16},{9,1},{17,9},{25,17},{10,2},{18,10},{26,18},{... | collective-permute-start | bytes 98312 | tf_op jit(solution)/shard_map/ppermute | solution.py:19
  88.3 7.2 %collective-permute-start.10 = (f32[4,1,1024]{2,1,0:T(1,128)S(1)}, f32[4,1,1024]{2,1,0:T(1,128)S(1)}, u32[]{:S(2)}, u32[]{:S(2)}) collective-permute-start(f32[4,1,1024]{2,1,0:T(1,128)S(1)} %slice.284), channel_id=1, source_target_pairs={{4,0},{5,1},{6,2},{7,3},{12,8},{13,9},{14,10},{15,11},{20,16},{21,... | collective-permute-start | bytes 49160 | tf_op jit(solution)/shard_map/ppermute | solution.py:19
  89.7 5.9 %collective-permute-start.11 = (f32[4,8,1]{2,1,0:T(8,128)S(1)}, f32[4,8,1]{2,1,0:T(8,128)S(1)}, u32[]{:S(2)}, u32[]{:S(2)}) collective-permute-start(f32[4,8,1]{2,1,0:T(8,128)S(1)} %slice.286), channel_id=1, source_target_pairs={{1,0},{2,1},{3,2},{5,4},{6,5},{7,6},{9,8},{10,9},{11,10},{13,12},{... | collective-permute-start | bytes 392 | tf_op jit(solution)/shard_map/ppermute | solution.py:19
  96.1 11.6 %collective-permute-start.12 = (f32[1,8,1024]{2,1,0:T(8,128)S(1)}, f32[1,8,1024]{2,1,0:T(8,128)S(1)}, u32[]{:S(2)}, u32[]{:S(2)}) collective-permute-start(f32[1,8,1024]{2,1,0:T(8,128)S(1)} %slice_bitcast_fusion.26), channel_id=1, source_target_pairs={{0,8},{8,16},{16,24},{1,9},{9,17},{17,25},{2,10},{10,18},{18,26},{... | collective-permute-start | bytes 98312 | tf_op jit(solution)/shard_map/ppermute | solution.py:19
  100.6 7.1 %collective-permute-start.13 = (f32[4,1,1024]{2,1,0:T(1,128)S(1)}, f32[4,1,1024]{2,1,0:T(1,128)S(1)}, u32[]{:S(2)}, u32[]{:S(2)}) collective-permute-start(f32[4,1,1024]{2,1,0:T(1,128)S(1)} %slice_bitcast_fusion.30), channel_id=1, source_target_pairs={{0,4},{1,5},{2,6},{3,7},{8,12},{9,13},{10,14},{11,15},{16,20},{17,... | collective-permute-start | bytes 49160 | tf_op jit(solution)/shard_map/ppermute | solution.py:19
  102.5 5.1 %collective-permute-start.14 = (f32[4,8,1]{1,0,2:T(4,128)S(1)}, f32[4,8,1]{1,0,2:T(4,128)S(1)}, u32[]{:S(2)}, u32[]{:S(2)}) collective-permute-start(f32[4,8,1]{1,0,2:T(4,128)S(1)} %bitcast.176), channel_id=1, source_target_pairs={{0,1},{1,2},{2,3},{4,5},{5,6},{6,7},{8,9},{9,10},{10,11},{12,13},{... | collective-permute-start | bytes 392 | tf_op jit(solution)/shard_map/ppermute | solution.py:19
  107.8 8.6 %collective-permute-start.15 = (f32[1,8,1024]{2,1,0:T(8,128)S(1)}, f32[1,8,1024]{2,1,0:T(8,128)S(1)}, u32[]{:S(2)}, u32[]{:S(2)}) collective-permute-start(f32[1,8,1024]{2,1,0:T(8,128)S(1)} %slice.297), channel_id=1, source_target_pairs={{8,0},{16,8},{24,16},{9,1},{17,9},{25,17},{10,2},{18,10},{26,18},{... | collective-permute-start | bytes 98312 | tf_op jit(solution)/shard_map/ppermute | solution.py:19
  109.1 7.2 %collective-permute-start.16 = (f32[4,1,1024]{2,1,0:T(1,128)S(1)}, f32[4,1,1024]{2,1,0:T(1,128)S(1)}, u32[]{:S(2)}, u32[]{:S(2)}) collective-permute-start(f32[4,1,1024]{2,1,0:T(1,128)S(1)} %slice.299), channel_id=1, source_target_pairs={{4,0},{5,1},{6,2},{7,3},{12,8},{13,9},{14,10},{15,11},{20,16},{21,... | collective-permute-start | bytes 49160 | tf_op jit(solution)/shard_map/ppermute | solution.py:19
  110.5 5.9 %collective-permute-start.17 = (f32[4,8,1]{2,1,0:T(8,128)S(1)}, f32[4,8,1]{2,1,0:T(8,128)S(1)}, u32[]{:S(2)}, u32[]{:S(2)}) collective-permute-start(f32[4,8,1]{2,1,0:T(8,128)S(1)} %slice.301), channel_id=1, source_target_pairs={{1,0},{2,1},{3,2},{5,4},{6,5},{7,6},{9,8},{10,9},{11,10},{13,12},{... | collective-permute-start | bytes 392 | tf_op jit(solution)/shard_map/ppermute | solution.py:19
  116.9 12.3 %collective-permute-start.18 = (f32[1,8,1024]{2,1,0:T(8,128)S(1)}, f32[1,8,1024]{2,1,0:T(8,128)S(1)}, u32[]{:S(2)}, u32[]{:S(2)}) collective-permute-start(f32[1,8,1024]{2,1,0:T(8,128)S(1)} %slice_bitcast_fusion.25), channel_id=1, source_target_pairs={{0,8},{8,16},{16,24},{1,9},{9,17},{17,25},{2,10},{10,18},{18,26},{... | collective-permute-start | bytes 98312 | tf_op jit(solution)/shard_map/ppermute | solution.py:19
  122.2 7.1 %collective-permute-start.19 = (f32[4,1,1024]{2,1,0:T(1,128)S(1)}, f32[4,1,1024]{2,1,0:T(1,128)S(1)}, u32[]{:S(2)}, u32[]{:S(2)}) collective-permute-start(f32[4,1,1024]{2,1,0:T(1,128)S(1)} %slice_bitcast_fusion.29), channel_id=1, source_target_pairs={{0,4},{1,5},{2,6},{3,7},{8,12},{9,13},{10,14},{11,15},{16,20},{17,... | collective-permute-start | bytes 49160 | tf_op jit(solution)/shard_map/ppermute | solution.py:19
  124.1 5.1 %collective-permute-start.20 = (f32[4,8,1]{1,0,2:T(4,128)S(1)}, f32[4,8,1]{1,0,2:T(4,128)S(1)}, u32[]{:S(2)}, u32[]{:S(2)}) collective-permute-start(f32[4,8,1]{1,0,2:T(4,128)S(1)} %bitcast.177), channel_id=1, source_target_pairs={{0,1},{1,2},{2,3},{4,5},{5,6},{6,7},{8,9},{9,10},{10,11},{12,13},{... | collective-permute-start | bytes 392 | tf_op jit(solution)/shard_map/ppermute | solution.py:19
  129.4 8.6 %collective-permute-start.21 = (f32[1,8,1024]{2,1,0:T(8,128)S(1)}, f32[1,8,1024]{2,1,0:T(8,128)S(1)}, u32[]{:S(2)}, u32[]{:S(2)}) collective-permute-start(f32[1,8,1024]{2,1,0:T(8,128)S(1)} %slice.312), channel_id=1, source_target_pairs={{8,0},{16,8},{24,16},{9,1},{17,9},{25,17},{10,2},{18,10},{26,18},{... | collective-permute-start | bytes 98312 | tf_op jit(solution)/shard_map/ppermute | solution.py:19
  130.7 7.2 %collective-permute-start.22 = (f32[4,1,1024]{2,1,0:T(1,128)S(1)}, f32[4,1,1024]{2,1,0:T(1,128)S(1)}, u32[]{:S(2)}, u32[]{:S(2)}) collective-permute-start(f32[4,1,1024]{2,1,0:T(1,128)S(1)} %slice.314), channel_id=1, source_target_pairs={{4,0},{5,1},{6,2},{7,3},{12,8},{13,9},{14,10},{15,11},{20,16},{21,... | collective-permute-start | bytes 49160 | tf_op jit(solution)/shard_map/ppermute | solution.py:19
  132.1 5.9 %collective-permute-start.23 = (f32[4,8,1]{2,1,0:T(8,128)S(1)}, f32[4,8,1]{2,1,0:T(8,128)S(1)}, u32[]{:S(2)}, u32[]{:S(2)}) collective-permute-start(f32[4,8,1]{2,1,0:T(8,128)S(1)} %slice.316), channel_id=1, source_target_pairs={{1,0},{2,1},{3,2},{5,4},{6,5},{7,6},{9,8},{10,9},{11,10},{13,12},{... | collective-permute-start | bytes 392 | tf_op jit(solution)/shard_map/ppermute | solution.py:19
  138.6 12.5 %collective-permute-start.24 = (f32[1,8,1024]{2,1,0:T(8,128)S(1)}, f32[1,8,1024]{2,1,0:T(8,128)S(1)}, u32[]{:S(2)}, u32[]{:S(2)}) collective-permute-start(f32[1,8,1024]{2,1,0:T(8,128)S(1)} %slice_bitcast_fusion.24), channel_id=1, source_target_pairs={{0,8},{8,16},{16,24},{1,9},{9,17},{17,25},{2,10},{10,18},{18,26},{... | collective-permute-start | bytes 98312 | tf_op jit(solution)/shard_map/ppermute | solution.py:19
  144.0 7.1 %collective-permute-start.25 = (f32[4,1,1024]{2,1,0:T(1,128)S(1)}, f32[4,1,1024]{2,1,0:T(1,128)S(1)}, u32[]{:S(2)}, u32[]{:S(2)}) collective-permute-start(f32[4,1,1024]{2,1,0:T(1,128)S(1)} %slice_bitcast_fusion.28), channel_id=1, source_target_pairs={{0,4},{1,5},{2,6},{3,7},{8,12},{9,13},{10,14},{11,15},{16,20},{17,... | collective-permute-start | bytes 49160 | tf_op jit(solution)/shard_map/ppermute | solution.py:19
  145.9 5.1 %collective-permute-start.26 = (f32[4,8,1]{1,0,2:T(4,128)S(1)}, f32[4,8,1]{1,0,2:T(4,128)S(1)}, u32[]{:S(2)}, u32[]{:S(2)}) collective-permute-start(f32[4,8,1]{1,0,2:T(4,128)S(1)} %bitcast.178), channel_id=1, source_target_pairs={{0,1},{1,2},{2,3},{4,5},{5,6},{6,7},{8,9},{9,10},{10,11},{12,13},{... | collective-permute-start | bytes 392 | tf_op jit(solution)/shard_map/ppermute | solution.py:19
Sparse Core Ops, SparseCore 0:
  30.7 27.8 reduce-scatter.1
where the time goes:
time: 160 us; the launch traced here: 159 us
  starting transfers between devices  70.6 us (44%)
  waiting for transfers between devices  45.9 us (29%)
  other arithmetic  21.5 us (13%)
  between operations  14.2 us (9%)
  matrix products  3.82 us (2%)
  local copies, waits for them, and re-layouts  2.68 us (2%)
    ppermute x27, starting transfers between devices, passed_along(): return lax.ppermute(block, axis, route)  67.2 us
    ppermute x27, waiting for transfers between devices, passed_along(): return lax.ppermute(block, axis, route)  22.8 us
    reduce_scatter x1, waiting for transfers between devices, per_device(): lax.psum_scatter(full_term, 'ang', scatter_dimension=2, tiled=True)  18.1 us
    another operation x1, other arithmetic  17.4 us
    all_to_all x1, waiting for transfers between devices, per_device(): lax.all_to_all(column_part, 'ang', split_axis=0, concat_axis=2, tiled=True)  4.97 us
    all_to_all x1, starting transfers between devices, per_device(): lax.all_to_all(column_part, 'ang', split_axis=0, concat_axis=2, tiled=True)  3.32 us
  transfers between devices with their start and end apart: 29, of which 10 were waited for; matrix products, arithmetic and copies ran while one was open for 1% of the time, Pallas kernels for 0%

commit v1 on v0

v1 whole, which is shorter than its diff:
```python
import functools
import math

import jax
import jax.numpy as jnp
from jax import lax
from jax.experimental import pallas as pl
from jax.experimental.pallas import tpu as pltpu
from jax.sharding import PartitionSpec as P

NX = 4096
TV_STEPS = 4
HALO = TV_STEPS
CHUNK = 128

smooth_weight = 0.5
dual_step = 1.0 / 12.0

NT = (((1,), (1,)), ((), ()))


def unit_circle(phase):
    phase = phase & (NX - 1)
    quarter = (phase + NX // 8) // (NX // 4)
    angle = (phase - quarter * (NX // 4)).astype(jnp.float32) * (2.0 * math.pi / NX)
    square = angle * angle
    sine = angle * (1.0 + square * (-1.0 / 6 + square * (1.0 / 120 + square * (-1.0 / 5040 + square * (1.0 / 362880)))))
    cosine = 1.0 + square * (-0.5 + square * (1.0 / 24 + square * (-1.0 / 720 + square * (1.0 / 40320))))
    odd = (quarter & 1) == 1
    first = jnp.where(odd, -sine, cosine)
    second = jnp.where(odd, cosine, sine)
    flip = (quarter & 2) == 2
    return jnp.where(flip, -first, first), jnp.where(flip, -second, second)


def project_kernel(
    place_ref, data_ref, offsets_ref, view_ref, taps_ref, weight_ref, volume_ref, multiplier_ref, edge_ref,
    out_ref,
    spread_ref, grid_ref, cos_ref, sin_ref, step_cos_ref, step_sin_ref, part_cos_ref, part_sin_ref, lines_ref, halo_ref, vm_ref,
):
    ang, gx = place_ref[0], place_ref[1]
    samples = data_ref.shape[1]
    lines = data_ref.shape[0] // 2
    block_size = spread_ref.shape[0]
    columns = volume_ref.shape[1]
    local_lines = volume_ref.shape[0]
    dests, window, _ = out_ref.shape
    block = window - 2 * HALO

    pieces = []
    for piece in range(samples // 128):
        view = view_ref[pl.ds(piece, 1), :]
        found = jnp.zeros((1, 128), jnp.float32)
        lane = jnp.broadcast_to(view & 127, (8, 128))
        for row in range(weight_ref.shape[0]):
            table = jnp.broadcast_to(weight_ref[pl.ds(row, 1), :], (8, 128))
            picked = jnp.take_along_axis(table, lane, axis=1)[:1]
            found = jnp.where(view // 128 == row, picked, found)
        pieces.append(found)
    weight = jnp.concatenate(pieces, axis=1)
    values = [weight * taps_ref[pl.ds(tap, 1), :] for tap in range(taps_ref.shape[0])]
    offsets = jnp.concatenate([offsets_ref[pl.ds(piece, 1), :] for piece in range(samples // 128)], axis=1)

    rows = 16
    cell = lax.broadcasted_iota(jnp.int32, (rows, samples), 0)
    start = jnp.broadcast_to(offsets, (rows, samples))
    values = [jnp.broadcast_to(value, (rows, samples)) for value in values]
    for first in range(0, block_size, rows):
        tap = cell - (start - first)
        spread = jnp.zeros((rows, samples), jnp.float32)
        for index, value in enumerate(values):
            spread = jnp.where(tap == index, value, spread)
        spread_ref[pl.ds(first, rows), :] = spread.astype(jnp.bfloat16)

    grid_ref[...] = lax.dot_general(
        data_ref[...], spread_ref[...], NT, preferred_element_type=jnp.float32
    ).astype(jnp.bfloat16)

    lines_ref[...] = jnp.zeros_like(lines_ref)
    lines_ref[pl.ds(pl.multiple_of(ang * local_lines, 8), local_lines), :] = volume_ref[...] + multiplier_ref[...]
    halo_ref[...] = jnp.zeros_like(halo_ref)
    halo_ref[pl.ds(pl.multiple_of(ang * local_lines, 8), local_lines), :] = edge_ref[...]
    edges = halo_ref[...].T
    vm_ref[pl.ds(0, HALO), :] = edges[:HALO]
    vm_ref[pl.ds(HALO + columns, HALO), :] = edges[HALO : 2 * HALO]
    for first in range(0, columns, 128):
        vm_ref[pl.ds(HALO + first, 128), :] = lines_ref[:, pl.ds(first, 128)].T

    freq = ang * block_size + lax.broadcasted_iota(jnp.int32, (8, block_size), 1)
    row = lax.broadcasted_iota(jnp.int32, (8, block_size), 0)
    base_cos, base_sin = unit_circle(freq * (gx * columns - HALO + row))
    for first in range(0, CHUNK // 8, 8):
        step_cos_ref[pl.ds(first, 8), :], step_sin_ref[pl.ds(first, 8), :] = unit_circle(freq * (8 * (row + first)))
    for first in range(0, part_cos_ref.shape[0], 8):
        part_cos_ref[pl.ds(first, 8), :], part_sin_ref[pl.ds(first, 8), :] = unit_circle(
            freq * (CHUNK * (row + first))
        )

    total = columns + 2 * HALO
    for part in range(pl.cdiv(total, CHUNK)):
        first = part * CHUNK
        count = min(CHUNK, total - first)
        slot = part % 2
        part_cos, part_sin = part_cos_ref[pl.ds(part, 1), :], part_sin_ref[pl.ds(part, 1), :]
        here_cos = base_cos * part_cos - base_sin * part_sin
        here_sin = base_sin * part_cos + base_cos * part_sin
        for step in range(0, pl.cdiv(count, 8), 2):
            pair_cos, pair_sin = [], []
            for one in (step, step + 1):
                step_cos, step_sin = step_cos_ref[pl.ds(one, 1), :], step_sin_ref[pl.ds(one, 1), :]
                pair_cos.append(here_cos * step_cos - here_sin * step_sin)
                pair_sin.append(-(here_sin * step_cos + here_cos * step_sin))
            cos_ref[slot, pl.ds(8 * step, 16), :] = jnp.concatenate(pair_cos, axis=0).astype(jnp.bfloat16)
            sin_ref[slot, pl.ds(8 * step, 16), :] = jnp.concatenate(pair_sin, axis=0).astype(jnp.bfloat16)
        made = max(16, count)
        total_part = lax.dot_general(
            cos_ref[slot, pl.ds(0, made), :], grid_ref[pl.ds(0, lines), :], NT, preferred_element_type=jnp.float32
        ) + lax.dot_general(
            sin_ref[slot, pl.ds(0, made), :], grid_ref[pl.ds(lines, lines), :], NT, preferred_element_type=jnp.float32
        )
        sent = vm_ref[pl.ds(first, count), :] - total_part[:count] * NX ** (-0.5)
        for dest in range(dests):
            low, high = max(first, dest * block), min(first + count, dest * block + window)
            if low < high:
                out_ref[dest, pl.ds(low - dest * block, high - low), :] = sent[low - first : high - first]


def project(place, data, offsets, view_index, taps, view_weight, volume, multiplier, edge, dests):
    lines = data.shape[0] // 2
    samples = data.shape[1]
    columns = volume.shape[1]
    block_size = NX // lax.axis_size("ang")
    window = columns // dests + 2 * HALO
    parts = pl.cdiv(columns + 2 * HALO, CHUNK)
    vmem = pl.BlockSpec(memory_space=pltpu.VMEM)
    return pl.pallas_call(
        project_kernel,
        out_shape=jax.ShapeDtypeStruct((dests, window, lines), jnp.float32),
        in_specs=[pl.BlockSpec(memory_space=pltpu.SMEM)] + [vmem] * 8,
        out_specs=vmem,
        scratch_shapes=[
            pltpu.VMEM((block_size, samples), jnp.bfloat16),
            pltpu.VMEM((2 * lines, block_size), jnp.bfloat16),
            pltpu.VMEM((2, CHUNK, block_size), jnp.bfloat16),
            pltpu.VMEM((2, CHUNK, block_size), jnp.bfloat16),
            pltpu.VMEM((CHUNK // 8, block_size), jnp.float32),
            pltpu.VMEM((CHUNK // 8, block_size), jnp.float32),
            pltpu.VMEM((8 * pl.cdiv(parts, 8), block_size), jnp.float32),
            pltpu.VMEM((8 * pl.cdiv(parts, 8), block_size), jnp.float32),
            pltpu.VMEM((lines, columns), jnp.float32),
            pltpu.VMEM((lines, 128), jnp.float32),
            pltpu.VMEM((columns + 2 * HALO, lines), jnp.float32),
        ],
        name="project",
    )(place, data, offsets, view_index, taps, view_weight, volume, multiplier, edge)


def smooth_kernel(planes, place_ref, parts_ref, out_ref):
    dests, local_lines, block = out_ref.shape
    sources, window, lines = parts_ref.shape
    groups = dests * local_lines // lines
    angs = sources // groups
    rows = lines // planes
    lane = lax.broadcasted_iota(jnp.int32, (window, lines), 1)
    lane_row = lane % rows
    column = place_ref[2] + lax.broadcasted_iota(jnp.int32, (window, lines), 0)
    plane_open = lane // rows < planes - 1
    row_first = lane_row == 0
    row_last = lane_row == rows - 1
    cell_open = (column >= 0) & (column < NX - 1)
    zero = jnp.float32(0.0)

    source = []
    for group in range(groups):
        total = parts_ref[group]
        for ang in range(1, angs):
            total = total + parts_ref[ang * groups + group]
        source.append(total)
    scaled = [value / smooth_weight for value in source]

    def down(values):
        lower = []
        for group in range(groups):
            previous = values[group - 1]
            lower.append(
                jnp.where(
                    row_first, pltpu.roll(previous, lines - (rows - 1), 1), pltpu.roll(values[group], 1, 1)
                )
            )
        return lower

    flow = None
    for repeat in range(TV_STEPS + 1):
        if flow is None:
            target = [-value for value in scaled]
        else:
            lower_row = down([f[1] for f in flow])
            local_div = []
            for group in range(groups):
                f0, f1, f2 = flow[group]
                plane_part = f0 - pltpu.roll(f0, rows, 1)
                row_part = f1 - lower_row[group]
                cell_part = f2 - pltpu.roll(f2, 1, 0)
                local_div.append(plane_part + row_part + cell_part)
            if repeat == TV_STEPS:
                for group in range(groups):
                    done = source[group] - smooth_weight * local_div[group]
                    turned = done[HALO : HALO + block].T
                    for ang in range(angs):
                        out_ref[ang * groups + group] = turned[ang * local_lines : (ang + 1) * local_lines]
                return
            target = [local_div[group] - scaled[group] for group in range(groups)]
        updated = []
        for group in range(groups):
            here = target[group]
            slope_plane = jnp.where(plane_open, pltpu.roll(here, lines - rows, 1) - here, zero)
            if group + 1 < groups:
                upper = jnp.where(
                    row_last, pltpu.roll(target[group + 1], rows - 1, 1), pltpu.roll(here, lines - 1, 1)
                )
                slope_row = upper - here
            else:
                slope_row = jnp.where(row_last, zero, pltpu.roll(here, lines - 1, 1) - here)
            slope_cell = jnp.where(cell_open, pltpu.roll(here, window - 1, 0) - here, zero)
            slope_norm = jnp.sqrt(slope_plane * slope_plane + slope_row * slope_row + slope_cell * slope_cell)
            scale = 1.0 / (1.0 + dual_step * slope_norm)
            moved = [dual_step * slope_plane, dual_step * slope_row, dual_step * slope_cell]
            if flow is not None:
                moved = [f + m for f, m in zip(flow[group], moved)]
            updated.append([m * scale for m in moved])
        flow = updated


def smooth(place, parts, planes, local_lines):
    sources, window, lines = parts.shape
    vmem = pl.BlockSpec(memory_space=pltpu.VMEM)
    return pl.pallas_call(
        functools.partial(smooth_kernel, planes),
        out_shape=jax.ShapeDtypeStruct((sources, local_lines, window - 2 * HALO), jnp.float32),
        in_specs=[pl.BlockSpec(memory_space=pltpu.SMEM), vmem],
        out_specs=vmem,
        name="smooth",
    )(place, parts)


def passed_along(block, axis, distance):
    devices = range(lax.axis_size(axis))
    route = [(i - distance, i) for i in devices if i - distance in devices]
    return lax.ppermute(block, axis, route)


def per_device(spectrum_data, offsets, view_index, kernel, view_weight, volume, multiplier):
    local_planes, rows, columns = volume.shape
    planes = spectrum_data.shape[1]
    samples = spectrum_data.shape[3]
    dests = lax.axis_size("ang") * lax.axis_size("gy")
    block = columns // dests
    local_lines = local_planes * rows
    lines = planes * rows
    ang, gy, gx = lax.axis_index("ang"), lax.axis_index("gy"), lax.axis_index("gx")
    first_column = gx * columns + (ang * lax.axis_size("gy") + gy) * block - HALO
    place = jnp.stack([ang, gx, first_column]).astype(jnp.int32)

    volume = volume.reshape(local_lines, columns)
    multiplier = multiplier.reshape(local_lines, columns)
    left = passed_along(volume[:, -HALO:] + multiplier[:, -HALO:], "gx", 1)
    right = passed_along(volume[:, :HALO] + multiplier[:, :HALO], "gx", -1)
    edge = jnp.pad(jnp.concatenate([left, right], axis=1), ((0, 0), (0, 128 - 2 * HALO)))
    views = view_weight.shape[0]
    weight_rows = -(-views // 128)
    table = jnp.pad(view_weight, (0, weight_rows * 128 - views)).reshape(weight_rows, 128)
    parts = project(
        place,
        spectrum_data.reshape(2 * lines, samples),
        offsets.reshape(samples // 128, 128),
        view_index.reshape(samples // 128, 128),
        kernel,
        table,
        volume,
        multiplier,
        edge,
        dests,
    )
    parts = lax.all_to_all(parts, ("ang", "gy"), split_axis=0, concat_axis=0)
    done = smooth(place, parts, planes, local_lines)
    done = lax.all_to_all(done, ("ang", "gy"), split_axis=0, concat_axis=0)
    return jnp.transpose(done, (1, 0, 2)).reshape(local_planes, rows, columns)


def solution(mesh):
    placed = (
        P(None, None, "gy", "ang"),
        P("ang"),
        P("ang"),
        P(None, "ang"),
        P(),
        P("ang", "gy", "gx"),
        P("ang", "gy", "gx"),
    )
    return jax.shard_map(
        per_device, mesh=mesh, in_specs=placed, out_specs=P("ang", "gy", "gx"), check_vma=False
    )
```

time: 160 us -> 44.6 us (0.28)
  starting transfers between devices: 70.6 us -> 6.24 us
  waiting for transfers between devices: 45.9 us -> 2.39 us
  blocking collectives: 0 us -> 23 us
  other arithmetic: 21.5 us -> 2.17 us
  between operations: 14.2 us -> 0.04 us
  Pallas kernels: 0 us -> 8.23 us
  matrix products: 3.82 us -> 0 us
    ppermute x27 -> x2, starting transfers between devices: 67.2 us -> 6.24 us  [passed_along(): return lax.ppermute(block, axis, route)]
    all_to_all x0 -> x2, blocking collectives: none -> 23 us  [the longest x1 14.2 us: per_device(): parts = lax.all_to_all(parts, ('ang', 'gy'), split_axis=0, concat_axis=0)]
    ppermute x27 -> x2, waiting for transfers between devices: 22.8 us -> 2.39 us  [passed_along(): return lax.ppermute(block, axis, route)]
    reduce_scatter x1 -> x0, waiting for transfers between devices: 18.1 us -> none  [per_device(): lax.psum_scatter(full_term, 'ang', scatter_dimension=2, tiled=True)]
    another operation x1, other arithmetic: 17.4 us -> 0.65 us  [per_device(): place = jnp.stack([ang, gx, first_column]).astype(jnp.int32)]
    pallas_call x0 -> x2, Pallas kernels: none -> 8.23 us  [the longest x1 5.02 us: project(): pl.pallas_call(project_kernel, out_shape=jax.ShapeDtypeStruct((dests, win...]
    all_to_all x1 -> x0, waiting for transfers between devices: 4.97 us -> none  [per_device(): lax.all_to_all(column_part, 'ang', split_axis=0, concat_axis=2, tiled=True)]
    dot_general x2 -> x0, matrix products: 3.82 us -> none  [the longest x1 2.24 us: per_device(): jnp.dot(spectrum_data.reshape(2 * flat_rows, spectrum_data.shape[3]), spr...]
  transfers between devices with their start and end apart: 29 -> 2, of which waited for: 10 -> 1; matrix products, arithmetic and copies ran while one was open for 1% -> 3% of each run, Pallas kernels for 0% -> 0%
where the time goes in v1:
time: 44.6 us; the launch traced here: 44.1 us
  blocking collectives  23 us (52%)
  Pallas kernels  8.23 us (18%)
  starting transfers between devices  6.24 us (14%)
  waiting for transfers between devices  2.39 us (5%)
  other arithmetic  2.17 us (5%)
  local copies, waits for them, and re-layouts  2.04 us (5%)
    all_to_all x1, blocking collectives, per_device(): parts = lax.all_to_all(parts, ('ang', 'gy'), split_axis=0, concat_axis=0)  14.2 us
    all_to_all x1, blocking collectives, per_device(): done = lax.all_to_all(done, ('ang', 'gy'), split_axis=0, concat_axis=0)  8.78 us
    ppermute x2, starting transfers between devices, passed_along(): return lax.ppermute(block, axis, route)  6.24 us
    pallas_call x1, Pallas kernels, project(): pl.pallas_call(project_kernel, out_shape=jax.ShapeDtypeStruct((dests, win...  5.02 us
    pallas_call x1, Pallas kernels, smooth(): pl.pallas_call(functools.partial(smooth_kernel, planes), out_shape=jax.Sh...  3.21 us
    ppermute x2, waiting for transfers between devices, passed_along(): return lax.ppermute(block, axis, route)  2.39 us
  transfers between devices with their start and end apart: 2, of which 1 were waited for; matrix products, arithmetic and copies ran while one was open for 3% of the time, Pallas kernels for 0%

profile of v1, /device:TPU:0, one launch (start us, length us, event | category | flops | bytes accessed | tf_op | source)
XLA Modules:
  0.0 44.1 jit_solution(17367987723033116072)
XLA Ops:
  0.0 0.8 %slice_add_fusion.1 = (f32[32,4]{1,0:T(8,128)S(1)}, f32[32,4]{1,0:T(8,128)S(1)}) fusion(f32[32,1024]{1,0:T(8,128)} %bitcast.15, f32[32,1024]{1,0:T(8,128)} %bitcast.13), kind=kLoop, calls=%fused_computation.3 | loop fusion | flops 256 | bytes 3072 | tf_op jit(solution)/shard_map/add | solution.py:266
  0.8 5.0 %collective-permute-start = (f32[32,4]{1,0:T(8,128)S(1)}, f32[32,4]{1,0:T(8,128)S(1)}, u32[]{:S(2)}, u32[]{:S(2)}) collective-permute-start(f32[32,4]{1,0:T(8,128)S(1)} %get-tuple-element.5), channel_id=1, source_target_pairs={{0,1},{1,2},{2,3},{4,5},{5,6},{6,7},{8,9},{9,10},{10,11},{12,13},{... | collective-permute-start | bytes 1544 | tf_op jit(solution)/shard_map/ppermute | solution.py:249
  5.8 1.3 %collective-permute-start.1 = (f32[32,4]{1,0:T(8,128)S(1)}, f32[32,4]{1,0:T(8,128)S(1)}, u32[]{:S(2)}, u32[]{:S(2)}) collective-permute-start(f32[32,4]{1,0:T(8,128)S(1)} %get-tuple-element.6), channel_id=1, source_target_pairs={{1,0},{2,1},{3,2},{5,4},{6,5},{7,6},{9,8},{10,9},{11,10},{13,12},{... | collective-permute-start | bytes 1544 | tf_op jit(solution)/shard_map/ppermute | solution.py:249
  7.1 0.0 copy-start
  7.1 0.7 %copy-done = f32[1500]{0:T(1024)S(1)} copy-done((f32[1500]{0:T(1024)S(1)}, f32[1500]{0:T(1024)}, u32[]{:S(2)}) %copy-start) | copy-done | bytes 6024
  7.8 0.6 %pad_bitcast_fusion.weight_ref = f32[12,128]{1,0:T(8,128)} fusion(f32[1500]{0:T(1024)S(1)} %copy-done), kind=kLoop, calls=%fused_computation.4 | loop fusion | bytes 12144 | tf_op jit(solution)/shard_map/reshape | solution.py:271
  8.4 0.6 %pad_add_fusion.place_ref = s32[3]{0:T(128)} fusion(s32[1]{0:T(128)} %bitcast.2, s32[1]{0:T(128)} %bitcast.1, s32[1]{0:T(128)} %bitcast), kind=kLoop, calls=%fused_computation.5 | loop fusion | flops 6 | bytes 24 | tf_op jit(solution)/shard_map/stack | solution.py:262
  9.0 0.0 collective-permute-done
  9.0 2.4 %collective-permute-done.1 = f32[32,4]{1,0:T(8,128)S(1)} collective-permute-done((f32[32,4]{1,0:T(8,128)S(1)}, f32[32,4]{1,0:T(8,128)S(1)}, u32[]{:S(2)}, u32[]{:S(2)}) %collective-permute-start.1) | collective-permute-done | bytes 544 | tf_op jit(solution)/shard_map/ppermute | solution.py:249
  11.4 0.7 %select_maximum_fusion.edge_ref = f32[32,128]{1,0:T(8,128)} fusion(f32[32,4]{1,0:T(8,128)S(1)} %collective-permute-done.1, f32[32,4]{1,0:T(8,128)S(1)} %collective-permute-done), kind=kLoop, calls=%fused_computation | loop fusion | flops 16384 | bytes 17408 | tf_op jit(solution)/shard_map/concatenate | solution.py:268
  12.1 5.0 %project.1 = f32[8,136,128]{2,1,0:T(8,128)} custom-call(s32[3]{0:T(128)} %pad_add_fusion.place_ref, bf16[256,512]{1,0:T(8,128)(2,1)} %bitcast.12, s32[4,128]{1,0:T(4,128)} %bitcast.17, s32[4,128]{1,0:T(4,128)} %bitcast.18, f32[4,512]{1,0:T(4,128)} %taps_ref.1, f32[12,128]{1,0:T(8,128)} %pad_bitcast_fusion.weight_ref, f32[32,1024]{1,0:T(8,128)} %bitcast.14, ...), custom_call_target="tpu_custom_call" | custom-call | tf_op jit(solution)/shard_map/project/pallas_call | solution.py:136
  17.1 14.2 %all_to_all.10.parts_ref = f32[8,136,128]{2,1,0:T(8,128)} all-to-all(f32[8,136,128]{2,1,0:T(8,128)} %project.1), channel_id=1, replica_groups=mesh['ang'=4,'gy'=2,'gx'=4] {'ang','gy'}, dimensions={0} | all-to-all | bytes 1114112 | tf_op jit(solution)/shard_map/all_to_all | solution.py:284
  31.4 3.2 %smooth.1 = f32[8,32,128]{2,1,0:T(8,128)} custom-call(s32[3]{0:T(128)} %pad_add_fusion.place_ref, f32[8,136,128]{2,1,0:T(8,128)} %all_to_all.10.parts_ref), custom_call_target="tpu_custom_call" | custom-call | tf_op jit(solution)/shard_map/smooth/pallas_call | solution.py:237
  34.6 8.8 %all_to_all.11 = f32[8,32,128]{2,1,0:T(8,128)S(1)} all-to-all(f32[8,32,128]{2,1,0:T(8,128)} %smooth.1), channel_id=1, replica_groups=mesh['ang'=4,'gy'=2,'gx'=4] {'ang','gy'}, dimensions={0} | all-to-all | bytes 262144 | tf_op jit(solution)/shard_map/all_to_all | solution.py:286
  43.4 0.1 copy.13
  43.4 0.7 %reshape.27 = f32[4,8,1024]{2,1,0:T(8,128)} reshape(f32[32,8,128]{2,1,0:T(8,128)S(1)} %copy.13) | data formatting | bytes 262144 | tf_op jit(solution)/shard_map/reshape | solution.py:287
Async XLA Ops:
  0.8 8.2 %collective-permute-start = (f32[32,4]{1,0:T(8,128)S(1)}, f32[32,4]{1,0:T(8,128)S(1)}, u32[]{:S(2)}, u32[]{:S(2)}) collective-permute-start(f32[32,4]{1,0:T(8,128)S(1)} %get-tuple-element.5), channel_id=1, source_target_pairs={{0,1},{1,2},{2,3},{4,5},{5,6},{6,7},{8,9},{9,10},{10,11},{12,13},{... | collective-permute-start | bytes 1544 | tf_op jit(solution)/shard_map/ppermute | solution.py:249
  5.8 5.6 %collective-permute-start.1 = (f32[32,4]{1,0:T(8,128)S(1)}, f32[32,4]{1,0:T(8,128)S(1)}, u32[]{:S(2)}, u32[]{:S(2)}) collective-permute-start(f32[32,4]{1,0:T(8,128)S(1)} %get-tuple-element.6), channel_id=1, source_target_pairs={{1,0},{2,1},{3,2},{5,4},{6,5},{7,6},{9,8},{10,9},{11,10},{13,12},{... | collective-permute-start | bytes 1544 | tf_op jit(solution)/shard_map/ppermute | solution.py:249
  7.1 0.7 %copy-start = (f32[1500]{0:T(1024)S(1)}, f32[1500]{0:T(1024)}, u32[]{:S(2)}) copy-start(f32[1500]{0:T(1024)} %param.11) | copy-start | bytes 18004

commit v2 on v1

--- a/solution.py
+++ b/solution.py
@@ -34,11 +34,11 @@
 
 
 def project_kernel(
-    place_ref, data_ref, offsets_ref, view_ref, taps_ref, weight_ref, volume_ref, multiplier_ref, edge_ref,
+    data_ref, offsets_ref, view_ref, taps_ref, weight_ref, volume_ref, multiplier_ref,
     out_ref,
-    spread_ref, grid_ref, cos_ref, sin_ref, step_cos_ref, step_sin_ref, part_cos_ref, part_sin_ref, lines_ref, halo_ref, vm_ref,
+    spread_ref, grid_ref, cos_ref, sin_ref, step_cos_ref, step_sin_ref, part_cos_ref, part_sin_ref, lines_ref, vm_ref,
 ):
-    ang, gx = place_ref[0], place_ref[1]
+    ang, gx = lax.axis_index("ang"), lax.axis_index("gx")
     samples = data_ref.shape[1]
     lines = data_ref.shape[0] // 2
     block_size = spread_ref.shape[0]
@@ -47,15 +47,18 @@
     dests, window, _ = out_ref.shape
     block = window - 2 * HALO
 
+    views = weight_ref.shape[0]
     pieces = []
     for piece in range(samples // 128):
         view = view_ref[pl.ds(piece, 1), :]
         found = jnp.zeros((1, 128), jnp.float32)
         lane = jnp.broadcast_to(view & 127, (8, 128))
-        for row in range(weight_ref.shape[0]):
-            table = jnp.broadcast_to(weight_ref[pl.ds(row, 1), :], (8, 128))
-            picked = jnp.take_along_axis(table, lane, axis=1)[:1]
-            found = jnp.where(view // 128 == row, picked, found)
+        for first in range(0, views, 128):
+            table = weight_ref[pl.ds(first, min(128, views - first))].reshape(1, -1)
+            if views - first < 128:
+                table = jnp.concatenate([table, jnp.zeros((1, 128 - (views - first)), jnp.float32)], axis=1)
+            picked = jnp.take_along_axis(jnp.broadcast_to(table, (8, 128)), lane, axis=1)[:1]
+            found = jnp.where(view // 128 == first // 128, picked, found)
         pieces.append(found)
     weight = jnp.concatenate(pieces, axis=1)
     values = [weight * taps_ref[pl.ds(tap, 1), :] for tap in range(taps_ref.shape[0])]
@@ -78,11 +81,8 @@
 
     lines_ref[...] = jnp.zeros_like(lines_ref)
     lines_ref[pl.ds(pl.multiple_of(ang * local_lines, 8), local_lines), :] = volume_ref[...] + multiplier_ref[...]
-    halo_ref[...] = jnp.zeros_like(halo_ref)
-    halo_ref[pl.ds(pl.multiple_of(ang * local_lines, 8), local_lines), :] = edge_ref[...]
-    edges = halo_ref[...].T
-    vm_ref[pl.ds(0, HALO), :] = edges[:HALO]
-    vm_ref[pl.ds(HALO + columns, HALO), :] = edges[HALO : 2 * HALO]
+    vm_ref[pl.ds(0, HALO), :] = jnp.zeros((HALO, lines), jnp.float32)
+    vm_ref[pl.ds(HALO + columns, HALO), :] = jnp.zeros((HALO, lines), jnp.float32)
     for first in range(0, columns, 128):
         vm_ref[pl.ds(HALO + first, 128), :] = lines_ref[:, pl.ds(first, 128)].T
 
@@ -125,7 +125,7 @@
                 out_ref[dest, pl.ds(low - dest * block, high - low), :] = sent[low - first : high - first]
 
 
-def project(place, data, offsets, view_index, taps, view_weight, volume, multiplier, edge, dests):
+def project(data, offsets, view_index, taps, view_weight, volume, multiplier, dests):
     lines = data.shape[0] // 2
     samples = data.shape[1]
     columns = volume.shape[1]
@@ -135,8 +135,8 @@
     vmem = pl.BlockSpec(memory_space=pltpu.VMEM)
     return pl.pallas_call(
         project_kernel,
-        out_shape=jax.ShapeDtypeStruct((dests, window, lines), jnp.float32),
-        in_specs=[pl.BlockSpec(memory_space=pltpu.SMEM)] + [vmem] * 8,
+        out_shape=pltpu.VMEM((dests, window, lines), jnp.float32),
+        in_specs=[vmem] * 7,
         out_specs=vmem,
         scratch_shapes=[
             pltpu.VMEM((block_size, samples), jnp.bfloat16),
@@ -148,14 +148,41 @@
             pltpu.VMEM((8 * pl.cdiv(parts, 8), block_size), jnp.float32),
             pltpu.VMEM((8 * pl.cdiv(parts, 8), block_size), jnp.float32),
             pltpu.VMEM((lines, columns), jnp.float32),
-            pltpu.VMEM((lines, 128), jnp.float32),
             pltpu.VMEM((columns + 2 * HALO, lines), jnp.float32),
         ],
+        cost_estimate=pl.CostEstimate(flops=4 * 10**9, transcendentals=0, bytes_accessed=10**6),
         name="project",
-    )(place, data, offsets, view_index, taps, view_weight, volume, multiplier, edge)
-
-
-def smooth_kernel(planes, place_ref, parts_ref, out_ref):
+    )(data, offsets, view_index, taps, view_weight, volume, multiplier)
+
+
+def close_kernel(parts_ref, left_ref, right_ref, out_ref, halo_ref):
+    ang = lax.axis_index("ang")
+    dests, window, lines = parts_ref.shape
+    local_lines = left_ref.shape[0]
+    halo_ref[...] = jnp.zeros_like(halo_ref)
+    own = pl.ds(pl.multiple_of(ang * local_lines, 8), local_lines)
+    halo_ref[own, pl.ds(0, HALO)] = left_ref[...]
+    halo_ref[own, pl.ds(HALO, HALO)] = right_ref[...]
+    edges = halo_ref[...].T
+    out_ref[0, pl.ds(0, HALO), :] = parts_ref[0, pl.ds(0, HALO), :] + edges[:HALO]
+    last = pl.ds(window - HALO, HALO)
+    out_ref[dests - 1, last, :] = parts_ref[dests - 1, last, :] + edges[HALO : 2 * HALO]
+
+
+def close(parts, left, right):
+    vmem = pl.BlockSpec(memory_space=pltpu.VMEM)
+    return pl.pallas_call(
+        close_kernel,
+        out_shape=pltpu.VMEM(parts.shape, parts.dtype),
+        in_specs=[vmem] * 3,
+        out_specs=vmem,
+        scratch_shapes=[pltpu.VMEM((parts.shape[2], 128), jnp.float32)],
+        input_output_aliases={0: 0},
+        name="close",
+    )(parts, left, right)
+
+
+def smooth_kernel(planes, columns, parts_ref, out_ref):
     dests, local_lines, block = out_ref.shape
     sources, window, lines = parts_ref.shape
     groups = dests * local_lines // lines
@@ -163,7 +190,8 @@
     rows = lines // planes
     lane = lax.broadcasted_iota(jnp.int32, (window, lines), 1)
     lane_row = lane % rows
-    column = place_ref[2] + lax.broadcasted_iota(jnp.int32, (window, lines), 0)
+    place = lax.axis_index("ang") * groups + lax.axis_index("gy")
+    column = lax.axis_index("gx") * columns + place * block - HALO + lax.broadcasted_iota(jnp.int32, (window, lines), 0)
     plane_open = lane // rows < planes - 1
     row_first = lane_row == 0
     row_last = lane_row == rows - 1
@@ -231,16 +259,16 @@
         flow = updated
 
 
-def smooth(place, parts, planes, local_lines):
+def smooth(parts, planes, local_lines, columns):
     sources, window, lines = parts.shape
     vmem = pl.BlockSpec(memory_space=pltpu.VMEM)
     return pl.pallas_call(
-        functools.partial(smooth_kernel, planes),
-        out_shape=jax.ShapeDtypeStruct((sources, local_lines, window - 2 * HALO), jnp.float32),
-        in_specs=[pl.BlockSpec(memory_space=pltpu.SMEM), vmem],
+        functools.partial(smooth_kernel, planes, columns),
+        out_shape=pltpu.VMEM((sources, local_lines, window - 2 * HALO), jnp.float32),
+        in_specs=[vmem],
         out_specs=vmem,
         name="smooth",
-    )(place, parts)
+    )(parts)
 
 
 def passed_along(block, axis, distance):
@@ -254,35 +282,29 @@
     planes = spectrum_data.shape[1]
     samples = spectrum_data.shape[3]
     dests = lax.axis_size("ang") * lax.axis_size("gy")
-    block = columns // dests
     local_lines = local_planes * rows
     lines = planes * rows
-    ang, gy, gx = lax.axis_index("ang"), lax.axis_index("gy"), lax.axis_index("gx")
-    first_column = gx * columns + (ang * lax.axis_size("gy") + gy) * block - HALO
-    place = jnp.stack([ang, gx, first_column]).astype(jnp.int32)
 
     volume = volume.reshape(local_lines, columns)
     multiplier = multiplier.reshape(local_lines, columns)
     left = passed_along(volume[:, -HALO:] + multiplier[:, -HALO:], "gx", 1)
     right = passed_along(volume[:, :HALO] + multiplier[:, :HALO], "gx", -1)
-    edge = jnp.pad(jnp.concatenate([left, right], axis=1), ((0, 0), (0, 128 - 2 * HALO)))
-    views = view_weight.shape[0]
-    weight_rows = -(-views // 128)
-    table = jnp.pad(view_weight, (0, weight_rows * 128 - views)).reshape(weight_rows, 128)
     parts = project(
-        place,
         spectrum_data.reshape(2 * lines, samples),
         offsets.reshape(samples // 128, 128),
         view_index.reshape(samples // 128, 128),
         kernel,
-        table,
+        view_weight,
         volume,
         multiplier,
-        edge,
         dests,
     )
+    left = pltpu.with_memory_space_constraint(left, pltpu.VMEM)
+    right = pltpu.with_memory_space_constraint(right, pltpu.VMEM)
+    parts = close(parts, left, right)
     parts = lax.all_to_all(parts, ("ang", "gy"), split_axis=0, concat_axis=0)
-    done = smooth(place, parts, planes, local_lines)
+    parts = pltpu.with_memory_space_constraint(parts, pltpu.VMEM)
+    done = smooth(parts, planes, local_lines, columns)
     done = lax.all_to_all(done, ("ang", "gy"), split_axis=0, concat_axis=0)
     return jnp.transpose(done, (1, 0, 2)).reshape(local_planes, rows, columns)
 

time: 44.6 us -> 36.6 us (0.82)
  Pallas kernels: 8.23 us -> 5.85 us
  waiting for transfers between devices: 2.39 us -> 0.03 us
  other arithmetic: 2.17 us -> 0.84 us
  local copies, waits for them, and re-layouts: 2.04 us -> 0.76 us
  blocking collectives: 23 us -> 21.9 us
  starting transfers between devices: 6.24 us -> 6.87 us
    pallas_call x2 -> x3, Pallas kernels: 8.23 us -> 5.85 us  [the longest x1 4.21 us: project(): pl.pallas_call(project_kernel, out_shape=pltpu.VMEM((dests, window, lines...]
    ppermute x2, waiting for transfers between devices: 2.39 us -> 0.03 us  [passed_along(): return lax.ppermute(block, axis, route)]
    all_to_all x1, blocking collectives: 8.78 us -> 7.89 us  [per_device(): done = lax.all_to_all(done, ('ang', 'gy'), split_axis=0, concat_axis=0)]
    unnamed x2 -> x0, local copies, waits for them, and re-layouts: 0.69 us -> none
    concatenate x1 -> x0, other arithmetic: 0.68 us -> none  [per_device(): jnp.concatenate([left, right], axis=1)]
    another operation x1 -> x0, other arithmetic: 0.65 us -> none  [per_device(): place = jnp.stack([ang, gx, first_column]).astype(jnp.int32)]
    ppermute x2, starting transfers between devices: 6.24 us -> 6.87 us  [passed_along(): return lax.ppermute(block, axis, route)]
    reshape x1 -> x0, local copies, waits for them, and re-layouts: 0.59 us -> none  [per_device(): jnp.pad(view_weight, (0, weight_rows * 128 - views))]
  transfers between devices with their start and end apart: 2 -> 2, of which waited for: 1 -> 0; matrix products, arithmetic and copies ran while one was open for 3% -> 0% of each run, Pallas kernels for 0% -> 12%
where the time goes in v2:
time: 36.6 us; the launch traced here: 36.3 us
  blocking collectives  21.9 us (60%)
  starting transfers between devices  6.87 us (19%)
  Pallas kernels  5.85 us (16%)
  other arithmetic  0.84 us (2%)
  local copies, waits for them, and re-layouts  0.76 us (2%)
    all_to_all x1, blocking collectives, per_device(): parts = lax.all_to_all(parts, ('ang', 'gy'), split_axis=0, concat_axis=0)  14 us
    all_to_all x1, blocking collectives, per_device(): done = lax.all_to_all(done, ('ang', 'gy'), split_axis=0, concat_axis=0)  7.89 us
    ppermute x2, starting transfers between devices, passed_along(): return lax.ppermute(block, axis, route)  6.87 us
    pallas_call x1, Pallas kernels, project(): pl.pallas_call(project_kernel, out_shape=pltpu.VMEM((dests, window, lines...  4.21 us
    pallas_call x1, Pallas kernels, smooth(): pl.pallas_call(functools.partial(smooth_kernel, planes, columns), out_sha...  1.51 us
    add x1, other arithmetic, per_device(): right = passed_along(volume[:, :HALO] + multiplier[:, :HALO], 'gx', -1)  0.84 us
  transfers between devices with their start and end apart: 2, of which 0 were waited for; matrix products, arithmetic and copies ran while one was open for 0% of the time, Pallas kernels for 12%

profile of v2, /device:TPU:0, one launch (start us, length us, event | category | flops | bytes accessed | tf_op | source)
XLA Modules:
  0.0 36.3 jit_solution(1212572456802258462)
XLA Ops:
  0.0 0.8 %slice_add_fusion = (f32[32,4]{1,0:T(8,128)S(1)}, f32[32,4]{1,0:T(8,128)S(1)}) fusion(f32[32,1024]{1,0:T(8,128)} %bitcast.9, f32[32,1024]{1,0:T(8,128)} %bitcast.7), kind=kLoop, calls=%fused_computation | loop fusion | flops 256 | bytes 3072 | tf_op jit(solution)/shard_map/add | solution.py:291
  0.8 1.3 %collective-permute-start.1 = (f32[32,4]{1,0:T(8,128)S(1)}, f32[32,4]{1,0:T(8,128)S(1)}, u32[]{:S(2)}, u32[]{:S(2)}) collective-permute-start(f32[32,4]{1,0:T(8,128)S(1)} %get-tuple-element.5), channel_id=1, source_target_pairs={{1,0},{2,1},{3,2},{5,4},{6,5},{7,6},{9,8},{10,9},{11,10},{13,12},{... | collective-permute-start | bytes 1544 | tf_op jit(solution)/shard_map/ppermute | solution.py:277
  2.1 5.6 %collective-permute-start = (f32[32,4]{1,0:T(8,128)S(1)}, f32[32,4]{1,0:T(8,128)S(1)}, u32[]{:S(2)}, u32[]{:S(2)}) collective-permute-start(f32[32,4]{1,0:T(8,128)S(1)} %get-tuple-element.6), channel_id=1, source_target_pairs={{0,1},{1,2},{2,3},{4,5},{5,6},{6,7},{8,9},{9,10},{10,11},{12,13},{... | collective-permute-start | bytes 1544 | tf_op jit(solution)/shard_map/ppermute | solution.py:277
  7.7 4.2 %project.1.parts_ref = f32[8,136,128]{2,1,0:T(8,128)S(1)} custom-call(bf16[256,512]{1,0:T(8,128)(2,1)} %bitcast.11, s32[4,128]{1,0:T(4,128)} %bitcast.12, s32[4,128]{1,0:T(4,128)} %bitcast.13, f32[4,512]{1,0:T(4,128)} %taps_ref.1, f32[1500]{0:T(1024)} %weight_ref.1, f32[32,1024]{1,0:T(8,128)} %bitcast.8, f32[32,1024]{1,0:T(8,128)} %bitcast.10), custom_call_target="tpu_custom_call" | custom-call | flops 4000000000 | bytes 1000000 | tf_op jit(solution)/shard_map/project/pallas_call | solution.py:136
  11.9 0.0 collective-permute-done.1.right_ref
  11.9 0.0 collective-permute-done.left_ref
  12.0 0.1 close.1
  12.1 14.0 %all_to_all.10.parts_ref = f32[8,136,128]{2,1,0:T(8,128)S(1)} all-to-all(f32[8,136,128]{2,1,0:T(8,128)S(1)} %close.1), channel_id=1, replica_groups=mesh['ang'=4,'gy'=2,'gx'=4] {'ang','gy'}, dimensions={0} | all-to-all | bytes 1114112 | tf_op jit(solution)/shard_map/all_to_all | solution.py:305
  26.1 1.5 %smooth.1 = f32[8,32,128]{2,1,0:T(8,128)S(1)} custom-call(f32[8,136,128]{2,1,0:T(8,128)S(1)} %all_to_all.10.parts_ref), custom_call_target="tpu_custom_call" | custom-call | tf_op jit(solution)/shard_map/smooth/pallas_call | solution.py:265
  27.6 7.9 %all_to_all.11 = f32[8,32,128]{2,1,0:T(8,128)S(1)} all-to-all(f32[8,32,128]{2,1,0:T(8,128)S(1)} %smooth.1), channel_id=1, replica_groups=mesh['ang'=4,'gy'=2,'gx'=4] {'ang','gy'}, dimensions={0} | all-to-all | bytes 262144 | tf_op jit(solution)/shard_map/all_to_all | solution.py:308
  35.5 0.1 copy.9
  35.6 0.7 %reshape.23 = f32[4,8,1024]{2,1,0:T(8,128)} reshape(f32[32,8,128]{2,1,0:T(8,128)S(1)} %copy.9) | data formatting | bytes 262144 | tf_op jit(solution)/shard_map/reshape | solution.py:309
Async XLA Ops:
  0.8 11.1 %collective-permute-start.1 = (f32[32,4]{1,0:T(8,128)S(1)}, f32[32,4]{1,0:T(8,128)S(1)}, u32[]{:S(2)}, u32[]{:S(2)}) collective-permute-start(f32[32,4]{1,0:T(8,128)S(1)} %get-tuple-element.5), channel_id=1, source_target_pairs={{1,0},{2,1},{3,2},{5,4},{6,5},{7,6},{9,8},{10,9},{11,10},{13,12},{... | collective-permute-start | bytes 1544 | tf_op jit(solution)/shard_map/ppermute | solution.py:277
  2.1 9.8 %collective-permute-start = (f32[32,4]{1,0:T(8,128)S(1)}, f32[32,4]{1,0:T(8,128)S(1)}, u32[]{:S(2)}, u32[]{:S(2)}) collective-permute-start(f32[32,4]{1,0:T(8,128)S(1)} %get-tuple-element.6), channel_id=1, source_target_pairs={{0,1},{1,2},{2,3},{4,5},{5,6},{6,7},{8,9},{9,10},{10,11},{12,13},{... | collective-permute-start | bytes 1544 | tf_op jit(solution)/shard_map/ppermute | solution.py:277

commit v3 on v2

--- a/solution.py
+++ b/solution.py
@@ -155,21 +155,23 @@
     )(data, offsets, view_index, taps, view_weight, volume, multiplier)
 
 
-def close_kernel(parts_ref, left_ref, right_ref, out_ref, halo_ref):
+def close_kernel(parts_ref, inner_ref, outer_ref, out_ref, halo_ref):
     ang = lax.axis_index("ang")
+    even = lax.axis_index("gx") % 2 == 0
     dests, window, lines = parts_ref.shape
-    local_lines = left_ref.shape[0]
+    local_lines = inner_ref.shape[0]
     halo_ref[...] = jnp.zeros_like(halo_ref)
     own = pl.ds(pl.multiple_of(ang * local_lines, 8), local_lines)
-    halo_ref[own, pl.ds(0, HALO)] = left_ref[...]
-    halo_ref[own, pl.ds(HALO, HALO)] = right_ref[...]
+    inner, outer = inner_ref[...], outer_ref[...]
+    halo_ref[own, pl.ds(0, HALO)] = jnp.where(even, outer, inner)
+    halo_ref[own, pl.ds(HALO, HALO)] = jnp.where(even, inner, outer)
     edges = halo_ref[...].T
     out_ref[0, pl.ds(0, HALO), :] = parts_ref[0, pl.ds(0, HALO), :] + edges[:HALO]
     last = pl.ds(window - HALO, HALO)
     out_ref[dests - 1, last, :] = parts_ref[dests - 1, last, :] + edges[HALO : 2 * HALO]
 
 
-def close(parts, left, right):
+def close(parts, inner, outer):
     vmem = pl.BlockSpec(memory_space=pltpu.VMEM)
     return pl.pallas_call(
         close_kernel,
@@ -179,7 +181,7 @@
         scratch_shapes=[pltpu.VMEM((parts.shape[2], 128), jnp.float32)],
         input_output_aliases={0: 0},
         name="close",
-    )(parts, left, right)
+    )(parts, inner, outer)
 
 
 def smooth_kernel(planes, columns, parts_ref, out_ref):
@@ -271,9 +273,12 @@
     )(parts)
 
 
-def passed_along(block, axis, distance):
-    devices = range(lax.axis_size(axis))
-    route = [(i - distance, i) for i in devices if i - distance in devices]
+def exchanged(block, axis, shift):
+    count = lax.axis_size(axis)
+    route = []
+    for low in range(shift, count + shift - 1, 2):
+        pair = (low % count, (low + 1) % count)
+        route += [pair, pair[::-1]]
     return lax.ppermute(block, axis, route)
 
 
@@ -287,8 +292,11 @@
 
     volume = volume.reshape(local_lines, columns)
     multiplier = multiplier.reshape(local_lines, columns)
-    left = passed_along(volume[:, -HALO:] + multiplier[:, -HALO:], "gx", 1)
-    right = passed_along(volume[:, :HALO] + multiplier[:, :HALO], "gx", -1)
+    first_edge = volume[:, :HALO] + multiplier[:, :HALO]
+    last_edge = volume[:, -HALO:] + multiplier[:, -HALO:]
+    even = lax.axis_index("gx") % 2 == 0
+    inner = exchanged(jnp.where(even, last_edge, first_edge), "gx", 0)
+    outer = exchanged(jnp.where(even, first_edge, last_edge), "gx", 1)
     parts = project(
         spectrum_data.reshape(2 * lines, samples),
         offsets.reshape(samples // 128, 128),
@@ -299,9 +307,9 @@
         multiplier,
         dests,
     )
-    left = pltpu.with_memory_space_constraint(left, pltpu.VMEM)
-    right = pltpu.with_memory_space_constraint(right, pltpu.VMEM)
-    parts = close(parts, left, right)
+    inner = pltpu.with_memory_space_constraint(inner, pltpu.VMEM)
+    outer = pltpu.with_memory_space_constraint(outer, pltpu.VMEM)
+    parts = close(parts, inner, outer)
     parts = lax.all_to_all(parts, ("ang", "gy"), split_axis=0, concat_axis=0)
     parts = pltpu.with_memory_space_constraint(parts, pltpu.VMEM)
     done = smooth(parts, planes, local_lines, columns)

time: 36.6 us -> 34.3 us (0.937)
  starting transfers between devices: 6.87 us -> 5.09 us
  blocking collectives: 21.9 us -> 21.5 us
    ppermute x2, starting transfers between devices: 6.87 us -> 5.09 us  [exchanged(): return lax.ppermute(block, axis, route)]
    select_n x0 -> x1, other arithmetic: none -> 0.84 us  [per_device(): outer = exchanged(jnp.where(even, first_edge, last_edge), 'gx', 1)]
    add x1 -> x0, other arithmetic: 0.84 us -> none  [per_device(): right = passed_along(volume[:, :HALO] + multiplier[:, :HALO], 'gx', -1)]
    all_to_all x1, blocking collectives: 14 us -> 13.6 us  [per_device(): parts = lax.all_to_all(parts, ('ang', 'gy'), split_axis=0, concat_axis=0)]
where the time goes in v3:
time: 34.3 us; the launch traced here: 34.1 us
  blocking collectives  21.5 us (63%)
  Pallas kernels  5.86 us (17%)
  starting transfers between devices  5.09 us (15%)
  other arithmetic  0.84 us (2%)
  local copies, waits for them, and re-layouts  0.76 us (2%)
    all_to_all x1, blocking collectives, per_device(): parts = lax.all_to_all(parts, ('ang', 'gy'), split_axis=0, concat_axis=0)  13.6 us
    all_to_all x1, blocking collectives, per_device(): done = lax.all_to_all(done, ('ang', 'gy'), split_axis=0, concat_axis=0)  7.89 us
    ppermute x2, starting transfers between devices, exchanged(): return lax.ppermute(block, axis, route)  5.09 us
    pallas_call x1, Pallas kernels, project(): pl.pallas_call(project_kernel, out_shape=pltpu.VMEM((dests, window, lines...  4.21 us
    pallas_call x1, Pallas kernels, smooth(): pl.pallas_call(functools.partial(smooth_kernel, planes, columns), out_sha...  1.51 us
    select_n x1, other arithmetic, per_device(): outer = exchanged(jnp.where(even, first_edge, last_edge), 'gx', 1)  0.84 us
  transfers between devices with their start and end apart: 2, of which 0 were waited for; matrix products, arithmetic and copies ran while one was open for 0% of the time, Pallas kernels for 12%

profile of v3, /device:TPU:0, one launch (start us, length us, event | category | flops | bytes accessed | tf_op | source)
XLA Modules:
  0.0 34.1 jit_solution(13387902559900891947)
XLA Ops:
  0.0 0.8 %broadcast_select_fusion = (f32[32,4]{1,0:T(8,128)S(1)}, f32[32,4]{1,0:T(8,128)S(1)}) fusion(pred[]{:T(512)S(6)} %eq.5, f32[32,1024]{1,0:T(8,128)} %bitcast.9, f32[32,1024]{1,0:T(8,128)} %bitcast.7), kind=kLoop, calls=%fused_computation.2 | loop fusion | flops 512 | bytes 3073 | tf_op jit(solution)/shard_map/jit(_where)/select_n | solution.py:299
  0.8 5.1 %collective-permute-start.1 = (f32[32,4]{1,0:T(8,128)S(1)}, f32[32,4]{1,0:T(8,128)S(1)}, u32[]{:S(2)}, u32[]{:S(2)}) collective-permute-start(f32[32,4]{1,0:T(8,128)S(1)} %get-tuple-element.5), channel_id=1, source_target_pairs={{1,2},{2,1},{3,0},{0,3},{5,6},{6,5},{7,4},{4,7},{9,10},{10,9},{11,... | collective-permute-start | bytes 1544 | tf_op jit(solution)/shard_map/ppermute | solution.py:282
  5.9 0.0 collective-permute-start
  5.9 4.2 %project.1.parts_ref = f32[8,136,128]{2,1,0:T(8,128)S(1)} custom-call(bf16[256,512]{1,0:T(8,128)(2,1)} %bitcast.11, s32[4,128]{1,0:T(4,128)} %bitcast.12, s32[4,128]{1,0:T(4,128)} %bitcast.13, f32[4,512]{1,0:T(4,128)} %taps_ref.1, f32[1500]{0:T(1024)} %weight_ref.1, f32[32,1024]{1,0:T(8,128)} %bitcast.8, f32[32,1024]{1,0:T(8,128)} %bitcast.10), custom_call_target="tpu_custom_call" | custom-call | flops 4000000000 | bytes 1000000 | tf_op jit(solution)/shard_map/project/pallas_call | solution.py:136
  10.1 0.0 collective-permute-done.1.outer_ref
  10.1 0.0 collective-permute-done.inner_ref
  10.2 0.1 close.1
  10.3 13.6 %all_to_all.10.parts_ref = f32[8,136,128]{2,1,0:T(8,128)S(1)} all-to-all(f32[8,136,128]{2,1,0:T(8,128)S(1)} %close.1), channel_id=1, replica_groups=mesh['ang'=4,'gy'=2,'gx'=4] {'ang','gy'}, dimensions={0} | all-to-all | bytes 1114112 | tf_op jit(solution)/shard_map/all_to_all | solution.py:313
  23.9 1.5 %smooth.1 = f32[8,32,128]{2,1,0:T(8,128)S(1)} custom-call(f32[8,136,128]{2,1,0:T(8,128)S(1)} %all_to_all.10.parts_ref), custom_call_target="tpu_custom_call" | custom-call | tf_op jit(solution)/shard_map/smooth/pallas_call | solution.py:267
  25.4 7.9 %all_to_all.11 = f32[8,32,128]{2,1,0:T(8,128)S(1)} all-to-all(f32[8,32,128]{2,1,0:T(8,128)S(1)} %smooth.1), channel_id=1, replica_groups=mesh['ang'=4,'gy'=2,'gx'=4] {'ang','gy'}, dimensions={0} | all-to-all | bytes 262144 | tf_op jit(solution)/shard_map/all_to_all | solution.py:316
  33.3 0.1 copy.9
  33.4 0.7 %reshape.23 = f32[4,8,1024]{2,1,0:T(8,128)} reshape(f32[32,8,128]{2,1,0:T(8,128)S(1)} %copy.9) | data formatting | bytes 262144 | tf_op jit(solution)/shard_map/reshape | solution.py:317
Async XLA Ops:
  0.8 9.3 %collective-permute-start.1 = (f32[32,4]{1,0:T(8,128)S(1)}, f32[32,4]{1,0:T(8,128)S(1)}, u32[]{:S(2)}, u32[]{:S(2)}) collective-permute-start(f32[32,4]{1,0:T(8,128)S(1)} %get-tuple-element.5), channel_id=1, source_target_pairs={{1,2},{2,1},{3,0},{0,3},{5,6},{6,5},{7,4},{4,7},{9,10},{10,9},{11,... | collective-permute-start | bytes 1544 | tf_op jit(solution)/shard_map/ppermute | solution.py:282
  5.9 4.2 %collective-permute-start = (f32[32,4]{1,0:T(8,128)S(1)}, f32[32,4]{1,0:T(8,128)S(1)}, u32[]{:S(2)}, u32[]{:S(2)}) collective-permute-start(f32[32,4]{1,0:T(8,128)S(1)} %get-tuple-element.6), channel_id=1, source_target_pairs={{0,1},{1,0},{2,3},{3,2},{4,5},{5,4},{6,7},{7,6},{8,9},{9,8},{10,11... | collective-permute-start | bytes 1544 | tf_op jit(solution)/shard_map/ppermute | solution.py:282

commit v4 on v3

--- a/solution.py
+++ b/solution.py
@@ -12,6 +12,7 @@
 TV_STEPS = 4
 HALO = TV_STEPS
 CHUNK = 128
+VMEM_LIMIT = 24 * 2**20
 
 smooth_weight = 0.5
 dual_step = 1.0 / 12.0
@@ -33,20 +34,8 @@
     return jnp.where(flip, -first, first), jnp.where(flip, -second, second)
 
 
-def project_kernel(
-    data_ref, offsets_ref, view_ref, taps_ref, weight_ref, volume_ref, multiplier_ref,
-    out_ref,
-    spread_ref, grid_ref, cos_ref, sin_ref, step_cos_ref, step_sin_ref, part_cos_ref, part_sin_ref, lines_ref, vm_ref,
-):
-    ang, gx = lax.axis_index("ang"), lax.axis_index("gx")
-    samples = data_ref.shape[1]
-    lines = data_ref.shape[0] // 2
-    block_size = spread_ref.shape[0]
-    columns = volume_ref.shape[1]
-    local_lines = volume_ref.shape[0]
-    dests, window, _ = out_ref.shape
-    block = window - 2 * HALO
-
+def make_spread(offsets_ref, view_ref, taps_ref, weight_ref, spread_ref):
+    block_size, samples = spread_ref.shape
     views = weight_ref.shape[0]
     pieces = []
     for piece in range(samples // 128):
@@ -75,6 +64,61 @@
             spread = jnp.where(tap == index, value, spread)
         spread_ref[pl.ds(first, rows), :] = spread.astype(jnp.bfloat16)
 
+
+def make_angles(first_column, step_cos_ref, step_sin_ref, part_cos_ref, part_sin_ref):
+    block_size = step_cos_ref.shape[1]
+    freq = lax.axis_index("ang") * block_size + lax.broadcasted_iota(jnp.int32, (8, block_size), 1)
+    row = lax.broadcasted_iota(jnp.int32, (8, block_size), 0)
+    for first in range(0, CHUNK // 8, 8):
+        step_cos_ref[pl.ds(first, 8), :], step_sin_ref[pl.ds(first, 8), :] = unit_circle(freq * (8 * (row + first)))
+    for first in range(0, part_cos_ref.shape[0], 8):
+        part_cos_ref[pl.ds(first, 8), :], part_sin_ref[pl.ds(first, 8), :] = unit_circle(
+            freq * (CHUNK * (row + first))
+        )
+    return unit_circle(freq * (first_column + row))
+
+
+def make_waves(base, part, count, step_cos_ref, step_sin_ref, part_cos_ref, part_sin_ref, put):
+    base_cos, base_sin = base
+    part_cos, part_sin = part_cos_ref[pl.ds(part, 1), :], part_sin_ref[pl.ds(part, 1), :]
+    here_cos = base_cos * part_cos - base_sin * part_sin
+    here_sin = base_sin * part_cos + base_cos * part_sin
+    for step in range(0, pl.cdiv(count, 8), 2):
+        pair_cos, pair_sin = [], []
+        for one in (step, step + 1):
+            step_cos, step_sin = step_cos_ref[pl.ds(one, 1), :], step_sin_ref[pl.ds(one, 1), :]
+            pair_cos.append(here_cos * step_cos - here_sin * step_sin)
+            pair_sin.append(-(here_sin * step_cos + here_cos * step_sin))
+        put(
+            8 * step,
+            jnp.concatenate(pair_cos, axis=0).astype(jnp.bfloat16),
+            jnp.concatenate(pair_sin, axis=0).astype(jnp.bfloat16),
+        )
+
+
+def chunks(total):
+    return [(part, part * CHUNK, min(CHUNK, total - part * CHUNK)) for part in range(pl.cdiv(total, CHUNK))]
+
+
+def put_windows(out_ref, first, count, sent):
+    dests, window, _ = out_ref.shape
+    block = window - 2 * HALO
+    for dest in range(dests):
+        low, high = max(first, dest * block), min(first + count, dest * block + window)
+        if low < high:
+            out_ref[dest, pl.ds(low - dest * block, high - low), :] = sent[low - first : high - first]
+
+
+def project_kernel(
+    data_ref, offsets_ref, view_ref, taps_ref, weight_ref, volume_ref, multiplier_ref,
+    out_ref,
+    spread_ref, grid_ref, cos_ref, sin_ref, step_cos_ref, step_sin_ref, part_cos_ref, part_sin_ref, lines_ref, vm_ref,
+):
+    ang, gx = lax.axis_index("ang"), lax.axis_index("gx")
+    lines = data_ref.shape[0] // 2
+    local_lines, columns = volume_ref.shape
+
+    make_spread(offsets_ref, view_ref, taps_ref, weight_ref, spread_ref)
     grid_ref[...] = lax.dot_general(
         data_ref[...], spread_ref[...], NT, preferred_element_type=jnp.float32
     ).astype(jnp.bfloat16)
@@ -86,43 +130,23 @@
     for first in range(0, columns, 128):
         vm_ref[pl.ds(HALO + first, 128), :] = lines_ref[:, pl.ds(first, 128)].T
 
-    freq = ang * block_size + lax.broadcasted_iota(jnp.int32, (8, block_size), 1)
-    row = lax.broadcasted_iota(jnp.int32, (8, block_size), 0)
-    base_cos, base_sin = unit_circle(freq * (gx * columns - HALO + row))
-    for first in range(0, CHUNK // 8, 8):
-        step_cos_ref[pl.ds(first, 8), :], step_sin_ref[pl.ds(first, 8), :] = unit_circle(freq * (8 * (row + first)))
-    for first in range(0, part_cos_ref.shape[0], 8):
-        part_cos_ref[pl.ds(first, 8), :], part_sin_ref[pl.ds(first, 8), :] = unit_circle(
-            freq * (CHUNK * (row + first))
-        )
-
-    total = columns + 2 * HALO
-    for part in range(pl.cdiv(total, CHUNK)):
-        first = part * CHUNK
-        count = min(CHUNK, total - first)
+    angles = (step_cos_ref, step_sin_ref, part_cos_ref, part_sin_ref)
+    base = make_angles(gx * columns - HALO, *angles)
+    for part, first, count in chunks(columns + 2 * HALO):
         slot = part % 2
-        part_cos, part_sin = part_cos_ref[pl.ds(part, 1), :], part_sin_ref[pl.ds(part, 1), :]
-        here_cos = base_cos * part_cos - base_sin * part_sin
-        here_sin = base_sin * part_cos + base_cos * part_sin
-        for step in range(0, pl.cdiv(count, 8), 2):
-            pair_cos, pair_sin = [], []
-            for one in (step, step + 1):
-                step_cos, step_sin = step_cos_ref[pl.ds(one, 1), :], step_sin_ref[pl.ds(one, 1), :]
-                pair_cos.append(here_cos * step_cos - here_sin * step_sin)
-                pair_sin.append(-(here_sin * step_cos + here_cos * step_sin))
-            cos_ref[slot, pl.ds(8 * step, 16), :] = jnp.concatenate(pair_cos, axis=0).astype(jnp.bfloat16)
-            sin_ref[slot, pl.ds(8 * step, 16), :] = jnp.concatenate(pair_sin, axis=0).astype(jnp.bfloat16)
+
+        def put(at, cosines, sines):
+            cos_ref[slot, pl.ds(at, 16), :] = cosines
+            sin_ref[slot, pl.ds(at, 16), :] = sines
+
+        make_waves(base, part, count, *angles, put)
         made = max(16, count)
         total_part = lax.dot_general(
             cos_ref[slot, pl.ds(0, made), :], grid_ref[pl.ds(0, lines), :], NT, preferred_element_type=jnp.float32
         ) + lax.dot_general(
             sin_ref[slot, pl.ds(0, made), :], grid_ref[pl.ds(lines, lines), :], NT, preferred_element_type=jnp.float32
         )
-        sent = vm_ref[pl.ds(first, count), :] - total_part[:count] * NX ** (-0.5)
-        for dest in range(dests):
-            low, high = max(first, dest * block), min(first + count, dest * block + window)
-            if low < high:
-                out_ref[dest, pl.ds(low - dest * block, high - low), :] = sent[low - first : high - first]
+        put_windows(out_ref, first, count, vm_ref[pl.ds(first, count), :] - total_part[:count] * NX ** (-0.5))
 
 
 def project(data, offsets, view_index, taps, view_weight, volume, multiplier, dests):
@@ -151,6 +175,7 @@
             pltpu.VMEM((columns + 2 * HALO, lines), jnp.float32),
         ],
         cost_estimate=pl.CostEstimate(flops=4 * 10**9, transcendentals=0, bytes_accessed=10**6),
+        compiler_params=pltpu.CompilerParams(vmem_limit_bytes=VMEM_LIMIT),
         name="project",
     )(data, offsets, view_index, taps, view_weight, volume, multiplier)
 
@@ -180,19 +205,21 @@
         out_specs=vmem,
         scratch_shapes=[pltpu.VMEM((parts.shape[2], 128), jnp.float32)],
         input_output_aliases={0: 0},
+        compiler_params=pltpu.CompilerParams(vmem_limit_bytes=VMEM_LIMIT),
         name="close",
     )(parts, inner, outer)
 
 
 def smooth_kernel(planes, columns, parts_ref, out_ref):
     dests, local_lines, block = out_ref.shape
-    sources, window, lines = parts_ref.shape
-    groups = dests * local_lines // lines
-    angs = sources // groups
+    window = parts_ref.shape[1]
+    angs, groups = lax.axis_size("ang"), lax.axis_size("gy")
+    lines = angs * local_lines
     rows = lines // planes
+    joined = parts_ref.shape[0] == angs
     lane = lax.broadcasted_iota(jnp.int32, (window, lines), 1)
     lane_row = lane % rows
-    place = lax.axis_index("ang") * groups + lax.axis_index("gy")
+    place = lax.axis_index("gy") * angs + lax.axis_index("ang")
     column = lax.axis_index("gx") * columns + place * block - HALO + lax.broadcasted_iota(jnp.int32, (window, lines), 0)
     plane_open = lane // rows < planes - 1
     row_first = lane_row == 0
@@ -202,9 +229,13 @@
 
     source = []
     for group in range(groups):
-        total = parts_ref[group]
-        for ang in range(1, angs):
-            total = total + parts_ref[ang * groups + group]
+        total = None
+        for ang in range(angs):
+            if joined:
+                part = parts_ref[ang, :, pl.ds(group * lines, lines)]
+            else:
+                part = parts_ref[group * angs + ang]
+            total = part if total is None else total + part
         source.append(total)
     scaled = [value / smooth_weight for value in source]
 
@@ -237,7 +268,7 @@
                     done = source[group] - smooth_weight * local_div[group]
                     turned = done[HALO : HALO + block].T
                     for ang in range(angs):
-                        out_ref[ang * groups + group] = turned[ang * local_lines : (ang + 1) * local_lines]
+                        out_ref[group * angs + ang] = turned[ang * local_lines : (ang + 1) * local_lines]
                 return
             target = [local_div[group] - scaled[group] for group in range(groups)]
         updated = []
@@ -262,13 +293,15 @@
 
 
 def smooth(parts, planes, local_lines, columns):
-    sources, window, lines = parts.shape
+    window = parts.shape[1]
+    dests = lax.axis_size("ang") * lax.axis_size("gy")
     vmem = pl.BlockSpec(memory_space=pltpu.VMEM)
     return pl.pallas_call(
         functools.partial(smooth_kernel, planes, columns),
-        out_shape=pltpu.VMEM((sources, local_lines, window - 2 * HALO), jnp.float32),
+        out_shape=pltpu.VMEM((dests, local_lines, window - 2 * HALO), jnp.float32),
         in_specs=[vmem],
         out_specs=vmem,
+        compiler_params=pltpu.CompilerParams(vmem_limit_bytes=VMEM_LIMIT),
         name="smooth",
     )(parts)
 
@@ -282,6 +315,264 @@
     return lax.ppermute(block, axis, route)
 
 
+def pack_kernel(
+    data_ref, offsets_ref, view_ref, taps_ref, weight_ref, volume_ref, multiplier_ref,
+    sent_ref, data_out, offsets_out, view_out, taps_out, weight_out, own_ref,
+    volume_here, multiplier_here, sems,
+):
+    rows = data_ref.shape[0]
+    half = volume_ref.shape[1] // 2
+    first = lax.axis_index("gy") == 0
+    pairs = (
+        (data_ref, data_out),
+        (volume_ref, volume_here),
+        (multiplier_ref, multiplier_here),
+        (offsets_ref, offsets_out),
+        (view_ref, view_out),
+        (taps_ref, taps_out),
+        (weight_ref, weight_out),
+    )
+    copies = [pltpu.make_async_copy(source, target, sems.at[at]) for at, (source, target) in enumerate(pairs)]
+    for copy in copies:
+        copy.start()
+    copies[0].wait()
+    sent_ref[pl.ds(0, rows), :] = data_out[...].astype(jnp.float32)
+    copies[1].wait()
+    copies[2].wait()
+    low = volume_here[:, pl.ds(0, half)] + multiplier_here[:, pl.ds(0, half)]
+    high = volume_here[:, pl.ds(half, half)] + multiplier_here[:, pl.ds(half, half)]
+    below, above = low[:, half - HALO :], high[:, :HALO]
+    local_lines = low.shape[0]
+    own_ref[:, pl.ds(0, half)] = jnp.where(first, low, high)
+    own_ref[:, pl.ds(half, HALO)] = jnp.where(first, above, below)
+    sent_ref[pl.ds(rows, local_lines), :] = jnp.where(first, high, low)
+    sent_ref[pl.ds(rows + local_lines, local_lines), pl.ds(0, HALO)] = jnp.where(first, below, above)
+    for copy in copies[3:]:
+        copy.wait()
+
+
+def pack(data, offsets, view_index, taps, view_weight, volume, multiplier):
+    rows, samples = data.shape
+    local_lines, columns = volume.shape
+    vmem = pl.BlockSpec(memory_space=pltpu.VMEM)
+    return pl.pallas_call(
+        pack_kernel,
+        out_shape=[
+            pltpu.VMEM((rows + 2 * local_lines, samples), jnp.float32),
+            pltpu.VMEM(data.shape, data.dtype),
+            pltpu.VMEM(offsets.shape, offsets.dtype),
+            pltpu.VMEM(view_index.shape, view_index.dtype),
+            pltpu.VMEM(taps.shape, taps.dtype),
+            pltpu.VMEM(view_weight.shape, view_weight.dtype),
+            pltpu.VMEM((local_lines, columns // 2 + 128), jnp.float32),
+        ],
+        in_specs=[pl.BlockSpec(memory_space=pltpu.HBM)] * 7,
+        out_specs=[vmem] * 7,
+        scratch_shapes=[
+            pltpu.VMEM(volume.shape, volume.dtype),
+            pltpu.VMEM(multiplier.shape, multiplier.dtype),
+            pltpu.SemaphoreType.DMA((7,)),
+        ],
+        compiler_params=pltpu.CompilerParams(vmem_limit_bytes=VMEM_LIMIT),
+        name="pack",
+    )(
+        *(
+            pltpu.with_memory_space_constraint(array, pltpu.HBM)
+            for array in (data, offsets, view_index, taps, view_weight, volume, multiplier)
+        )
+    )
+
+
+def tables_kernel(
+    columns, offsets_ref, view_ref, taps_ref, weight_ref,
+    spread_ref, cos_ref, sin_ref,
+    step_cos_ref, step_sin_ref, part_cos_ref, part_sin_ref,
+):
+    make_spread(offsets_ref, view_ref, taps_ref, weight_ref, spread_ref)
+    angles = (step_cos_ref, step_sin_ref, part_cos_ref, part_sin_ref)
+    base = make_angles(lax.axis_index("gx") * 2 * columns + lax.axis_index("gy") * columns - HALO, *angles)
+    for part, first, count in chunks(columns + 2 * HALO):
+
+        def put(at, cosines, sines):
+            cos_ref[pl.ds(first + at, 16), :] = cosines
+            sin_ref[pl.ds(first + at, 16), :] = sines
+
+        make_waves(base, part, count, *angles, put)
+
+
+def tables(offsets, view_index, taps, view_weight, columns):
+    samples = taps.shape[1]
+    block_size = NX // lax.axis_size("ang")
+    made = 16 * pl.cdiv(columns + 2 * HALO, 16)
+    parts = 8 * pl.cdiv(pl.cdiv(columns + 2 * HALO, CHUNK), 8)
+    vmem = pl.BlockSpec(memory_space=pltpu.VMEM)
+    return pl.pallas_call(
+        functools.partial(tables_kernel, columns),
+        out_shape=[
+            pltpu.VMEM((block_size, samples), jnp.bfloat16),
+            pltpu.VMEM((made, block_size), jnp.bfloat16),
+            pltpu.VMEM((made, block_size), jnp.bfloat16),
+        ],
+        in_specs=[vmem] * 4,
+        out_specs=[vmem] * 3,
+        scratch_shapes=[
+            pltpu.VMEM((CHUNK // 8, block_size), jnp.float32),
+            pltpu.VMEM((CHUNK // 8, block_size), jnp.float32),
+            pltpu.VMEM((parts, block_size), jnp.float32),
+            pltpu.VMEM((parts, block_size), jnp.float32),
+        ],
+        cost_estimate=pl.CostEstimate(flops=2 * 10**9, transcendentals=0, bytes_accessed=10**6),
+        compiler_params=pltpu.CompilerParams(vmem_limit_bytes=VMEM_LIMIT),
+        name="tables",
+    )(offsets, view_index, taps, view_weight)
+
+
+def line_places(lines, local_lines):
+    gy, inner = lax.axis_index("gy"), lax.axis_index("ang") * local_lines
+    return [
+        pl.ds(pl.multiple_of(group * lines + inner, 8), local_lines) for group in (gy, 1 - gy)
+    ]
+
+
+def edge_kernel(lines, own_ref, got_ref, out_ref, lines_ref):
+    local_lines, half = own_ref.shape[0], own_ref.shape[1] - 128
+    rows = got_ref.shape[0] - 2 * local_lines
+    first = lax.axis_index("gy") == 0
+    lines_ref[...] = jnp.zeros_like(lines_ref)
+    own_place, other_place = line_places(lines, local_lines)
+    other = pl.ds(rows, local_lines)
+    for place, ref, at in ((own_place, own_ref, pl.ds(0, local_lines)), (other_place, got_ref, other)):
+        lines_ref[place, pl.ds(0, HALO)] = jnp.where(
+            first, ref[at, pl.ds(0, HALO)], ref[at, pl.ds(half - HALO, HALO)]
+        )
+    for group in range(2):
+        out_ref[:, pl.ds(group * lines, lines)] = lines_ref[pl.ds(group * lines, lines), :].T[:8]
+
+
+def edge(own, got, lines):
+    vmem = pl.BlockSpec(memory_space=pltpu.VMEM)
+    return pl.pallas_call(
+        functools.partial(edge_kernel, lines),
+        out_shape=pltpu.VMEM((8, 2 * lines), jnp.float32),
+        in_specs=[vmem] * 2,
+        out_specs=vmem,
+        scratch_shapes=[pltpu.VMEM((2 * lines, 128), jnp.float32)],
+        compiler_params=pltpu.CompilerParams(vmem_limit_bytes=VMEM_LIMIT),
+        name="edge",
+    )(own, got)
+
+
+def combine_kernel(
+    data_ref, own_ref, got_ref, spread_ref, cos_ref, sin_ref,
+    out_ref,
+    grid_ref, lines_ref, vm_ref,
+):
+    rows = data_ref.shape[0]
+    lines = rows // 2
+    local_lines, columns = own_ref.shape[0], own_ref.shape[1] - 128
+    gy = lax.axis_index("gy")
+    for group, data in ((gy, data_ref[...]), (1 - gy, got_ref[pl.ds(0, rows), :].astype(jnp.bfloat16))):
+        made = lax.dot_general(data, spread_ref[...], NT, preferred_element_type=jnp.float32).astype(jnp.bfloat16)
+        for component in range(2):
+            place = pl.multiple_of((2 * component + group) * lines, 16)
+            grid_ref[pl.ds(place, lines), :] = made[component * lines : (component + 1) * lines]
+
+    lines_ref[...] = jnp.zeros_like(lines_ref)
+    own_place, other_place = line_places(lines, local_lines)
+    side = pl.ds(columns, HALO)
+    lines_ref[own_place, pl.ds(0, columns)] = own_ref[:, pl.ds(0, columns)]
+    lines_ref[own_place, side] = own_ref[:, side]
+    lines_ref[other_place, pl.ds(0, columns)] = got_ref[pl.ds(rows, local_lines), :]
+    lines_ref[other_place, side] = got_ref[pl.ds(rows + local_lines, local_lines), pl.ds(0, HALO)]
+    for group in range(2):
+        group_lines = pl.ds(group * lines, lines)
+        inner = lines_ref[group_lines, pl.ds(columns, 128)].T[:HALO]
+        vm_ref[pl.ds(0, HALO), group_lines] = jnp.where(gy == 0, 0.0, inner)
+        vm_ref[pl.ds(HALO + columns, HALO), group_lines] = jnp.where(gy == 0, inner, 0.0)
+    for first in range(0, columns, 128):
+        for group in range(2):
+            vm_ref[pl.ds(HALO + first, 128), pl.ds(group * lines, lines)] = lines_ref[
+                pl.ds(group * lines, lines), pl.ds(first, 128)
+            ].T
+
+    for part, first, count in chunks(columns + 2 * HALO):
+        made = pl.ds(first, max(16, count))
+        total = lax.dot_general(
+            cos_ref[made, :], grid_ref[pl.ds(0, 2 * lines), :], NT, preferred_element_type=jnp.float32
+        ) + lax.dot_general(
+            sin_ref[made, :], grid_ref[pl.ds(2 * lines, 2 * lines), :], NT, preferred_element_type=jnp.float32
+        )
+        put_windows(out_ref, first, count, vm_ref[pl.ds(first, count), :] - total[:count] * NX ** (-0.5))
+
+
+def combine(data, own, got, spread, cosines, sines):
+    lines = data.shape[0] // 2
+    columns = own.shape[1] - 128
+    dests = lax.axis_size("ang")
+    vmem = pl.BlockSpec(memory_space=pltpu.VMEM)
+    return pl.pallas_call(
+        combine_kernel,
+        out_shape=pltpu.VMEM((dests, columns // dests + 2 * HALO, 2 * lines), jnp.float32),
+        in_specs=[vmem] * 6,
+        out_specs=vmem,
+        scratch_shapes=[
+            pltpu.VMEM((4 * lines, spread.shape[0]), jnp.bfloat16),
+            pltpu.VMEM((2 * lines, columns + 128), jnp.float32),
+            pltpu.VMEM((columns + 2 * HALO, 2 * lines), jnp.float32),
+        ],
+        cost_estimate=pl.CostEstimate(flops=2 * 10**9, transcendentals=0, bytes_accessed=10**6),
+        compiler_params=pltpu.CompilerParams(vmem_limit_bytes=VMEM_LIMIT),
+        name="combine",
+    )(data, own, got, spread, cosines, sines)
+
+
+def join_kernel(parts_ref, edge_ref, out_ref):
+    dests, window, _ = parts_ref.shape
+    first = lax.axis_index("gy") == 0
+    edge = edge_ref[...][:HALO]
+    out_ref[0, pl.ds(0, HALO), :] = parts_ref[0, pl.ds(0, HALO), :] + jnp.where(first, edge, 0.0)
+    last = pl.ds(window - HALO, HALO)
+    out_ref[dests - 1, last, :] = parts_ref[dests - 1, last, :] + jnp.where(first, 0.0, edge)
+
+
+def join(parts, got_edge):
+    vmem = pl.BlockSpec(memory_space=pltpu.VMEM)
+    return pl.pallas_call(
+        join_kernel,
+        out_shape=pltpu.VMEM(parts.shape, parts.dtype),
+        in_specs=[vmem] * 2,
+        out_specs=vmem,
+        input_output_aliases={0: 0},
+        compiler_params=pltpu.CompilerParams(vmem_limit_bytes=VMEM_LIMIT),
+        name="join",
+    )(parts, got_edge)
+
+
+def on_chip(*arrays):
+    return [pltpu.with_memory_space_constraint(array, pltpu.VMEM) for array in arrays]
+
+
+def project_paired(data, offsets, view_index, taps, view_weight, volume, multiplier):
+    lines = data.shape[0] // 2
+    columns = volume.shape[1] // 2
+    sent, data, offsets, view_index, taps, view_weight, own = pack(
+        data, offsets, view_index, taps, view_weight, volume, multiplier
+    )
+    got = lax.ppermute(sent, "gy", [(0, 1), (1, 0)])
+    spread, cosines, sines = tables(*on_chip(offsets, view_index, taps, view_weight), columns)
+    own, got = on_chip(own, got)
+    count = lax.axis_size("gx")
+    route = []
+    for low in range(count):
+        pair = (count + low, (low + 1) % count)
+        route += [pair, pair[::-1]]
+    got_edge = lax.ppermute(edge(own, got, lines), ("gy", "gx"), route)
+    data, spread, cosines, sines = on_chip(data, spread, cosines, sines)
+    parts = combine(data, own, got, spread, cosines, sines)
+    parts = join(*on_chip(parts, got_edge))
+    return lax.all_to_all(parts, "ang", split_axis=0, concat_axis=0)
+
+
 def per_device(spectrum_data, offsets, view_index, kernel, view_weight, volume, multiplier):
     local_planes, rows, columns = volume.shape
     planes = spectrum_data.shape[1]
@@ -292,12 +583,7 @@
 
     volume = volume.reshape(local_lines, columns)
     multiplier = multiplier.reshape(local_lines, columns)
-    first_edge = volume[:, :HALO] + multiplier[:, :HALO]
-    last_edge = volume[:, -HALO:] + multiplier[:, -HALO:]
-    even = lax.axis_index("gx") % 2 == 0
-    inner = exchanged(jnp.where(even, last_edge, first_edge), "gx", 0)
-    outer = exchanged(jnp.where(even, first_edge, last_edge), "gx", 1)
-    parts = project(
+    arrays = (
         spectrum_data.reshape(2 * lines, samples),
         offsets.reshape(samples // 128, 128),
         view_index.reshape(samples // 128, 128),
@@ -305,15 +591,19 @@
         view_weight,
         volume,
         multiplier,
-        dests,
     )
-    inner = pltpu.with_memory_space_constraint(inner, pltpu.VMEM)
-    outer = pltpu.with_memory_space_constraint(outer, pltpu.VMEM)
-    parts = close(parts, inner, outer)
-    parts = lax.all_to_all(parts, ("ang", "gy"), split_axis=0, concat_axis=0)
-    parts = pltpu.with_memory_space_constraint(parts, pltpu.VMEM)
-    done = smooth(parts, planes, local_lines, columns)
-    done = lax.all_to_all(done, ("ang", "gy"), split_axis=0, concat_axis=0)
+    if lax.axis_size("gy") == 2 and columns // 2 == samples:
+        parts = project_paired(*arrays)
+    else:
+        first_edge = volume[:, :HALO] + multiplier[:, :HALO]
+        last_edge = volume[:, -HALO:] + multiplier[:, -HALO:]
+        even = lax.axis_index("gx") % 2 == 0
+        inner = exchanged(jnp.where(even, last_edge, first_edge), "gx", 0)
+        outer = exchanged(jnp.where(even, first_edge, last_edge), "gx", 1)
+        parts = close(project(*arrays, dests), *on_chip(inner, outer))
+        parts = lax.all_to_all(parts, ("gy", "ang"), split_axis=0, concat_axis=0)
+    done = smooth(*on_chip(parts), planes, local_lines, columns)
+    done = lax.all_to_all(done, ("gy", "ang"), split_axis=0, concat_axis=0)
     return jnp.transpose(done, (1, 0, 2)).reshape(local_planes, rows, columns)
 
 

time: 34.3 us -> 32.3 us (0.942)
  blocking collectives: 21.5 us -> 18.8 us
  Pallas kernels: 5.86 us -> 7.23 us
  other arithmetic: 0.84 us -> 0 us
    all_to_all x2, blocking collectives: 21.5 us -> 18.8 us  [the longest x1 11.1 us: project_paired(): return lax.all_to_all(parts, 'ang', split_axis=0, concat_axis=0)]
    pallas_call x2 -> x5, Pallas kernels: 4.35 us -> 5.72 us  [the longest x1 2.46 us: combine(): pl.pallas_call(combine_kernel, out_shape=pltpu.VMEM((dests, columns // de...]
    select_n x1 -> x0, other arithmetic: 0.84 us -> none  [per_device(): outer = exchanged(jnp.where(even, first_edge, last_edge), 'gx', 1)]
  transfers between devices with their start and end apart: 2 -> 2, of which waited for: 0 -> 0; matrix products, arithmetic and copies ran while one was open for 0% -> 0% of each run, Pallas kernels for 12% -> 13%
where the time goes in v4:
time: 32.3 us; the launch traced here: 32.1 us
  blocking collectives  18.8 us (58%)
  Pallas kernels  7.23 us (22%)
  starting transfers between devices  5.3 us (16%)
  local copies, waits for them, and re-layouts  0.76 us (2%)
    all_to_all x1, blocking collectives, project_paired(): return lax.all_to_all(parts, 'ang', split_axis=0, concat_axis=0)  11.1 us
    all_to_all x1, blocking collectives, per_device(): done = lax.all_to_all(done, ('gy', 'ang'), split_axis=0, concat_axis=0)  7.71 us
    ppermute x1, starting transfers between devices, project_paired(): got_edge = lax.ppermute(edge(own, got, lines), ('gy', 'gx'), route)  4.74 us
    pallas_call x1, Pallas kernels, combine(): pl.pallas_call(combine_kernel, out_shape=pltpu.VMEM((dests, columns // de...  2.46 us
    pallas_call x1, Pallas kernels, tables(): pl.pallas_call(functools.partial(tables_kernel, columns), out_shape=[pltp...  1.83 us
    pallas_call x1, Pallas kernels, smooth(): pl.pallas_call(functools.partial(smooth_kernel, planes, columns), out_sha...  1.51 us
    pallas_call x1, Pallas kernels, pack(): pl.pallas_call(pack_kernel, out_shape=[pltpu.VMEM((rows + 2 * local_lines...  1.26 us
    reshape x1, local copies, waits for them, and re-layouts, per_device(): return jnp.transpose(done, (1, 0, 2)).reshape(local_planes, rows, columns)  0.68 us
  transfers between devices with their start and end apart: 2, of which 0 were waited for; matrix products, arithmetic and copies ran while one was open for 0% of the time, Pallas kernels for 13%

profile of v4, /device:TPU:0, one launch (start us, length us, event | category | flops | bytes accessed | tf_op | source)
XLA Modules:
  0.0 32.1 jit_solution(5904308863114390681)
XLA Ops:
  0.0 1.3 %pack.1 = (f32[320,512]{1,0:T(8,128)S(1)}, bf16[256,512]{1,0:T(8,128)(2,1)S(1)}, s32[4,128]{1,0:T(4,128)S(1)}, s32[4,128]{1,0:T(4,128)S(1)}, f32[4,512]{1,0:T(4,...) custom-call(bf16[256,512]{1,0:T(8,128)(2,1)} %bitcast.7, s32[4,128]{1,0:T(4,128)} %bitcast.10, s32[4,128]{1,0:T(4,128)} %bitcast.11, ...), custom_call_target="tpu_custom_call" | custom-call | tf_op jit(solution)/shard_map/pack/pallas_call | solution.py:358
  1.3 0.6 %collective-permute-start = (f32[320,512]{1,0:T(8,128)S(1)}, f32[320,512]{1,0:T(8,128)S(1)}, u32[]{:S(2)}, u32[]{:S(2)}) collective-permute-start(f32[320,512]{1,0:T(8,128)S(1)} %get-tuple-element.17), channel_id=1, source_target_pairs={{0,4},{4,0},{1,5},{5,1},{2,6},{6,2},{3,7},{7,3},{8,12},{12,8},{9,1... | collective-permute-start | bytes 1966088 | tf_op jit(solution)/shard_map/ppermute | solution.py:561
  1.8 1.8 %tables.1 = (bf16[1024,512]{1,0:T(8,128)(2,1)S(1)}, bf16[528,1024]{1,0:T(8,128)(2,1)S(1)}, bf16[528,1024]{1,0:T(8,128)(2,1)S(1)}) custom-call(s32[4,128]{1,0:T(4,128)S(1)} %get-tuple-element.18.offsets_ref, s32[4,128]{1,0:T(4,128)S(1)} %get-tuple-element.19.view_ref, f32[4,512]{1,0:T(4,128)S(1)} %get-tuple-element.20.taps_ref, ...), custom_call_target="tpu_custom_call" | custom-call | flops 2000000000 | bytes 1000000 | tf_op jit(solution)/shard_map/tables/pallas_call | solution.py:409
  3.7 0.0 collective-permute-done.got_ref
  3.7 0.1 edge.1
  3.8 4.7 %collective-permute-start.1 = (f32[8,256]{1,0:T(8,128)S(1)}, f32[8,256]{1,0:T(8,128)S(1)}, u32[]{:S(2)}, u32[]{:S(2)}) collective-permute-start(f32[8,256]{1,0:T(8,128)S(1)} %edge.1), channel_id=1, source_target_pairs={{4,1},{1,4},{5,2},{2,5},{6,3},{3,6},{7,0},{0,7},{12,9},{9,12},{13,... | collective-permute-start | bytes 24584 | tf_op jit(solution)/shard_map/ppermute | solution.py:569
  8.6 2.5 %combine.1.parts_ref = f32[4,136,256]{2,1,0:T(8,128)S(1)} custom-call(bf16[256,512]{1,0:T(8,128)(2,1)S(1)} %get-tuple-element.15.data_ref, f32[32,640]{1,0:T(8,128)S(1)} %get-tuple-element.16.own_ref, f32[320,512]{1,0:T(8,128)S(1)} %collective-permute-done.got_ref, bf16[1024,512]{1,0:T(8,128)(2,1)S(1)} %get-tuple-element.22.spread_ref, ...), custom_call_target="tpu_custom_call" | custom-call | flops 2000000000 | bytes 1000000 | tf_op jit(solution)/shard_map/combine/pallas_call | solution.py:513
  11.0 0.0 collective-permute-done.1.edge_ref
  11.1 11.1 %all_to_all.10.parts_ref = f32[4,136,256]{2,1,0:T(8,128)S(1)} all-to-all(f32[4,136,256]{2,1,0:T(8,128)S(1)} %join.1), channel_id=1, replica_groups=mesh['ang'=4,'gy'=2,'gx'=4] {'ang'}, dimensions={0} | all-to-all | bytes 1114112 | tf_op jit(solution)/shard_map/all_to_all | solution.py:573
  22.1 1.5 %smooth.1 = f32[8,32,128]{2,1,0:T(8,128)S(1)} custom-call(f32[4,136,256]{2,1,0:T(8,128)S(1)} %all_to_all.10.parts_ref), custom_call_target="tpu_custom_call" | custom-call | tf_op jit(solution)/shard_map/smooth/pallas_call | solution.py:299
  23.6 7.7 %all_to_all.11 = f32[8,32,128]{2,1,0:T(8,128)S(1)} all-to-all(f32[8,32,128]{2,1,0:T(8,128)S(1)} %smooth.1), channel_id=1, replica_groups=mesh['ang'=4,'gy'=2,'gx'=4] {'gy','ang'}, dimensions={0} | all-to-all | bytes 262144 | tf_op jit(solution)/shard_map/all_to_all | solution.py:606
  31.4 0.1 copy.9
  31.4 0.7 %reshape.23 = f32[4,8,1024]{2,1,0:T(8,128)} reshape(f32[32,8,128]{2,1,0:T(8,128)S(1)} %copy.9) | data formatting | bytes 262144 | tf_op jit(solution)/shard_map/reshape | solution.py:607
  (1 shorter events, 0.0 us)
Async XLA Ops:
  1.3 2.4 %collective-permute-start = (f32[320,512]{1,0:T(8,128)S(1)}, f32[320,512]{1,0:T(8,128)S(1)}, u32[]{:S(2)}, u32[]{:S(2)}) collective-permute-start(f32[320,512]{1,0:T(8,128)S(1)} %get-tuple-element.17), channel_id=1, source_target_pairs={{0,4},{4,0},{1,5},{5,1},{2,6},{6,2},{3,7},{7,3},{8,12},{12,8},{9,1... | collective-permute-start | bytes 1966088 | tf_op jit(solution)/shard_map/ppermute | solution.py:561
  3.8 7.2 %collective-permute-start.1 = (f32[8,256]{1,0:T(8,128)S(1)}, f32[8,256]{1,0:T(8,128)S(1)}, u32[]{:S(2)}, u32[]{:S(2)}) collective-permute-start(f32[8,256]{1,0:T(8,128)S(1)} %edge.1), channel_id=1, source_target_pairs={{4,1},{1,4},{5,2},{2,5},{6,3},{3,6},{7,0},{0,7},{12,9},{9,12},{13,... | collective-permute-start | bytes 24584 | tf_op jit(solution)/shard_map/ppermute | solution.py:569

commit v5 on v4

--- a/solution.py
+++ b/solution.py
@@ -210,13 +210,13 @@
     )(parts, inner, outer)
 
 
-def smooth_kernel(planes, columns, parts_ref, out_ref):
+def smooth_kernel(planes, columns, *refs):
+    *parts_refs, out_ref = refs
     dests, local_lines, block = out_ref.shape
-    window = parts_ref.shape[1]
+    window = parts_refs[0].shape[-2]
     angs, groups = lax.axis_size("ang"), lax.axis_size("gy")
     lines = angs * local_lines
     rows = lines // planes
-    joined = parts_ref.shape[0] == angs
     lane = lax.broadcasted_iota(jnp.int32, (window, lines), 1)
     lane_row = lane % rows
     place = lax.axis_index("gy") * angs + lax.axis_index("ang")
@@ -231,10 +231,10 @@
     for group in range(groups):
         total = None
         for ang in range(angs):
-            if joined:
-                part = parts_ref[ang, :, pl.ds(group * lines, lines)]
+            if len(parts_refs) > 1:
+                part = parts_refs[ang][:, pl.ds(group * lines, lines)]
             else:
-                part = parts_ref[group * angs + ang]
+                part = parts_refs[0][group * angs + ang]
             total = part if total is None else total + part
         source.append(total)
     scaled = [value / smooth_weight for value in source]
@@ -293,17 +293,17 @@
 
 
 def smooth(parts, planes, local_lines, columns):
-    window = parts.shape[1]
+    window = parts[0].shape[-2]
     dests = lax.axis_size("ang") * lax.axis_size("gy")
     vmem = pl.BlockSpec(memory_space=pltpu.VMEM)
     return pl.pallas_call(
         functools.partial(smooth_kernel, planes, columns),
         out_shape=pltpu.VMEM((dests, local_lines, window - 2 * HALO), jnp.float32),
-        in_specs=[vmem],
+        in_specs=[vmem] * len(parts),
         out_specs=vmem,
         compiler_params=pltpu.CompilerParams(vmem_limit_bytes=VMEM_LIMIT),
         name="smooth",
-    )(parts)
+    )(*parts)
 
 
 def exchanged(block, axis, shift):
@@ -385,17 +385,18 @@
 
 def tables_kernel(
     columns, offsets_ref, view_ref, taps_ref, weight_ref,
-    spread_ref, cos_ref, sin_ref,
+    spread_ref, wave_ref,
     step_cos_ref, step_sin_ref, part_cos_ref, part_sin_ref,
 ):
+    block_size = spread_ref.shape[0]
     make_spread(offsets_ref, view_ref, taps_ref, weight_ref, spread_ref)
     angles = (step_cos_ref, step_sin_ref, part_cos_ref, part_sin_ref)
     base = make_angles(lax.axis_index("gx") * 2 * columns + lax.axis_index("gy") * columns - HALO, *angles)
     for part, first, count in chunks(columns + 2 * HALO):
 
         def put(at, cosines, sines):
-            cos_ref[pl.ds(first + at, 16), :] = cosines
-            sin_ref[pl.ds(first + at, 16), :] = sines
+            wave_ref[pl.ds(first + at, 16), pl.ds(0, block_size)] = cosines
+            wave_ref[pl.ds(first + at, 16), pl.ds(block_size, block_size)] = sines
 
         make_waves(base, part, count, *angles, put)
 
@@ -410,11 +411,10 @@
         functools.partial(tables_kernel, columns),
         out_shape=[
             pltpu.VMEM((block_size, samples), jnp.bfloat16),
-            pltpu.VMEM((made, block_size), jnp.bfloat16),
-            pltpu.VMEM((made, block_size), jnp.bfloat16),
+            pltpu.VMEM((made, 2 * block_size), jnp.bfloat16),
         ],
         in_specs=[vmem] * 4,
-        out_specs=[vmem] * 3,
+        out_specs=[vmem] * 2,
         scratch_shapes=[
             pltpu.VMEM((CHUNK // 8, block_size), jnp.float32),
             pltpu.VMEM((CHUNK // 8, block_size), jnp.float32),
@@ -462,20 +462,23 @@
     )(own, got)
 
 
-def combine_kernel(
-    data_ref, own_ref, got_ref, spread_ref, cos_ref, sin_ref,
-    out_ref,
-    grid_ref, lines_ref, vm_ref,
-):
+def grid_kernel(data_ref, own_ref, got_ref, spread_ref, grid_ref, vm_ref, both_ref, lines_ref):
     rows = data_ref.shape[0]
     lines = rows // 2
+    block_size = spread_ref.shape[0]
     local_lines, columns = own_ref.shape[0], own_ref.shape[1] - 128
     gy = lax.axis_index("gy")
-    for group, data in ((gy, data_ref[...]), (1 - gy, got_ref[pl.ds(0, rows), :].astype(jnp.bfloat16))):
-        made = lax.dot_general(data, spread_ref[...], NT, preferred_element_type=jnp.float32).astype(jnp.bfloat16)
-        for component in range(2):
+    for component in range(2):
+        for group, ref in ((gy, data_ref), (1 - gy, got_ref)):
             place = pl.multiple_of((2 * component + group) * lines, 16)
-            grid_ref[pl.ds(place, lines), :] = made[component * lines : (component + 1) * lines]
+            both_ref[pl.ds(place, lines), :] = ref[pl.ds(component * lines, lines), :].astype(jnp.bfloat16)
+    for component in range(2):
+        grid_ref[pl.ds(component * block_size, block_size), :] = lax.dot_general(
+            spread_ref[...],
+            both_ref[pl.ds(2 * component * lines, 2 * lines), :],
+            NT,
+            preferred_element_type=jnp.float32,
+        ).astype(jnp.bfloat16)
 
     lines_ref[...] = jnp.zeros_like(lines_ref)
     own_place, other_place = line_places(lines, local_lines)
@@ -489,63 +492,61 @@
         inner = lines_ref[group_lines, pl.ds(columns, 128)].T[:HALO]
         vm_ref[pl.ds(0, HALO), group_lines] = jnp.where(gy == 0, 0.0, inner)
         vm_ref[pl.ds(HALO + columns, HALO), group_lines] = jnp.where(gy == 0, inner, 0.0)
-    for first in range(0, columns, 128):
-        for group in range(2):
-            vm_ref[pl.ds(HALO + first, 128), pl.ds(group * lines, lines)] = lines_ref[
-                pl.ds(group * lines, lines), pl.ds(first, 128)
-            ].T
-
-    for part, first, count in chunks(columns + 2 * HALO):
-        made = pl.ds(first, max(16, count))
-        total = lax.dot_general(
-            cos_ref[made, :], grid_ref[pl.ds(0, 2 * lines), :], NT, preferred_element_type=jnp.float32
-        ) + lax.dot_general(
-            sin_ref[made, :], grid_ref[pl.ds(2 * lines, 2 * lines), :], NT, preferred_element_type=jnp.float32
-        )
-        put_windows(out_ref, first, count, vm_ref[pl.ds(first, count), :] - total[:count] * NX ** (-0.5))
-
-
-def combine(data, own, got, spread, cosines, sines):
+        for first in range(0, columns, 128):
+            vm_ref[pl.ds(HALO + first, 128), group_lines] = lines_ref[group_lines, pl.ds(first, 128)].T
+
+
+def grid(data, own, got, spread):
     lines = data.shape[0] // 2
     columns = own.shape[1] - 128
-    dests = lax.axis_size("ang")
-    vmem = pl.BlockSpec(memory_space=pltpu.VMEM)
-    return pl.pallas_call(
-        combine_kernel,
-        out_shape=pltpu.VMEM((dests, columns // dests + 2 * HALO, 2 * lines), jnp.float32),
-        in_specs=[vmem] * 6,
-        out_specs=vmem,
-        scratch_shapes=[
-            pltpu.VMEM((4 * lines, spread.shape[0]), jnp.bfloat16),
-            pltpu.VMEM((2 * lines, columns + 128), jnp.float32),
+    vmem = pl.BlockSpec(memory_space=pltpu.VMEM)
+    return pl.pallas_call(
+        grid_kernel,
+        out_shape=[
+            pltpu.VMEM((2 * spread.shape[0], 2 * lines), jnp.bfloat16),
             pltpu.VMEM((columns + 2 * HALO, 2 * lines), jnp.float32),
         ],
-        cost_estimate=pl.CostEstimate(flops=2 * 10**9, transcendentals=0, bytes_accessed=10**6),
-        compiler_params=pltpu.CompilerParams(vmem_limit_bytes=VMEM_LIMIT),
-        name="combine",
-    )(data, own, got, spread, cosines, sines)
-
-
-def join_kernel(parts_ref, edge_ref, out_ref):
-    dests, window, _ = parts_ref.shape
-    first = lax.axis_index("gy") == 0
+        in_specs=[vmem] * 4,
+        out_specs=[vmem] * 2,
+        scratch_shapes=[
+            pltpu.VMEM((4 * lines, data.shape[1]), jnp.bfloat16),
+            pltpu.VMEM((2 * lines, columns + 128), jnp.float32),
+        ],
+        cost_estimate=pl.CostEstimate(flops=10**9, transcendentals=0, bytes_accessed=10**6),
+        compiler_params=pltpu.CompilerParams(vmem_limit_bytes=VMEM_LIMIT),
+        name="grid",
+    )(data, own, got, spread)
+
+
+def block_kernel(apart, wave_ref, grid_ref, vm_ref, edge_ref, out_ref):
+    window = out_ref.shape[0]
+    block = window - 2 * HALO
+    angs = lax.axis_size("ang")
+    dest = lax.axis_index("ang") ^ apart
+    gy = lax.axis_index("gy")
+    first = pl.multiple_of(dest * block, 16)
+    made = 16 * pl.cdiv(window, 16)
+    total = jnp.dot(wave_ref[pl.ds(first, made), :], grid_ref[...], preferred_element_type=jnp.float32)
+    out_ref[...] = vm_ref[pl.ds(first, window), :] - total[:window] * NX ** (-0.5)
     edge = edge_ref[...][:HALO]
-    out_ref[0, pl.ds(0, HALO), :] = parts_ref[0, pl.ds(0, HALO), :] + jnp.where(first, edge, 0.0)
-    last = pl.ds(window - HALO, HALO)
-    out_ref[dests - 1, last, :] = parts_ref[dests - 1, last, :] + jnp.where(first, 0.0, edge)
-
-
-def join(parts, got_edge):
-    vmem = pl.BlockSpec(memory_space=pltpu.VMEM)
-    return pl.pallas_call(
-        join_kernel,
-        out_shape=pltpu.VMEM(parts.shape, parts.dtype),
-        in_specs=[vmem] * 2,
+    opens = jnp.logical_and(dest == 0, gy == 0)
+    out_ref[pl.ds(0, HALO), :] += jnp.where(opens, edge, 0.0)
+    closes = jnp.logical_and(dest == angs - 1, gy == 1)
+    out_ref[pl.ds(window - HALO, HALO), :] += jnp.where(closes, edge, 0.0)
+
+
+def block_of(apart, wave, grid, vm, got_edge):
+    window = (vm.shape[0] - 2 * HALO) // lax.axis_size("ang") + 2 * HALO
+    vmem = pl.BlockSpec(memory_space=pltpu.VMEM)
+    return pl.pallas_call(
+        functools.partial(block_kernel, apart),
+        out_shape=pltpu.VMEM((window, vm.shape[1]), jnp.float32),
+        in_specs=[vmem] * 4,
         out_specs=vmem,
-        input_output_aliases={0: 0},
-        compiler_params=pltpu.CompilerParams(vmem_limit_bytes=VMEM_LIMIT),
-        name="join",
-    )(parts, got_edge)
+        cost_estimate=pl.CostEstimate(flops=10**9, transcendentals=0, bytes_accessed=10**6),
+        compiler_params=pltpu.CompilerParams(vmem_limit_bytes=VMEM_LIMIT),
+        name=f"block{apart}",
+    )(wave, grid, vm, got_edge)
 
 
 def on_chip(*arrays):
@@ -559,7 +560,7 @@
         data, offsets, view_index, taps, view_weight, volume, multiplier
     )
     got = lax.ppermute(sent, "gy", [(0, 1), (1, 0)])
-    spread, cosines, sines = tables(*on_chip(offsets, view_index, taps, view_weight), columns)
+    spread, wave = tables(*on_chip(offsets, view_index, taps, view_weight), columns)
     own, got = on_chip(own, got)
     count = lax.axis_size("gx")
     route = []
@@ -567,10 +568,14 @@
         pair = (count + low, (low + 1) % count)
         route += [pair, pair[::-1]]
     got_edge = lax.ppermute(edge(own, got, lines), ("gy", "gx"), route)
-    data, spread, cosines, sines = on_chip(data, spread, cosines, sines)
-    parts = combine(data, own, got, spread, cosines, sines)
-    parts = join(*on_chip(parts, got_edge))
-    return lax.all_to_all(parts, "ang", split_axis=0, concat_axis=0)
+    gridded, vm = grid(*on_chip(data, own, got, spread))
+    wave, gridded, vm, got_edge = on_chip(wave, gridded, vm, got_edge)
+    angs = lax.axis_size("ang")
+    parts = []
+    for apart in range(angs - 1, 0, -1):
+        part = block_of(apart, wave, gridded, vm, got_edge)
+        parts.append(lax.ppermute(part, "ang", [(ang, ang ^ apart) for ang in range(angs)]))
+    return [block_of(0, wave, gridded, vm, got_edge)] + parts
 
 
 def per_device(spectrum_data, offsets, view_index, kernel, view_weight, volume, multiplier):
@@ -592,7 +597,8 @@
         volume,
         multiplier,
     )
-    if lax.axis_size("gy") == 2 and columns // 2 == samples:
+    angs = lax.axis_size("ang")
+    if lax.axis_size("gy") == 2 and columns // 2 == samples and angs & (angs - 1) == 0:
         parts = project_paired(*arrays)
     else:
         first_edge = volume[:, :HALO] + multiplier[:, :HALO]
@@ -601,8 +607,8 @@
         inner = exchanged(jnp.where(even, last_edge, first_edge), "gx", 0)
         outer = exchanged(jnp.where(even, first_edge, last_edge), "gx", 1)
         parts = close(project(*arrays, dests), *on_chip(inner, outer))
-        parts = lax.all_to_all(parts, ("gy", "ang"), split_axis=0, concat_axis=0)
-    done = smooth(*on_chip(parts), planes, local_lines, columns)
+        parts = [lax.all_to_all(parts, ("gy", "ang"), split_axis=0, concat_axis=0)]
+    done = smooth(on_chip(*parts), planes, local_lines, columns)
     done = lax.all_to_all(done, ("gy", "ang"), split_axis=0, concat_axis=0)
     return jnp.transpose(done, (1, 0, 2)).reshape(local_planes, rows, columns)
 

time: 32.3 us -> 29.5 us (0.913)
  blocking collectives: 18.8 us -> 7.91 us
  waiting for transfers between devices: 0.01 us -> 4.81 us
  starting transfers between devices: 5.3 us -> 8.98 us
  Pallas kernels: 7.23 us -> 6.86 us
    all_to_all x1 -> x0, blocking collectives: 11.1 us -> none  [project_paired(): return lax.all_to_all(parts, 'ang', split_axis=0, concat_axis=0)]
    ppermute x0 -> x3, waiting for transfers between devices: none -> 4.22 us  [project_paired(): lax.ppermute(part, 'ang', [(ang, ang ^ apart) for ang in range(angs)])]
    ppermute x0 -> x3, starting transfers between devices: none -> 3.68 us  [project_paired(): lax.ppermute(part, 'ang', [(ang, ang ^ apart) for ang in range(angs)])]
    ppermute x1, waiting for transfers between devices: 0.01 us -> 0.59 us  [project_paired(): got_edge = lax.ppermute(edge(own, got, lines), ('gy', 'gx'), route)]
    pallas_call x2 -> x5, Pallas kernels: 2.49 us -> 2.11 us  [the longest x4 1.33 us: block_of(): pl.pallas_call(functools.partial(block_kernel, apart), out_shape=pltpu.VM...]
  transfers between devices with their start and end apart: 2 -> 5, of which waited for: 0 -> 4; matrix products, arithmetic and copies ran while one was open for 0% -> 0% of each run, Pallas kernels for 13% -> 12%
where the time goes in v5:
time: 29.5 us; the launch traced here: 29.4 us
  starting transfers between devices  8.98 us (30%)
  blocking collectives  7.91 us (27%)
  Pallas kernels  6.86 us (23%)
  waiting for transfers between devices  4.81 us (16%)
  local copies, waits for them, and re-layouts  0.76 us (3%)
    all_to_all x1, blocking collectives, per_device(): done = lax.all_to_all(done, ('gy', 'ang'), split_axis=0, concat_axis=0)  7.91 us
    ppermute x1, starting transfers between devices, project_paired(): got_edge = lax.ppermute(edge(own, got, lines), ('gy', 'gx'), route)  4.74 us
    ppermute x3, waiting for transfers between devices, project_paired(): lax.ppermute(part, 'ang', [(ang, ang ^ apart) for ang in range(angs)])  4.22 us
    ppermute x3, starting transfers between devices, project_paired(): lax.ppermute(part, 'ang', [(ang, ang ^ apart) for ang in range(angs)])  3.68 us
    pallas_call x1, Pallas kernels, tables(): pl.pallas_call(functools.partial(tables_kernel, columns), out_shape=[pltp...  1.83 us
    pallas_call x1, Pallas kernels, smooth(): pl.pallas_call(functools.partial(smooth_kernel, planes, columns), out_sha...  1.52 us
    pallas_call x4, Pallas kernels, block_of(): pl.pallas_call(functools.partial(block_kernel, apart), out_shape=pltpu.VM...  1.33 us
    pallas_call x1, Pallas kernels, pack(): pl.pallas_call(pack_kernel, out_shape=[pltpu.VMEM((rows + 2 * local_lines...  1.26 us
  transfers between devices with their start and end apart: 5, of which 4 were waited for; matrix products, arithmetic and copies ran while one was open for 0% of the time, Pallas kernels for 12%

profile of v5, /device:TPU:0, one launch (start us, length us, event | category | flops | bytes accessed | tf_op | source)
XLA Modules:
  0.0 29.4 jit_solution(8397657997963780446)
XLA Ops:
  0.0 1.3 %pack.1 = (f32[320,512]{1,0:T(8,128)S(1)}, bf16[256,512]{1,0:T(8,128)(2,1)S(1)}, s32[4,128]{1,0:T(4,128)S(1)}, s32[4,128]{1,0:T(4,128)S(1)}, f32[4,512]{1,0:T(4,...) custom-call(bf16[256,512]{1,0:T(8,128)(2,1)} %bitcast.7, s32[4,128]{1,0:T(4,128)} %bitcast.10, s32[4,128]{1,0:T(4,128)} %bitcast.11, ...), custom_call_target="tpu_custom_call" | custom-call | tf_op jit(solution)/shard_map/pack/pallas_call | solution.py:358
  1.3 0.6 %collective-permute-start = (f32[320,512]{1,0:T(8,128)S(1)}, f32[320,512]{1,0:T(8,128)S(1)}, u32[]{:S(2)}, u32[]{:S(2)}) collective-permute-start(f32[320,512]{1,0:T(8,128)S(1)} %get-tuple-element.23), channel_id=1, source_target_pairs={{0,4},{4,0},{1,5},{5,1},{2,6},{6,2},{3,7},{7,3},{8,12},{12,8},{9,1... | collective-permute-start | bytes 1966088 | tf_op jit(solution)/shard_map/ppermute | solution.py:562
  1.8 1.8 %tables.1 = (bf16[1024,512]{1,0:T(8,128)(2,1)S(1)}, bf16[528,2048]{1,0:T(8,128)(2,1)S(1)}) custom-call(s32[4,128]{1,0:T(4,128)S(1)} %get-tuple-element.16.offsets_ref, s32[4,128]{1,0:T(4,128)S(1)} %get-tuple-element.17.view_ref, f32[4,512]{1,0:T(4,128)S(1)} %get-tuple-element.18.taps_ref, f32[1500]{0:T(1024)S(1)} %get-tuple-element.19.weight_ref), custom_call_target="tpu_custom_call" | custom-call | flops 2000000000 | bytes 1000000 | tf_op jit(solution)/shard_map/tables/pallas_call | solution.py:410
  3.7 0.0 collective-permute-done.got_ref
  3.7 0.1 edge.1
  3.8 4.7 %collective-permute-start.1 = (f32[8,256]{1,0:T(8,128)S(1)}, f32[8,256]{1,0:T(8,128)S(1)}, u32[]{:S(2)}, u32[]{:S(2)}) collective-permute-start(f32[8,256]{1,0:T(8,128)S(1)} %edge.1), channel_id=1, source_target_pairs={{4,1},{1,4},{5,2},{2,5},{6,3},{3,6},{7,0},{0,7},{12,9},{9,12},{13,... | collective-permute-start | bytes 24584 | tf_op jit(solution)/shard_map/ppermute | solution.py:570
  8.6 0.8 %grid.1 = (bf16[2048,256]{1,0:T(8,128)(2,1)S(1)}, f32[520,256]{1,0:T(8,128)S(1)}) custom-call(bf16[256,512]{1,0:T(8,128)(2,1)S(1)} %get-tuple-element.21.data_ref, f32[32,640]{1,0:T(8,128)S(1)} %get-tuple-element.22.own_ref, f32[320,512]{1,0:T(8,128)S(1)} %collective-permute-done.got_ref, bf16[1024,512]{1,0:T(8,128)(2,1)S(1)} %get-tuple-element.24.spread_ref), custom_call_target="tpu_custom_call" | custom-call | flops 1000000000 | bytes 1000000 | tf_op jit(solution)/shard_map/grid/pallas_call | solution.py:503
  9.3 0.6 %collective-permute-done.1.edge_ref = f32[8,256]{1,0:T(8,128)S(1)} collective-permute-done((f32[8,256]{1,0:T(8,128)S(1)}, f32[8,256]{1,0:T(8,128)S(1)}, u32[]{:S(2)}, u32[]{:S(2)}) %collective-permute-start.1) | collective-permute-done | bytes 8224 | tf_op jit(solution)/shard_map/ppermute | solution.py:570
  9.9 0.3 %block3.1 = f32[136,256]{1,0:T(8,128)S(1)} custom-call(bf16[528,2048]{1,0:T(8,128)(2,1)S(1)} %get-tuple-element.20.wave_ref, bf16[2048,256]{1,0:T(8,128)(2,1)S(1)} %get-tuple-element.25.grid_ref, f32[520,256]{1,0:T(8,128)S(1)} %get-tuple-element.26.vm_ref, f32[8,256]{1,0:T(8,128)S(1)} %collective-permute-done.1.edge_ref), custom_call_target="tpu_custom_call" | custom-call | flops 1000000000 | bytes 1000000 | tf_op jit(solution)/shard_map/block3/pallas_call | solution.py:541
  10.3 2.5 %collective-permute-start.2 = (f32[136,256]{1,0:T(8,128)S(1)}, f32[136,256]{1,0:T(8,128)S(1)}, u32[]{:S(2)}, u32[]{:S(2)}) collective-permute-start(f32[136,256]{1,0:T(8,128)S(1)} %block3.1), channel_id=1, source_target_pairs={{0,24},{8,16},{16,8},{24,0},{1,25},{9,17},{17,9},{25,1},{2,26},{10... | collective-permute-start | bytes 417800 | tf_op jit(solution)/shard_map/ppermute | solution.py:577
  12.8 0.3 %block2.1 = f32[136,256]{1,0:T(8,128)S(1)} custom-call(bf16[528,2048]{1,0:T(8,128)(2,1)S(1)} %get-tuple-element.20.wave_ref, bf16[2048,256]{1,0:T(8,128)(2,1)S(1)} %get-tuple-element.25.grid_ref, f32[520,256]{1,0:T(8,128)S(1)} %get-tuple-element.26.vm_ref, f32[8,256]{1,0:T(8,128)S(1)} %collective-permute-done.1.edge_ref), custom_call_target="tpu_custom_call" | custom-call | flops 1000000000 | bytes 1000000 | tf_op jit(solution)/shard_map/block2/pallas_call | solution.py:541
  13.1 0.6 %collective-permute-start.3 = (f32[136,256]{1,0:T(8,128)S(1)}, f32[136,256]{1,0:T(8,128)S(1)}, u32[]{:S(2)}, u32[]{:S(2)}) collective-permute-start(f32[136,256]{1,0:T(8,128)S(1)} %block2.1), channel_id=1, source_target_pairs={{0,16},{8,24},{16,0},{24,8},{1,17},{9,25},{17,1},{25,9},{2,18},{10... | collective-permute-start | bytes 417800 | tf_op jit(solution)/shard_map/ppermute | solution.py:577
  13.7 0.3 %block1.1 = f32[136,256]{1,0:T(8,128)S(1)} custom-call(bf16[528,2048]{1,0:T(8,128)(2,1)S(1)} %get-tuple-element.20.wave_ref, bf16[2048,256]{1,0:T(8,128)(2,1)S(1)} %get-tuple-element.25.grid_ref, f32[520,256]{1,0:T(8,128)S(1)} %get-tuple-element.26.vm_ref, f32[8,256]{1,0:T(8,128)S(1)} %collective-permute-done.1.edge_ref), custom_call_target="tpu_custom_call" | custom-call | flops 1000000000 | bytes 1000000 | tf_op jit(solution)/shard_map/block1/pallas_call | solution.py:541
  14.1 0.6 %collective-permute-start.4 = (f32[136,256]{1,0:T(8,128)S(1)}, f32[136,256]{1,0:T(8,128)S(1)}, u32[]{:S(2)}, u32[]{:S(2)}) collective-permute-start(f32[136,256]{1,0:T(8,128)S(1)} %block1.1), channel_id=1, source_target_pairs={{0,8},{8,0},{16,24},{24,16},{1,9},{9,1},{17,25},{25,17},{2,10},{10... | collective-permute-start | bytes 417800 | tf_op jit(solution)/shard_map/ppermute | solution.py:577
  14.6 0.3 %block0.1.refs_0_ = f32[136,256]{1,0:T(8,128)S(1)} custom-call(bf16[528,2048]{1,0:T(8,128)(2,1)S(1)} %get-tuple-element.20.wave_ref, bf16[2048,256]{1,0:T(8,128)(2,1)S(1)} %get-tuple-element.25.grid_ref, f32[520,256]{1,0:T(8,128)S(1)} %get-tuple-element.26.vm_ref, f32[8,256]{1,0:T(8,128)S(1)} %collective-permute-done.1.edge_ref), custom_call_target="tpu_custom_call" | custom-call | flops 1000000000 | bytes 1000000 | tf_op jit(solution)/shard_map/block0/pallas_call | solution.py:541
  15.0 2.0 %collective-permute-done.2.refs_1_ = f32[136,256]{1,0:T(8,128)S(1)} collective-permute-done((f32[136,256]{1,0:T(8,128)S(1)}, f32[136,256]{1,0:T(8,128)S(1)}, u32[]{:S(2)}, u32[]{:S(2)}) %collective-permute-start.2) | collective-permute-done | bytes 139296 | tf_op jit(solution)/shard_map/ppermute | solution.py:577
  17.0 1.5 %collective-permute-done.3.refs_2_ = f32[136,256]{1,0:T(8,128)S(1)} collective-permute-done((f32[136,256]{1,0:T(8,128)S(1)}, f32[136,256]{1,0:T(8,128)S(1)}, u32[]{:S(2)}, u32[]{:S(2)}) %collective-permute-start.3) | collective-permute-done | bytes 139296 | tf_op jit(solution)/shard_map/ppermute | solution.py:577
  18.5 0.7 %collective-permute-done.4.refs_3_ = f32[136,256]{1,0:T(8,128)S(1)} collective-permute-done((f32[136,256]{1,0:T(8,128)S(1)}, f32[136,256]{1,0:T(8,128)S(1)}, u32[]{:S(2)}, u32[]{:S(2)}) %collective-permute-start.4) | collective-permute-done | bytes 139296 | tf_op jit(solution)/shard_map/ppermute | solution.py:577
  19.2 1.5 %smooth.1 = f32[8,32,128]{2,1,0:T(8,128)S(1)} custom-call(f32[136,256]{1,0:T(8,128)S(1)} %block0.1.refs_0_, f32[136,256]{1,0:T(8,128)S(1)} %collective-permute-done.2.refs_1_, f32[136,256]{1,0:T(8,128)S(1)} %collective-permute-done.3.refs_2_, f32[136,256]{1,0:T(8,128)S(1)} %collective-permute-done.4.refs_3_), custom_call_target="tpu_custom_call" | custom-call | tf_op jit(solution)/shard_map/smooth/pallas_call | solution.py:299
  20.7 7.9 %all_to_all.5 = f32[8,32,128]{2,1,0:T(8,128)S(1)} all-to-all(f32[8,32,128]{2,1,0:T(8,128)S(1)} %smooth.1), channel_id=1, replica_groups=mesh['ang'=4,'gy'=2,'gx'=4] {'gy','ang'}, dimensions={0} | all-to-all | bytes 262144 | tf_op jit(solution)/shard_map/all_to_all | solution.py:612
  28.6 0.1 copy.8
  28.7 0.7 %reshape.23 = f32[4,8,1024]{2,1,0:T(8,128)} reshape(f32[32,8,128]{2,1,0:T(8,128)S(1)} %copy.8) | data formatting | bytes 262144 | tf_op jit(solution)/shard_map/reshape | solution.py:613
Async XLA Ops:
  1.3 2.4 %collective-permute-start = (f32[320,512]{1,0:T(8,128)S(1)}, f32[320,512]{1,0:T(8,128)S(1)}, u32[]{:S(2)}, u32[]{:S(2)}) collective-permute-start(f32[320,512]{1,0:T(8,128)S(1)} %get-tuple-element.23), channel_id=1, source_target_pairs={{0,4},{4,0},{1,5},{5,1},{2,6},{6,2},{3,7},{7,3},{8,12},{12,8},{9,1... | collective-permute-start | bytes 1966088 | tf_op jit(solution)/shard_map/ppermute | solution.py:562
  3.8 6.1 %collective-permute-start.1 = (f32[8,256]{1,0:T(8,128)S(1)}, f32[8,256]{1,0:T(8,128)S(1)}, u32[]{:S(2)}, u32[]{:S(2)}) collective-permute-start(f32[8,256]{1,0:T(8,128)S(1)} %edge.1), channel_id=1, source_target_pairs={{4,1},{1,4},{5,2},{2,5},{6,3},{3,6},{7,0},{0,7},{12,9},{9,12},{13,... | collective-permute-start | bytes 24584 | tf_op jit(solution)/shard_map/ppermute | solution.py:570
  10.3 6.7 %collective-permute-start.2 = (f32[136,256]{1,0:T(8,128)S(1)}, f32[136,256]{1,0:T(8,128)S(1)}, u32[]{:S(2)}, u32[]{:S(2)}) collective-permute-start(f32[136,256]{1,0:T(8,128)S(1)} %block3.1), channel_id=1, source_target_pairs={{0,24},{8,16},{16,8},{24,0},{1,25},{9,17},{17,9},{25,1},{2,26},{10... | collective-permute-start | bytes 417800 | tf_op jit(solution)/shard_map/ppermute | solution.py:577
  13.1 5.3 %collective-permute-start.3 = (f32[136,256]{1,0:T(8,128)S(1)}, f32[136,256]{1,0:T(8,128)S(1)}, u32[]{:S(2)}, u32[]{:S(2)}) collective-permute-start(f32[136,256]{1,0:T(8,128)S(1)} %block2.1), channel_id=1, source_target_pairs={{0,16},{8,24},{16,0},{24,8},{1,17},{9,25},{17,1},{25,9},{2,18},{10... | collective-permute-start | bytes 417800 | tf_op jit(solution)/shard_map/ppermute | solution.py:577
  14.1 5.1 %collective-permute-start.4 = (f32[136,256]{1,0:T(8,128)S(1)}, f32[136,256]{1,0:T(8,128)S(1)}, u32[]{:S(2)}, u32[]{:S(2)}) collective-permute-start(f32[136,256]{1,0:T(8,128)S(1)} %block1.1), channel_id=1, source_target_pairs={{0,8},{8,0},{16,24},{24,16},{1,9},{9,1},{17,25},{25,17},{2,10},{10... | collective-permute-start | bytes 417800 | tf_op jit(solution)/shard_map/ppermute | solution.py:577

commit v6 on v5

--- a/solution.py
+++ b/solution.py
@@ -7,6 +7,7 @@
 from jax.experimental import pallas as pl
 from jax.experimental.pallas import tpu as pltpu
 from jax.sharding import PartitionSpec as P
+
 
 NX = 4096
 TV_STEPS = 4
@@ -55,13 +56,13 @@
 
     rows = 16
     cell = lax.broadcasted_iota(jnp.int32, (rows, samples), 0)
-    start = jnp.broadcast_to(offsets, (rows, samples))
+    starts = [jnp.broadcast_to(offsets + index, (rows, samples)) for index in range(len(values))]
     values = [jnp.broadcast_to(value, (rows, samples)) for value in values]
     for first in range(0, block_size, rows):
-        tap = cell - (start - first)
+        here = cell + first
         spread = jnp.zeros((rows, samples), jnp.float32)
-        for index, value in enumerate(values):
-            spread = jnp.where(tap == index, value, spread)
+        for start, value in zip(starts, values):
+            spread = jnp.where(here == start, value, spread)
         spread_ref[pl.ds(first, rows), :] = spread.astype(jnp.bfloat16)
 
 
@@ -70,12 +71,12 @@
     freq = lax.axis_index("ang") * block_size + lax.broadcasted_iota(jnp.int32, (8, block_size), 1)
     row = lax.broadcasted_iota(jnp.int32, (8, block_size), 0)
     for first in range(0, CHUNK // 8, 8):
-        step_cos_ref[pl.ds(first, 8), :], step_sin_ref[pl.ds(first, 8), :] = unit_circle(freq * (8 * (row + first)))
+        step_cos_ref[pl.ds(first, 8), :], step_sin_ref[pl.ds(first, 8), :] = unit_circle(-freq * (8 * (row + first)))
     for first in range(0, part_cos_ref.shape[0], 8):
         part_cos_ref[pl.ds(first, 8), :], part_sin_ref[pl.ds(first, 8), :] = unit_circle(
-            freq * (CHUNK * (row + first))
+            -freq * (CHUNK * (row + first))
         )
-    return unit_circle(freq * (first_column + row))
+    return unit_circle(-freq * (first_column + row))
 
 
 def make_waves(base, part, count, step_cos_ref, step_sin_ref, part_cos_ref, part_sin_ref, put):
@@ -88,7 +89,7 @@
         for one in (step, step + 1):
             step_cos, step_sin = step_cos_ref[pl.ds(one, 1), :], step_sin_ref[pl.ds(one, 1), :]
             pair_cos.append(here_cos * step_cos - here_sin * step_sin)
-            pair_sin.append(-(here_sin * step_cos + here_cos * step_sin))
+            pair_sin.append(here_sin * step_cos + here_cos * step_sin)
         put(
             8 * step,
             jnp.concatenate(pair_cos, axis=0).astype(jnp.bfloat16),
@@ -183,7 +184,7 @@
 def close_kernel(parts_ref, inner_ref, outer_ref, out_ref, halo_ref):
     ang = lax.axis_index("ang")
     even = lax.axis_index("gx") % 2 == 0
-    dests, window, lines = parts_ref.shape
+    dests, window, _ = parts_ref.shape
     local_lines = inner_ref.shape[0]
     halo_ref[...] = jnp.zeros_like(halo_ref)
     own = pl.ds(pl.multiple_of(ang * local_lines, 8), local_lines)
@@ -212,7 +213,7 @@
 
 def smooth_kernel(planes, columns, *refs):
     *parts_refs, out_ref = refs
-    dests, local_lines, block = out_ref.shape
+    _, local_lines, block = out_ref.shape
     window = parts_refs[0].shape[-2]
     angs, groups = lax.axis_size("ang"), lax.axis_size("gy")
     lines = angs * local_lines
@@ -237,7 +238,7 @@
                 part = parts_refs[0][group * angs + ang]
             total = part if total is None else total + part
         source.append(total)
-    scaled = [value / smooth_weight for value in source]
+    scaled = [value * (dual_step / smooth_weight) for value in source]
 
     def down(values):
         lower = []
@@ -270,7 +271,7 @@
                     for ang in range(angs):
                         out_ref[group * angs + ang] = turned[ang * local_lines : (ang + 1) * local_lines]
                 return
-            target = [local_div[group] - scaled[group] for group in range(groups)]
+            target = [dual_step * local_div[group] - scaled[group] for group in range(groups)]
         updated = []
         for group in range(groups):
             here = target[group]
@@ -283,9 +284,9 @@
             else:
                 slope_row = jnp.where(row_last, zero, pltpu.roll(here, lines - 1, 1) - here)
             slope_cell = jnp.where(cell_open, pltpu.roll(here, window - 1, 0) - here, zero)
-            slope_norm = jnp.sqrt(slope_plane * slope_plane + slope_row * slope_row + slope_cell * slope_cell)
-            scale = 1.0 / (1.0 + dual_step * slope_norm)
-            moved = [dual_step * slope_plane, dual_step * slope_row, dual_step * slope_cell]
+            square = slope_plane * slope_plane + slope_row * slope_row + slope_cell * slope_cell
+            scale = 1.0 / (1.0 + square * lax.rsqrt(jnp.maximum(square, 1e-30)))
+            moved = [slope_plane, slope_row, slope_cell]
             if flow is not None:
                 moved = [f + m for f, m in zip(flow[group], moved)]
             updated.append([m * scale for m in moved])
@@ -315,18 +316,29 @@
     return lax.ppermute(block, axis, route)
 
 
+def line_places(lines, local_lines):
+    gy, inner = lax.axis_index("gy"), lax.axis_index("ang") * local_lines
+    return [
+        pl.ds(pl.multiple_of(group * lines + inner, 8), local_lines) for group in (gy, 1 - gy)
+    ]
+
+
 def pack_kernel(
     data_ref, offsets_ref, view_ref, taps_ref, weight_ref, volume_ref, multiplier_ref,
-    sent_ref, data_out, offsets_out, view_out, taps_out, weight_out, own_ref,
-    volume_here, multiplier_here, sems,
+    sent_ref, data_out, offsets_out, view_out, taps_out, weight_out, own_ref, wave_ref, edge_ref, edge_sent_ref,
+    volume_here, multiplier_here, step_cos_ref, step_sin_ref, part_cos_ref, part_sin_ref, lines_ref, sems,
 ):
     rows = data_ref.shape[0]
-    half = volume_ref.shape[1] // 2
-    first = lax.axis_index("gy") == 0
+    lines = rows // 2
+    local_lines, columns = volume_ref.shape
+    half = columns // 2
+    block_size = wave_ref.shape[1] // 2
+    gx, gy = lax.axis_index("gx"), lax.axis_index("gy")
+    first_core = gy == 0
     pairs = (
-        (data_ref, data_out),
         (volume_ref, volume_here),
         (multiplier_ref, multiplier_here),
+        (data_ref, data_out),
         (offsets_ref, offsets_out),
         (view_ref, view_out),
         (taps_ref, taps_out),
@@ -335,18 +347,39 @@
     copies = [pltpu.make_async_copy(source, target, sems.at[at]) for at, (source, target) in enumerate(pairs)]
     for copy in copies:
         copy.start()
+
+    lines_ref[...] = jnp.zeros_like(lines_ref)
+    angles = (step_cos_ref, step_sin_ref, part_cos_ref, part_sin_ref)
+    base = make_angles(gx * columns + gy * half - HALO, *angles)
+    for part, first, count in chunks(half + 2 * HALO):
+
+        def put(at, cosines, sines):
+            wave_ref[pl.ds(first + at, 16), pl.ds(0, block_size)] = cosines
+            wave_ref[pl.ds(first + at, 16), pl.ds(block_size, block_size)] = sines
+
+        make_waves(base, part, count, *angles, put)
+
     copies[0].wait()
-    sent_ref[pl.ds(0, rows), :] = data_out[...].astype(jnp.float32)
     copies[1].wait()
-    copies[2].wait()
     low = volume_here[:, pl.ds(0, half)] + multiplier_here[:, pl.ds(0, half)]
     high = volume_here[:, pl.ds(half, half)] + multiplier_here[:, pl.ds(half, half)]
+    outer = (low[:, :HALO], high[:, half - HALO :])
+    place = line_places(lines, local_lines)[0]
+    lines_ref[place, pl.ds(0, HALO)] = jnp.where(first_core, outer[0], outer[1])
+    lines_ref[place, pl.ds(8, HALO)] = jnp.where(first_core, outer[1], outer[0])
+    for group in range(2):
+        group_lines = pl.ds(group * lines, lines)
+        turned = lines_ref[group_lines, :].T
+        edge_ref[:, group_lines] = turned[:8]
+        edge_sent_ref[:, group_lines] = turned[8:16]
+
     below, above = low[:, half - HALO :], high[:, :HALO]
-    local_lines = low.shape[0]
-    own_ref[:, pl.ds(0, half)] = jnp.where(first, low, high)
-    own_ref[:, pl.ds(half, HALO)] = jnp.where(first, above, below)
-    sent_ref[pl.ds(rows, local_lines), :] = jnp.where(first, high, low)
-    sent_ref[pl.ds(rows + local_lines, local_lines), pl.ds(0, HALO)] = jnp.where(first, below, above)
+    own_ref[:, pl.ds(0, half)] = jnp.where(first_core, low, high)
+    own_ref[:, pl.ds(half, HALO)] = jnp.where(first_core, above, below)
+    sent_ref[pl.ds(rows, local_lines), :] = jnp.where(first_core, high, low)
+    sent_ref[pl.ds(rows + local_lines, local_lines), pl.ds(0, HALO)] = jnp.where(first_core, below, above)
+    copies[2].wait()
+    sent_ref[pl.ds(0, rows), :] = data_out[...].astype(jnp.float32)
     for copy in copies[3:]:
         copy.wait()
 
@@ -354,6 +387,9 @@
 def pack(data, offsets, view_index, taps, view_weight, volume, multiplier):
     rows, samples = data.shape
     local_lines, columns = volume.shape
+    block_size = NX // lax.axis_size("ang")
+    made = 16 * pl.cdiv(columns // 2 + 2 * HALO, 16)
+    parts = 8 * pl.cdiv(pl.cdiv(columns // 2 + 2 * HALO, CHUNK), 8)
     vmem = pl.BlockSpec(memory_space=pltpu.VMEM)
     return pl.pallas_call(
         pack_kernel,
@@ -365,12 +401,20 @@
             pltpu.VMEM(taps.shape, taps.dtype),
             pltpu.VMEM(view_weight.shape, view_weight.dtype),
             pltpu.VMEM((local_lines, columns // 2 + 128), jnp.float32),
+            pltpu.VMEM((made, 2 * block_size), jnp.bfloat16),
+            pltpu.VMEM((8, rows), jnp.float32),
+            pltpu.VMEM((8, rows), jnp.float32),
         ],
         in_specs=[pl.BlockSpec(memory_space=pltpu.HBM)] * 7,
-        out_specs=[vmem] * 7,
+        out_specs=[vmem] * 10,
         scratch_shapes=[
             pltpu.VMEM(volume.shape, volume.dtype),
             pltpu.VMEM(multiplier.shape, multiplier.dtype),
+            pltpu.VMEM((CHUNK // 8, block_size), jnp.float32),
+            pltpu.VMEM((CHUNK // 8, block_size), jnp.float32),
+            pltpu.VMEM((parts, block_size), jnp.float32),
+            pltpu.VMEM((parts, block_size), jnp.float32),
+            pltpu.VMEM((rows, 128), jnp.float32),
             pltpu.SemaphoreType.DMA((7,)),
         ],
         compiler_params=pltpu.CompilerParams(vmem_limit_bytes=VMEM_LIMIT),
@@ -383,83 +427,18 @@
     )
 
 
-def tables_kernel(
-    columns, offsets_ref, view_ref, taps_ref, weight_ref,
-    spread_ref, wave_ref,
-    step_cos_ref, step_sin_ref, part_cos_ref, part_sin_ref,
-):
-    block_size = spread_ref.shape[0]
-    make_spread(offsets_ref, view_ref, taps_ref, weight_ref, spread_ref)
-    angles = (step_cos_ref, step_sin_ref, part_cos_ref, part_sin_ref)
-    base = make_angles(lax.axis_index("gx") * 2 * columns + lax.axis_index("gy") * columns - HALO, *angles)
-    for part, first, count in chunks(columns + 2 * HALO):
-
-        def put(at, cosines, sines):
-            wave_ref[pl.ds(first + at, 16), pl.ds(0, block_size)] = cosines
-            wave_ref[pl.ds(first + at, 16), pl.ds(block_size, block_size)] = sines
-
-        make_waves(base, part, count, *angles, put)
-
-
-def tables(offsets, view_index, taps, view_weight, columns):
-    samples = taps.shape[1]
+def spread_of(offsets, view_index, taps, view_weight):
     block_size = NX // lax.axis_size("ang")
-    made = 16 * pl.cdiv(columns + 2 * HALO, 16)
-    parts = 8 * pl.cdiv(pl.cdiv(columns + 2 * HALO, CHUNK), 8)
     vmem = pl.BlockSpec(memory_space=pltpu.VMEM)
     return pl.pallas_call(
-        functools.partial(tables_kernel, columns),
-        out_shape=[
-            pltpu.VMEM((block_size, samples), jnp.bfloat16),
-            pltpu.VMEM((made, 2 * block_size), jnp.bfloat16),
-        ],
+        make_spread,
+        out_shape=pltpu.VMEM((block_size, taps.shape[1]), jnp.bfloat16),
         in_specs=[vmem] * 4,
-        out_specs=[vmem] * 2,
-        scratch_shapes=[
-            pltpu.VMEM((CHUNK // 8, block_size), jnp.float32),
-            pltpu.VMEM((CHUNK // 8, block_size), jnp.float32),
-            pltpu.VMEM((parts, block_size), jnp.float32),
-            pltpu.VMEM((parts, block_size), jnp.float32),
-        ],
+        out_specs=vmem,
         cost_estimate=pl.CostEstimate(flops=2 * 10**9, transcendentals=0, bytes_accessed=10**6),
         compiler_params=pltpu.CompilerParams(vmem_limit_bytes=VMEM_LIMIT),
-        name="tables",
+        name="spread",
     )(offsets, view_index, taps, view_weight)
-
-
-def line_places(lines, local_lines):
-    gy, inner = lax.axis_index("gy"), lax.axis_index("ang") * local_lines
-    return [
-        pl.ds(pl.multiple_of(group * lines + inner, 8), local_lines) for group in (gy, 1 - gy)
-    ]
-
-
-def edge_kernel(lines, own_ref, got_ref, out_ref, lines_ref):
-    local_lines, half = own_ref.shape[0], own_ref.shape[1] - 128
-    rows = got_ref.shape[0] - 2 * local_lines
-    first = lax.axis_index("gy") == 0
-    lines_ref[...] = jnp.zeros_like(lines_ref)
-    own_place, other_place = line_places(lines, local_lines)
-    other = pl.ds(rows, local_lines)
-    for place, ref, at in ((own_place, own_ref, pl.ds(0, local_lines)), (other_place, got_ref, other)):
-        lines_ref[place, pl.ds(0, HALO)] = jnp.where(
-            first, ref[at, pl.ds(0, HALO)], ref[at, pl.ds(half - HALO, HALO)]
-        )
-    for group in range(2):
-        out_ref[:, pl.ds(group * lines, lines)] = lines_ref[pl.ds(group * lines, lines), :].T[:8]
-
-
-def edge(own, got, lines):
-    vmem = pl.BlockSpec(memory_space=pltpu.VMEM)
-    return pl.pallas_call(
-        functools.partial(edge_kernel, lines),
-        out_shape=pltpu.VMEM((8, 2 * lines), jnp.float32),
-        in_specs=[vmem] * 2,
-        out_specs=vmem,
-        scratch_shapes=[pltpu.VMEM((2 * lines, 128), jnp.float32)],
-        compiler_params=pltpu.CompilerParams(vmem_limit_bytes=VMEM_LIMIT),
-        name="edge",
-    )(own, got)
 
 
 def grid_kernel(data_ref, own_ref, got_ref, spread_ref, grid_ref, vm_ref, both_ref, lines_ref):
@@ -545,7 +524,6 @@
         out_specs=vmem,
         cost_estimate=pl.CostEstimate(flops=10**9, transcendentals=0, bytes_accessed=10**6),
         compiler_params=pltpu.CompilerParams(vmem_limit_bytes=VMEM_LIMIT),
-        name=f"block{apart}",
     )(wave, grid, vm, got_edge)
 
 
@@ -554,20 +532,18 @@
 
 
 def project_paired(data, offsets, view_index, taps, view_weight, volume, multiplier):
-    lines = data.shape[0] // 2
-    columns = volume.shape[1] // 2
-    sent, data, offsets, view_index, taps, view_weight, own = pack(
+    sent, data, offsets, view_index, taps, view_weight, own, wave, near, near_sent = pack(
         data, offsets, view_index, taps, view_weight, volume, multiplier
     )
+    near_got = lax.ppermute(near_sent, "gy", [(0, 1), (1, 0)])
     got = lax.ppermute(sent, "gy", [(0, 1), (1, 0)])
-    spread, wave = tables(*on_chip(offsets, view_index, taps, view_weight), columns)
-    own, got = on_chip(own, got)
+    spread = spread_of(*on_chip(offsets, view_index, taps, view_weight))
     count = lax.axis_size("gx")
     route = []
     for low in range(count):
         pair = (count + low, (low + 1) % count)
         route += [pair, pair[::-1]]
-    got_edge = lax.ppermute(edge(own, got, lines), ("gy", "gx"), route)
+    got_edge = lax.ppermute(near + near_got, ("gy", "gx"), route)
     gridded, vm = grid(*on_chip(data, own, got, spread))
     wave, gridded, vm, got_edge = on_chip(wave, gridded, vm, got_edge)
     angs = lax.axis_size("ang")
@@ -623,6 +599,4 @@
         P("ang", "gy", "gx"),
         P("ang", "gy", "gx"),
     )
-    return jax.shard_map(
-        per_device, mesh=mesh, in_specs=placed, out_specs=P("ang", "gy", "gx"), check_vma=False
-    )
+    return jax.shard_map(per_device, mesh=mesh, in_specs=placed, out_specs=P("ang", "gy", "gx"), check_vma=False)

time: 29.5 us -> 29.4 us (level)
  Pallas kernels: 6.86 us -> 5.74 us
  waiting for transfers between devices: 4.81 us -> 5.74 us
    pallas_call x2 -> x1, Pallas kernels: 1.97 us -> 0.84 us  [spread_of(): pl.pallas_call(make_spread, out_shape=pltpu.VMEM((block_size, taps.shape[...]
    ppermute x1 -> x2, waiting for transfers between devices: 0.59 us -> 1.39 us  [the longest x1 0.81 us: project_paired(): near_got = lax.ppermute(near_sent, 'gy', [(0, 1), (1, 0)])]
    ppermute x1 -> x2, starting transfers between devices: 4.74 us -> 4.78 us  [the longest x1 4.7 us: project_paired(): got_edge = lax.ppermute(near + near_got, ('gy', 'gx'), route)]
  transfers between devices with their start and end apart: 5 -> 6, of which waited for: 4 -> 5; matrix products, arithmetic and copies ran while one was open for 0% -> 0% of each run, Pallas kernels for 12% -> 9%
where the time goes in v6:
time: 29.4 us; the launch traced here: 29.2 us
  starting transfers between devices  9.02 us (31%)
  blocking collectives  7.91 us (27%)
  Pallas kernels  5.74 us (20%)
  waiting for transfers between devices  5.74 us (20%)
  local copies, waits for them, and re-layouts  0.76 us (3%)
    all_to_all x1, blocking collectives, per_device(): done = lax.all_to_all(done, ('gy', 'ang'), split_axis=0, concat_axis=0)  7.91 us
    ppermute x1, starting transfers between devices, project_paired(): got_edge = lax.ppermute(near + near_got, ('gy', 'gx'), route)  4.7 us
    ppermute x3, waiting for transfers between devices, project_paired(): lax.ppermute(part, 'ang', [(ang, ang ^ apart) for ang in range(angs)])  4.35 us
    ppermute x3, starting transfers between devices, project_paired(): lax.ppermute(part, 'ang', [(ang, ang ^ apart) for ang in range(angs)])  3.68 us
    pallas_call x1, Pallas kernels, smooth(): pl.pallas_call(functools.partial(smooth_kernel, planes, columns), out_sha...  1.41 us
    pallas_call x1, Pallas kernels, pack(): pl.pallas_call(pack_kernel, out_shape=[pltpu.VMEM((rows + 2 * local_lines...  1.38 us
    pallas_call x4, Pallas kernels, block_of(): pl.pallas_call(functools.partial(block_kernel, apart), out_shape=pltpu.VM...  1.33 us
    pallas_call x1, Pallas kernels, spread_of(): pl.pallas_call(make_spread, out_shape=pltpu.VMEM((block_size, taps.shape[...  0.84 us
  transfers between devices with their start and end apart: 6, of which 5 were waited for; matrix products, arithmetic and copies ran while one was open for 0% of the time, Pallas kernels for 9%

profile of v6, /device:TPU:0, one launch (start us, length us, event | category | flops | bytes accessed | tf_op | source)
XLA Modules:
  0.0 29.2 jit_solution(11815164760277666354)
XLA Ops:
  0.0 1.4 %pack.1 = (f32[320,512]{1,0:T(8,128)S(1)}, bf16[256,512]{1,0:T(8,128)(2,1)S(1)}, s32[4,128]{1,0:T(4,128)S(1)}, s32[4,128]{1,0:T(4,128)S(1)}, f32[4,512]{1,0:T(4,...) custom-call(bf16[256,512]{1,0:T(8,128)(2,1)} %bitcast.7, ...), custom_call_target="tpu_custom_call" | custom-call | tf_op jit(solution)/shard_map/pack/pallas_call | solution.py:394
  1.4 0.6 %collective-permute-start = (f32[320,512]{1,0:T(8,128)S(1)}, f32[320,512]{1,0:T(8,128)S(1)}, u32[]{:S(2)}, u32[]{:S(2)}) collective-permute-start(f32[320,512]{1,0:T(8,128)S(1)} %get-tuple-element.20), channel_id=1, source_target_pairs={{0,4},{4,0},{1,5},{5,1},{2,6},{6,2},{3,7},{7,3},{8,12},{12,8},{9,1... | collective-permute-start | bytes 1966088 | tf_op jit(solution)/shard_map/ppermute | solution.py:539
  1.9 0.1 collective-permute-start.1
  2.0 0.8 %spread.1.spread_ref = bf16[1024,512]{1,0:T(8,128)(2,1)S(1)} custom-call(s32[4,128]{1,0:T(4,128)S(1)} %get-tuple-element.21.offsets_ref, s32[4,128]{1,0:T(4,128)S(1)} %get-tuple-element.22.view_ref, f32[4,512]{1,0:T(4,128)S(1)} %get-tuple-element.23.taps_ref, f32[1500]{0:T(1024)S(1)} %get-tuple-element.24.weight_ref), custom_call_target="tpu_custom_call" | custom-call | flops 2000000000 | bytes 1000000 | tf_op jit(solution)/shard_map/spread/pallas_call | solution.py:433
  2.9 0.8 %collective-permute-done.1 = f32[8,256]{1,0:T(8,128)S(1)} collective-permute-done((f32[8,256]{1,0:T(8,128)S(1)}, f32[8,256]{1,0:T(8,128)S(1)}, u32[]{:S(2)}, u32[]{:S(2)}) %collective-permute-start.1) | collective-permute-done | bytes 8224 | tf_op jit(solution)/shard_map/ppermute | solution.py:538
  3.7 4.7 %collective-permute-start.2 = (f32[8,256]{1,0:T(8,128)S(1)}, f32[8,256]{1,0:T(8,128)S(1)}, u32[]{:S(2)}, u32[]{:S(2)}) collective-permute-start(f32[8,256]{1,0:T(8,128)S(1)} %add.3), channel_id=1, source_target_pairs={{4,1},{1,4},{5,2},{2,5},{6,3},{3,6},{7,0},{0,7},{12,9},{9,12},{13,... | collective-permute-start | bytes 24584 | tf_op jit(solution)/shard_map/ppermute | solution.py:546
  8.4 0.0 collective-permute-done.got_ref
  8.4 0.8 %grid.1 = (bf16[2048,256]{1,0:T(8,128)(2,1)S(1)}, f32[520,256]{1,0:T(8,128)S(1)}) custom-call(bf16[256,512]{1,0:T(8,128)(2,1)S(1)} %get-tuple-element.18.data_ref, f32[32,640]{1,0:T(8,128)S(1)} %get-tuple-element.19.own_ref, f32[320,512]{1,0:T(8,128)S(1)} %collective-permute-done.got_ref, bf16[1024,512]{1,0:T(8,128)(2,1)S(1)} %spread.1.spread_ref), custom_call_target="tpu_custom_call" | custom-call | flops 1000000000 | bytes 1000000 | tf_op jit(solution)/shard_map/grid/pallas_call | solution.py:482
  9.2 0.6 %collective-permute-done.2.edge_ref = f32[8,256]{1,0:T(8,128)S(1)} collective-permute-done((f32[8,256]{1,0:T(8,128)S(1)}, f32[8,256]{1,0:T(8,128)S(1)}, u32[]{:S(2)}, u32[]{:S(2)}) %collective-permute-start.2) | collective-permute-done | bytes 8224 | tf_op jit(solution)/shard_map/ppermute | solution.py:546
  9.8 0.3 %shard_map.74 = f32[136,256]{1,0:T(8,128)S(1)} custom-call(bf16[528,2048]{1,0:T(8,128)(2,1)S(1)} %get-tuple-element.17.wave_ref, bf16[2048,256]{1,0:T(8,128)(2,1)S(1)} %get-tuple-element.25.grid_ref, f32[520,256]{1,0:T(8,128)S(1)} %get-tuple-element.26.vm_ref, f32[8,256]{1,0:T(8,128)S(1)} %collective-permute-done.2.edge_ref), custom_call_target="tpu_custom_call" | custom-call | flops 1000000000 | bytes 1000000 | tf_op jit(solution)/shard_map/pallas_call | solution.py:520
  10.1 2.7 %collective-permute-start.3 = (f32[136,256]{1,0:T(8,128)S(1)}, f32[136,256]{1,0:T(8,128)S(1)}, u32[]{:S(2)}, u32[]{:S(2)}) collective-permute-start(f32[136,256]{1,0:T(8,128)S(1)} %shard_map.74), channel_id=1, source_target_pairs={{0,24},{8,16},{16,8},{24,0},{1,25},{9,17},{17,9},{25,1},{2,26},{10... | collective-permute-start | bytes 417800 | tf_op jit(solution)/shard_map/ppermute | solution.py:553
  12.8 0.3 %shard_map.75 = f32[136,256]{1,0:T(8,128)S(1)} custom-call(bf16[528,2048]{1,0:T(8,128)(2,1)S(1)} %get-tuple-element.17.wave_ref, bf16[2048,256]{1,0:T(8,128)(2,1)S(1)} %get-tuple-element.25.grid_ref, f32[520,256]{1,0:T(8,128)S(1)} %get-tuple-element.26.vm_ref, f32[8,256]{1,0:T(8,128)S(1)} %collective-permute-done.2.edge_ref), custom_call_target="tpu_custom_call" | custom-call | flops 1000000000 | bytes 1000000 | tf_op jit(solution)/shard_map/pallas_call | solution.py:520
  13.1 0.6 %collective-permute-start.4 = (f32[136,256]{1,0:T(8,128)S(1)}, f32[136,256]{1,0:T(8,128)S(1)}, u32[]{:S(2)}, u32[]{:S(2)}) collective-permute-start(f32[136,256]{1,0:T(8,128)S(1)} %shard_map.75), channel_id=1, source_target_pairs={{0,16},{8,24},{16,0},{24,8},{1,17},{9,25},{17,1},{25,9},{2,18},{10... | collective-permute-start | bytes 417800 | tf_op jit(solution)/shard_map/ppermute | solution.py:553
  13.7 0.3 %shard_map.76 = f32[136,256]{1,0:T(8,128)S(1)} custom-call(bf16[528,2048]{1,0:T(8,128)(2,1)S(1)} %get-tuple-element.17.wave_ref, bf16[2048,256]{1,0:T(8,128)(2,1)S(1)} %get-tuple-element.25.grid_ref, f32[520,256]{1,0:T(8,128)S(1)} %get-tuple-element.26.vm_ref, f32[8,256]{1,0:T(8,128)S(1)} %collective-permute-done.2.edge_ref), custom_call_target="tpu_custom_call" | custom-call | flops 1000000000 | bytes 1000000 | tf_op jit(solution)/shard_map/pallas_call | solution.py:520
  14.0 0.4 %collective-permute-start.5 = (f32[136,256]{1,0:T(8,128)S(1)}, f32[136,256]{1,0:T(8,128)S(1)}, u32[]{:S(2)}, u32[]{:S(2)}) collective-permute-start(f32[136,256]{1,0:T(8,128)S(1)} %shard_map.76), channel_id=1, source_target_pairs={{0,8},{8,0},{16,24},{24,16},{1,9},{9,1},{17,25},{25,17},{2,10},{10... | collective-permute-start | bytes 417800 | tf_op jit(solution)/shard_map/ppermute | solution.py:553
  14.4 0.3 %shard_map.73.refs_0_ = f32[136,256]{1,0:T(8,128)S(1)} custom-call(bf16[528,2048]{1,0:T(8,128)(2,1)S(1)} %get-tuple-element.17.wave_ref, bf16[2048,256]{1,0:T(8,128)(2,1)S(1)} %get-tuple-element.25.grid_ref, f32[520,256]{1,0:T(8,128)S(1)} %get-tuple-element.26.vm_ref, f32[8,256]{1,0:T(8,128)S(1)} %collective-permute-done.2.edge_ref), custom_call_target="tpu_custom_call" | custom-call | flops 1000000000 | bytes 1000000 | tf_op jit(solution)/shard_map/pallas_call | solution.py:520
  14.8 2.0 %collective-permute-done.3.refs_1_ = f32[136,256]{1,0:T(8,128)S(1)} collective-permute-done((f32[136,256]{1,0:T(8,128)S(1)}, f32[136,256]{1,0:T(8,128)S(1)}, u32[]{:S(2)}, u32[]{:S(2)}) %collective-permute-start.3) | collective-permute-done | bytes 139296 | tf_op jit(solution)/shard_map/ppermute | solution.py:553
  16.8 1.5 %collective-permute-done.4.refs_2_ = f32[136,256]{1,0:T(8,128)S(1)} collective-permute-done((f32[136,256]{1,0:T(8,128)S(1)}, f32[136,256]{1,0:T(8,128)S(1)}, u32[]{:S(2)}, u32[]{:S(2)}) %collective-permute-start.4) | collective-permute-done | bytes 139296 | tf_op jit(solution)/shard_map/ppermute | solution.py:553
  18.3 0.8 %collective-permute-done.5.refs_3_ = f32[136,256]{1,0:T(8,128)S(1)} collective-permute-done((f32[136,256]{1,0:T(8,128)S(1)}, f32[136,256]{1,0:T(8,128)S(1)}, u32[]{:S(2)}, u32[]{:S(2)}) %collective-permute-start.5) | collective-permute-done | bytes 139296 | tf_op jit(solution)/shard_map/ppermute | solution.py:553
  19.1 1.4 %smooth.1 = f32[8,32,128]{2,1,0:T(8,128)S(1)} custom-call(f32[136,256]{1,0:T(8,128)S(1)} %shard_map.73.refs_0_, f32[136,256]{1,0:T(8,128)S(1)} %collective-permute-done.3.refs_1_, f32[136,256]{1,0:T(8,128)S(1)} %collective-permute-done.4.refs_2_, f32[136,256]{1,0:T(8,128)S(1)} %collective-permute-done.5.refs_3_), custom_call_target="tpu_custom_call" | custom-call | tf_op jit(solution)/shard_map/smooth/pallas_call | solution.py:300
  20.5 7.9 %all_to_all.5 = f32[8,32,128]{2,1,0:T(8,128)S(1)} all-to-all(f32[8,32,128]{2,1,0:T(8,128)S(1)} %smooth.1), channel_id=1, replica_groups=mesh['ang'=4,'gy'=2,'gx'=4] {'gy','ang'}, dimensions={0} | all-to-all | bytes 262144 | tf_op jit(solution)/shard_map/all_to_all | solution.py:588
  28.5 0.1 copy.8
  28.5 0.7 %reshape.23 = f32[4,8,1024]{2,1,0:T(8,128)} reshape(f32[32,8,128]{2,1,0:T(8,128)S(1)} %copy.8) | data formatting | bytes 262144 | tf_op jit(solution)/shard_map/reshape | solution.py:589
  (1 shorter events, 0.0 us)
Async XLA Ops:
  1.4 7.0 %collective-permute-start = (f32[320,512]{1,0:T(8,128)S(1)}, f32[320,512]{1,0:T(8,128)S(1)}, u32[]{:S(2)}, u32[]{:S(2)}) collective-permute-start(f32[320,512]{1,0:T(8,128)S(1)} %get-tuple-element.20), channel_id=1, source_target_pairs={{0,4},{4,0},{1,5},{5,1},{2,6},{6,2},{3,7},{7,3},{8,12},{12,8},{9,1... | collective-permute-start | bytes 1966088 | tf_op jit(solution)/shard_map/ppermute | solution.py:539
  1.9 1.7 %collective-permute-start.1 = (f32[8,256]{1,0:T(8,128)S(1)}, f32[8,256]{1,0:T(8,128)S(1)}, u32[]{:S(2)}, u32[]{:S(2)}) collective-permute-start(f32[8,256]{1,0:T(8,128)S(1)} %get-tuple-element.28), channel_id=1, source_target_pairs={{0,4},{4,0},{1,5},{5,1},{2,6},{6,2},{3,7},{7,3},{8,12},{12,8},{9,1... | collective-permute-start | bytes 24584 | tf_op jit(solution)/shard_map/ppermute | solution.py:538
  3.7 6.1 %collective-permute-start.2 = (f32[8,256]{1,0:T(8,128)S(1)}, f32[8,256]{1,0:T(8,128)S(1)}, u32[]{:S(2)}, u32[]{:S(2)}) collective-permute-start(f32[8,256]{1,0:T(8,128)S(1)} %add.3), channel_id=1, source_target_pairs={{4,1},{1,4},{5,2},{2,5},{6,3},{3,6},{7,0},{0,7},{12,9},{9,12},{13,... | collective-permute-start | bytes 24584 | tf_op jit(solution)/shard_map/ppermute | solution.py:546
  10.1 6.7 %collective-permute-start.3 = (f32[136,256]{1,0:T(8,128)S(1)}, f32[136,256]{1,0:T(8,128)S(1)}, u32[]{:S(2)}, u32[]{:S(2)}) collective-permute-start(f32[136,256]{1,0:T(8,128)S(1)} %shard_map.74), channel_id=1, source_target_pairs={{0,24},{8,16},{16,8},{24,0},{1,25},{9,17},{17,9},{25,1},{2,26},{10... | collective-permute-start | bytes 417800 | tf_op jit(solution)/shard_map/ppermute | solution.py:553
  13.1 5.2 %collective-permute-start.4 = (f32[136,256]{1,0:T(8,128)S(1)}, f32[136,256]{1,0:T(8,128)S(1)}, u32[]{:S(2)}, u32[]{:S(2)}) collective-permute-start(f32[136,256]{1,0:T(8,128)S(1)} %shard_map.75), channel_id=1, source_target_pairs={{0,16},{8,24},{16,0},{24,8},{1,17},{9,25},{17,1},{25,9},{2,18},{10... | collective-permute-start | bytes 417800 | tf_op jit(solution)/shard_map/ppermute | solution.py:553
  14.0 5.1 %collective-permute-start.5 = (f32[136,256]{1,0:T(8,128)S(1)}, f32[136,256]{1,0:T(8,128)S(1)}, u32[]{:S(2)}, u32[]{:S(2)}) collective-permute-start(f32[136,256]{1,0:T(8,128)S(1)} %shard_map.76), channel_id=1, source_target_pairs={{0,8},{8,0},{16,24},{24,16},{1,9},{9,1},{17,25},{25,17},{2,10},{10... | collective-permute-start | bytes 417800 | tf_op jit(solution)/shard_map/ppermute | solution.py:553

commit v7 on v6

--- a/solution.py
+++ b/solution.py
@@ -13,6 +13,7 @@
 TV_STEPS = 4
 HALO = TV_STEPS
 CHUNK = 128
+PIECE = 72
 VMEM_LIMIT = 24 * 2**20
 
 smooth_weight = 0.5
@@ -212,85 +213,99 @@
 
 
 def smooth_kernel(planes, columns, *refs):
-    *parts_refs, out_ref = refs
+    *parts_refs, out_ref, done_ref = refs
     _, local_lines, block = out_ref.shape
     window = parts_refs[0].shape[-2]
     angs, groups = lax.axis_size("ang"), lax.axis_size("gy")
     lines = angs * local_lines
     rows = lines // planes
-    lane = lax.broadcasted_iota(jnp.int32, (window, lines), 1)
-    lane_row = lane % rows
+    size = min(PIECE, window)
+    pieces = [(first, min(size, window - first)) for first in range(0, window, size)]
+    tiles = len(pieces)
+    lanes = [lax.broadcasted_iota(jnp.int32, (height, lines), 1) for _, height in pieces]
+    inside = lax.broadcasted_iota(jnp.int32, (8, lines), 0)
+    plane_opens = [lane // rows < planes - 1 for lane in lanes]
+    row_firsts = [lane % rows == 0 for lane in lanes]
+    row_lasts = [lane % rows == rows - 1 for lane in lanes]
     place = lax.axis_index("gy") * angs + lax.axis_index("ang")
-    column = lax.axis_index("gx") * columns + place * block - HALO + lax.broadcasted_iota(jnp.int32, (window, lines), 0)
-    plane_open = lane // rows < planes - 1
-    row_first = lane_row == 0
-    row_last = lane_row == rows - 1
-    cell_open = (column >= 0) & (column < NX - 1)
+    first_column = lax.axis_index("gx") * columns + place * block - HALO
     zero = jnp.float32(0.0)
 
-    source = []
+    def part(ang, group, tile):
+        at = pl.ds(*pieces[tile])
+        if len(parts_refs) > 1:
+            return parts_refs[ang][at, pl.ds(group * lines, lines)]
+        return parts_refs[0][group * angs + ang, at, :]
+
+    source = [[sum((part(ang, group, tile) for ang in range(1, angs)), part(0, group, tile)) for group in range(groups)]
+              for tile in range(tiles)]
+
+    def divergence(flow, tile):
+        rolled = [pltpu.roll(flow[tile][group][1], 1, 1) for group in range(groups)]
+        result = []
+        for group in range(groups):
+            f0, f1, f2 = flow[tile][group]
+            wrapped = pltpu.roll(flow[tile][group - 1][1], lines - (rows - 1), 1)
+            lower_row = jnp.where(row_firsts[tile], wrapped, rolled[group])
+            lower_cell = pltpu.roll(f2, 1, 0)
+            if tile > 0:
+                before = flow[tile - 1][group][2]
+                opening = jnp.where(inside == 0, pltpu.roll(before[-8:], 1, 0), lower_cell[:8])
+                lower_cell = jnp.concatenate([opening, lower_cell[8:]], axis=0)
+            result.append((f0 - pltpu.roll(f0, rows, 1)) + (f1 - lower_row) + (f2 - lower_cell))
+        return result
+
+    def target_of(flow, tile):
+        scaled = [value * (dual_step / smooth_weight) for value in source[tile]]
+        if flow is None:
+            return [-value for value in scaled]
+        return [dual_step * div - value for div, value in zip(divergence(flow, tile), scaled)]
+
+    flow = None
+    for _ in range(TV_STEPS):
+        updated = []
+        after = target_of(flow, 0)
+        for tile in range(tiles):
+            target = after
+            after = target_of(flow, tile + 1) if tile + 1 < tiles else target
+            _, height = pieces[tile]
+            plane_open, row_last = plane_opens[tile], row_lasts[tile]
+            moved_groups = []
+            for group in range(groups):
+                here = target[group]
+                slope_plane = jnp.where(plane_open, pltpu.roll(here, lines - rows, 1) - here, zero)
+                upper_row = pltpu.roll(here, lines - 1, 1)
+                if group + 1 < groups:
+                    slope_row = jnp.where(row_last, pltpu.roll(target[group + 1], rows - 1, 1), upper_row) - here
+                else:
+                    slope_row = jnp.where(row_last, zero, upper_row - here)
+                upper_cell = pltpu.roll(here, height - 1, 0)
+                if tile + 1 < tiles:
+                    closing = jnp.where(inside == 7, pltpu.roll(after[group][:8], 7, 0), upper_cell[-8:])
+                    upper_cell = jnp.concatenate([upper_cell[:-8], closing], axis=0)
+                slope_cell = upper_cell - here
+                if tile == 0:
+                    opening = jnp.where(first_column + inside >= 0, slope_cell[:8], zero)
+                    slope_cell = jnp.concatenate([opening, slope_cell[8:]], axis=0)
+                if tile == tiles - 1:
+                    column = first_column + window - 8 + inside
+                    closing = jnp.where(column < NX - 1, slope_cell[-8:], zero)
+                    slope_cell = jnp.concatenate([slope_cell[:-8], closing], axis=0)
+                square = slope_plane * slope_plane + slope_row * slope_row + slope_cell * slope_cell
+                scale = 1.0 / (1.0 + square * lax.rsqrt(jnp.maximum(square, 1e-30)))
+                moved = [slope_plane, slope_row, slope_cell]
+                if flow is not None:
+                    moved = [f + m for f, m in zip(flow[tile][group], moved)]
+                moved_groups.append([m * scale for m in moved])
+            updated.append(moved_groups)
+        flow = updated
+    for tile in range(tiles):
+        for group, div in enumerate(divergence(flow, tile)):
+            done_ref[group, pl.ds(*pieces[tile]), :] = source[tile][group] - smooth_weight * div
     for group in range(groups):
-        total = None
+        turned = done_ref[group, pl.ds(HALO, block), :].T
         for ang in range(angs):
-            if len(parts_refs) > 1:
-                part = parts_refs[ang][:, pl.ds(group * lines, lines)]
-            else:
-                part = parts_refs[0][group * angs + ang]
-            total = part if total is None else total + part
-        source.append(total)
-    scaled = [value * (dual_step / smooth_weight) for value in source]
-
-    def down(values):
-        lower = []
-        for group in range(groups):
-            previous = values[group - 1]
-            lower.append(
-                jnp.where(
-                    row_first, pltpu.roll(previous, lines - (rows - 1), 1), pltpu.roll(values[group], 1, 1)
-                )
-            )
-        return lower
-
-    flow = None
-    for repeat in range(TV_STEPS + 1):
-        if flow is None:
-            target = [-value for value in scaled]
-        else:
-            lower_row = down([f[1] for f in flow])
-            local_div = []
-            for group in range(groups):
-                f0, f1, f2 = flow[group]
-                plane_part = f0 - pltpu.roll(f0, rows, 1)
-                row_part = f1 - lower_row[group]
-                cell_part = f2 - pltpu.roll(f2, 1, 0)
-                local_div.append(plane_part + row_part + cell_part)
-            if repeat == TV_STEPS:
-                for group in range(groups):
-                    done = source[group] - smooth_weight * local_div[group]
-                    turned = done[HALO : HALO + block].T
-                    for ang in range(angs):
-                        out_ref[group * angs + ang] = turned[ang * local_lines : (ang + 1) * local_lines]
-                return
-            target = [dual_step * local_div[group] - scaled[group] for group in range(groups)]
-        updated = []
-        for group in range(groups):
-            here = target[group]
-            slope_plane = jnp.where(plane_open, pltpu.roll(here, lines - rows, 1) - here, zero)
-            if group + 1 < groups:
-                upper = jnp.where(
-                    row_last, pltpu.roll(target[group + 1], rows - 1, 1), pltpu.roll(here, lines - 1, 1)
-                )
-                slope_row = upper - here
-            else:
-                slope_row = jnp.where(row_last, zero, pltpu.roll(here, lines - 1, 1) - here)
-            slope_cell = jnp.where(cell_open, pltpu.roll(here, window - 1, 0) - here, zero)
-            square = slope_plane * slope_plane + slope_row * slope_row + slope_cell * slope_cell
-            scale = 1.0 / (1.0 + square * lax.rsqrt(jnp.maximum(square, 1e-30)))
-            moved = [slope_plane, slope_row, slope_cell]
-            if flow is not None:
-                moved = [f + m for f, m in zip(flow[group], moved)]
-            updated.append([m * scale for m in moved])
-        flow = updated
+            out_ref[group * angs + ang] = turned[ang * local_lines : (ang + 1) * local_lines]
 
 
 def smooth(parts, planes, local_lines, columns):
@@ -302,6 +317,9 @@
         out_shape=pltpu.VMEM((dests, local_lines, window - 2 * HALO), jnp.float32),
         in_specs=[vmem] * len(parts),
         out_specs=vmem,
+        scratch_shapes=[
+            pltpu.VMEM((lax.axis_size("gy"), window, lax.axis_size("ang") * local_lines), jnp.float32)
+        ],
         compiler_params=pltpu.CompilerParams(vmem_limit_bytes=VMEM_LIMIT),
         name="smooth",
     )(*parts)

time: 29.4 us -> 29.1 us (0.990)
  Pallas kernels: 5.74 us -> 5.42 us
    pallas_call x1, Pallas kernels: 1.41 us -> 1.09 us  [smooth(): pl.pallas_call(functools.partial(smooth_kernel, planes, columns), out_sha...]
where the time goes in v7:
time: 29.1 us; the launch traced here: 28.9 us
  starting transfers between devices  9.02 us (31%)
  blocking collectives  7.91 us (27%)
  waiting for transfers between devices  5.74 us (20%)
  Pallas kernels  5.42 us (19%)
  local copies, waits for them, and re-layouts  0.76 us (3%)
    all_to_all x1, blocking collectives, per_device(): done = lax.all_to_all(done, ('gy', 'ang'), split_axis=0, concat_axis=0)  7.91 us
    ppermute x1, starting transfers between devices, project_paired(): got_edge = lax.ppermute(near + near_got, ('gy', 'gx'), route)  4.7 us
    ppermute x3, waiting for transfers between devices, project_paired(): lax.ppermute(part, 'ang', [(ang, ang ^ apart) for ang in range(angs)])  4.35 us
    ppermute x3, starting transfers between devices, project_paired(): lax.ppermute(part, 'ang', [(ang, ang ^ apart) for ang in range(angs)])  3.68 us
    pallas_call x1, Pallas kernels, pack(): pl.pallas_call(pack_kernel, out_shape=[pltpu.VMEM((rows + 2 * local_lines...  1.38 us
    pallas_call x4, Pallas kernels, block_of(): pl.pallas_call(functools.partial(block_kernel, apart), out_shape=pltpu.VM...  1.33 us
    pallas_call x1, Pallas kernels, smooth(): pl.pallas_call(functools.partial(smooth_kernel, planes, columns), out_sha...  1.09 us
    pallas_call x1, Pallas kernels, spread_of(): pl.pallas_call(make_spread, out_shape=pltpu.VMEM((block_size, taps.shape[...  0.84 us
  transfers between devices with their start and end apart: 6, of which 5 were waited for; matrix products, arithmetic and copies ran while one was open for 0% of the time, Pallas kernels for 9%

profile of v7, /device:TPU:0, one launch (start us, length us, event | category | flops | bytes accessed | tf_op | source)
XLA Modules:
  0.0 28.9 jit_solution(16396755005150637254)
XLA Ops:
  0.0 1.4 %pack.1 = (f32[320,512]{1,0:T(8,128)S(1)}, bf16[256,512]{1,0:T(8,128)(2,1)S(1)}, s32[4,128]{1,0:T(4,128)S(1)}, s32[4,128]{1,0:T(4,128)S(1)}, f32[4,512]{1,0:T(4,...) custom-call(bf16[256,512]{1,0:T(8,128)(2,1)} %bitcast.7, ...), custom_call_target="tpu_custom_call" | custom-call | tf_op jit(solution)/shard_map/pack/pallas_call | solution.py:412
  1.4 0.6 %collective-permute-start = (f32[320,512]{1,0:T(8,128)S(1)}, f32[320,512]{1,0:T(8,128)S(1)}, u32[]{:S(2)}, u32[]{:S(2)}) collective-permute-start(f32[320,512]{1,0:T(8,128)S(1)} %get-tuple-element.20), channel_id=1, source_target_pairs={{0,4},{4,0},{1,5},{5,1},{2,6},{6,2},{3,7},{7,3},{8,12},{12,8},{9,1... | collective-permute-start | bytes 1966088 | tf_op jit(solution)/shard_map/ppermute | solution.py:557
  1.9 0.1 collective-permute-start.1
  2.0 0.8 %spread.1.spread_ref = bf16[1024,512]{1,0:T(8,128)(2,1)S(1)} custom-call(s32[4,128]{1,0:T(4,128)S(1)} %get-tuple-element.21.offsets_ref, s32[4,128]{1,0:T(4,128)S(1)} %get-tuple-element.22.view_ref, f32[4,512]{1,0:T(4,128)S(1)} %get-tuple-element.23.taps_ref, f32[1500]{0:T(1024)S(1)} %get-tuple-element.24.weight_ref), custom_call_target="tpu_custom_call" | custom-call | flops 2000000000 | bytes 1000000 | tf_op jit(solution)/shard_map/spread/pallas_call | solution.py:451
  2.9 0.8 %collective-permute-done.1 = f32[8,256]{1,0:T(8,128)S(1)} collective-permute-done((f32[8,256]{1,0:T(8,128)S(1)}, f32[8,256]{1,0:T(8,128)S(1)}, u32[]{:S(2)}, u32[]{:S(2)}) %collective-permute-start.1) | collective-permute-done | bytes 8224 | tf_op jit(solution)/shard_map/ppermute | solution.py:556
  3.7 4.7 %collective-permute-start.2 = (f32[8,256]{1,0:T(8,128)S(1)}, f32[8,256]{1,0:T(8,128)S(1)}, u32[]{:S(2)}, u32[]{:S(2)}) collective-permute-start(f32[8,256]{1,0:T(8,128)S(1)} %add.3), channel_id=1, source_target_pairs={{4,1},{1,4},{5,2},{2,5},{6,3},{3,6},{7,0},{0,7},{12,9},{9,12},{13,... | collective-permute-start | bytes 24584 | tf_op jit(solution)/shard_map/ppermute | solution.py:564
  8.4 0.0 collective-permute-done.got_ref
  8.4 0.8 %grid.1 = (bf16[2048,256]{1,0:T(8,128)(2,1)S(1)}, f32[520,256]{1,0:T(8,128)S(1)}) custom-call(bf16[256,512]{1,0:T(8,128)(2,1)S(1)} %get-tuple-element.18.data_ref, f32[32,640]{1,0:T(8,128)S(1)} %get-tuple-element.19.own_ref, f32[320,512]{1,0:T(8,128)S(1)} %collective-permute-done.got_ref, bf16[1024,512]{1,0:T(8,128)(2,1)S(1)} %spread.1.spread_ref), custom_call_target="tpu_custom_call" | custom-call | flops 1000000000 | bytes 1000000 | tf_op jit(solution)/shard_map/grid/pallas_call | solution.py:500
  9.2 0.6 %collective-permute-done.2.edge_ref = f32[8,256]{1,0:T(8,128)S(1)} collective-permute-done((f32[8,256]{1,0:T(8,128)S(1)}, f32[8,256]{1,0:T(8,128)S(1)}, u32[]{:S(2)}, u32[]{:S(2)}) %collective-permute-start.2) | collective-permute-done | bytes 8224 | tf_op jit(solution)/shard_map/ppermute | solution.py:564
  9.8 0.3 %shard_map.74 = f32[136,256]{1,0:T(8,128)S(1)} custom-call(bf16[528,2048]{1,0:T(8,128)(2,1)S(1)} %get-tuple-element.17.wave_ref, bf16[2048,256]{1,0:T(8,128)(2,1)S(1)} %get-tuple-element.25.grid_ref, f32[520,256]{1,0:T(8,128)S(1)} %get-tuple-element.26.vm_ref, f32[8,256]{1,0:T(8,128)S(1)} %collective-permute-done.2.edge_ref), custom_call_target="tpu_custom_call" | custom-call | flops 1000000000 | bytes 1000000 | tf_op jit(solution)/shard_map/pallas_call | solution.py:538
  10.1 2.7 %collective-permute-start.3 = (f32[136,256]{1,0:T(8,128)S(1)}, f32[136,256]{1,0:T(8,128)S(1)}, u32[]{:S(2)}, u32[]{:S(2)}) collective-permute-start(f32[136,256]{1,0:T(8,128)S(1)} %shard_map.74), channel_id=1, source_target_pairs={{0,24},{8,16},{16,8},{24,0},{1,25},{9,17},{17,9},{25,1},{2,26},{10... | collective-permute-start | bytes 417800 | tf_op jit(solution)/shard_map/ppermute | solution.py:571
  12.8 0.3 %shard_map.75 = f32[136,256]{1,0:T(8,128)S(1)} custom-call(bf16[528,2048]{1,0:T(8,128)(2,1)S(1)} %get-tuple-element.17.wave_ref, bf16[2048,256]{1,0:T(8,128)(2,1)S(1)} %get-tuple-element.25.grid_ref, f32[520,256]{1,0:T(8,128)S(1)} %get-tuple-element.26.vm_ref, f32[8,256]{1,0:T(8,128)S(1)} %collective-permute-done.2.edge_ref), custom_call_target="tpu_custom_call" | custom-call | flops 1000000000 | bytes 1000000 | tf_op jit(solution)/shard_map/pallas_call | solution.py:538
  13.1 0.6 %collective-permute-start.4 = (f32[136,256]{1,0:T(8,128)S(1)}, f32[136,256]{1,0:T(8,128)S(1)}, u32[]{:S(2)}, u32[]{:S(2)}) collective-permute-start(f32[136,256]{1,0:T(8,128)S(1)} %shard_map.75), channel_id=1, source_target_pairs={{0,16},{8,24},{16,0},{24,8},{1,17},{9,25},{17,1},{25,9},{2,18},{10... | collective-permute-start | bytes 417800 | tf_op jit(solution)/shard_map/ppermute | solution.py:571
  13.7 0.3 %shard_map.76 = f32[136,256]{1,0:T(8,128)S(1)} custom-call(bf16[528,2048]{1,0:T(8,128)(2,1)S(1)} %get-tuple-element.17.wave_ref, bf16[2048,256]{1,0:T(8,128)(2,1)S(1)} %get-tuple-element.25.grid_ref, f32[520,256]{1,0:T(8,128)S(1)} %get-tuple-element.26.vm_ref, f32[8,256]{1,0:T(8,128)S(1)} %collective-permute-done.2.edge_ref), custom_call_target="tpu_custom_call" | custom-call | flops 1000000000 | bytes 1000000 | tf_op jit(solution)/shard_map/pallas_call | solution.py:538
  14.0 0.4 %collective-permute-start.5 = (f32[136,256]{1,0:T(8,128)S(1)}, f32[136,256]{1,0:T(8,128)S(1)}, u32[]{:S(2)}, u32[]{:S(2)}) collective-permute-start(f32[136,256]{1,0:T(8,128)S(1)} %shard_map.76), channel_id=1, source_target_pairs={{0,8},{8,0},{16,24},{24,16},{1,9},{9,1},{17,25},{25,17},{2,10},{10... | collective-permute-start | bytes 417800 | tf_op jit(solution)/shard_map/ppermute | solution.py:571
  14.4 0.3 %shard_map.73.refs_0_ = f32[136,256]{1,0:T(8,128)S(1)} custom-call(bf16[528,2048]{1,0:T(8,128)(2,1)S(1)} %get-tuple-element.17.wave_ref, bf16[2048,256]{1,0:T(8,128)(2,1)S(1)} %get-tuple-element.25.grid_ref, f32[520,256]{1,0:T(8,128)S(1)} %get-tuple-element.26.vm_ref, f32[8,256]{1,0:T(8,128)S(1)} %collective-permute-done.2.edge_ref), custom_call_target="tpu_custom_call" | custom-call | flops 1000000000 | bytes 1000000 | tf_op jit(solution)/shard_map/pallas_call | solution.py:538
  14.8 2.0 %collective-permute-done.3.refs_1_ = f32[136,256]{1,0:T(8,128)S(1)} collective-permute-done((f32[136,256]{1,0:T(8,128)S(1)}, f32[136,256]{1,0:T(8,128)S(1)}, u32[]{:S(2)}, u32[]{:S(2)}) %collective-permute-start.3) | collective-permute-done | bytes 139296 | tf_op jit(solution)/shard_map/ppermute | solution.py:571
  16.8 1.5 %collective-permute-done.4.refs_2_ = f32[136,256]{1,0:T(8,128)S(1)} collective-permute-done((f32[136,256]{1,0:T(8,128)S(1)}, f32[136,256]{1,0:T(8,128)S(1)}, u32[]{:S(2)}, u32[]{:S(2)}) %collective-permute-start.4) | collective-permute-done | bytes 139296 | tf_op jit(solution)/shard_map/ppermute | solution.py:571
  18.3 0.8 %collective-permute-done.5.refs_3_ = f32[136,256]{1,0:T(8,128)S(1)} collective-permute-done((f32[136,256]{1,0:T(8,128)S(1)}, f32[136,256]{1,0:T(8,128)S(1)}, u32[]{:S(2)}, u32[]{:S(2)}) %collective-permute-start.5) | collective-permute-done | bytes 139296 | tf_op jit(solution)/shard_map/ppermute | solution.py:571
  19.1 1.1 %smooth.1 = f32[8,32,128]{2,1,0:T(8,128)S(1)} custom-call(f32[136,256]{1,0:T(8,128)S(1)} %shard_map.73.refs_0_, f32[136,256]{1,0:T(8,128)S(1)} %collective-permute-done.3.refs_1_, f32[136,256]{1,0:T(8,128)S(1)} %collective-permute-done.4.refs_2_, f32[136,256]{1,0:T(8,128)S(1)} %collective-permute-done.5.refs_3_), custom_call_target="tpu_custom_call" | custom-call | tf_op jit(solution)/shard_map/smooth/pallas_call | solution.py:315
  20.2 7.9 %all_to_all.5 = f32[8,32,128]{2,1,0:T(8,128)S(1)} all-to-all(f32[8,32,128]{2,1,0:T(8,128)S(1)} %smooth.1), channel_id=1, replica_groups=mesh['ang'=4,'gy'=2,'gx'=4] {'gy','ang'}, dimensions={0} | all-to-all | bytes 262144 | tf_op jit(solution)/shard_map/all_to_all | solution.py:606
  28.1 0.1 copy.8
  28.2 0.7 %reshape.23 = f32[4,8,1024]{2,1,0:T(8,128)} reshape(f32[32,8,128]{2,1,0:T(8,128)S(1)} %copy.8) | data formatting | bytes 262144 | tf_op jit(solution)/shard_map/reshape | solution.py:607
  (1 shorter events, 0.0 us)
Async XLA Ops:
  1.4 7.0 %collective-permute-start = (f32[320,512]{1,0:T(8,128)S(1)}, f32[320,512]{1,0:T(8,128)S(1)}, u32[]{:S(2)}, u32[]{:S(2)}) collective-permute-start(f32[320,512]{1,0:T(8,128)S(1)} %get-tuple-element.20), channel_id=1, source_target_pairs={{0,4},{4,0},{1,5},{5,1},{2,6},{6,2},{3,7},{7,3},{8,12},{12,8},{9,1... | collective-permute-start | bytes 1966088 | tf_op jit(solution)/shard_map/ppermute | solution.py:557
  1.9 1.7 %collective-permute-start.1 = (f32[8,256]{1,0:T(8,128)S(1)}, f32[8,256]{1,0:T(8,128)S(1)}, u32[]{:S(2)}, u32[]{:S(2)}) collective-permute-start(f32[8,256]{1,0:T(8,128)S(1)} %get-tuple-element.28), channel_id=1, source_target_pairs={{0,4},{4,0},{1,5},{5,1},{2,6},{6,2},{3,7},{7,3},{8,12},{12,8},{9,1... | collective-permute-start | bytes 24584 | tf_op jit(solution)/shard_map/ppermute | solution.py:556
  3.7 6.1 %collective-permute-start.2 = (f32[8,256]{1,0:T(8,128)S(1)}, f32[8,256]{1,0:T(8,128)S(1)}, u32[]{:S(2)}, u32[]{:S(2)}) collective-permute-start(f32[8,256]{1,0:T(8,128)S(1)} %add.3), channel_id=1, source_target_pairs={{4,1},{1,4},{5,2},{2,5},{6,3},{3,6},{7,0},{0,7},{12,9},{9,12},{13,... | collective-permute-start | bytes 24584 | tf_op jit(solution)/shard_map/ppermute | solution.py:564
  10.1 6.7 %collective-permute-start.3 = (f32[136,256]{1,0:T(8,128)S(1)}, f32[136,256]{1,0:T(8,128)S(1)}, u32[]{:S(2)}, u32[]{:S(2)}) collective-permute-start(f32[136,256]{1,0:T(8,128)S(1)} %shard_map.74), channel_id=1, source_target_pairs={{0,24},{8,16},{16,8},{24,0},{1,25},{9,17},{17,9},{25,1},{2,26},{10... | collective-permute-start | bytes 417800 | tf_op jit(solution)/shard_map/ppermute | solution.py:571
  13.1 5.2 %collective-permute-start.4 = (f32[136,256]{1,0:T(8,128)S(1)}, f32[136,256]{1,0:T(8,128)S(1)}, u32[]{:S(2)}, u32[]{:S(2)}) collective-permute-start(f32[136,256]{1,0:T(8,128)S(1)} %shard_map.75), channel_id=1, source_target_pairs={{0,16},{8,24},{16,0},{24,8},{1,17},{9,25},{17,1},{25,9},{2,18},{10... | collective-permute-start | bytes 417800 | tf_op jit(solution)/shard_map/ppermute | solution.py:571
  14.0 5.1 %collective-permute-start.5 = (f32[136,256]{1,0:T(8,128)S(1)}, f32[136,256]{1,0:T(8,128)S(1)}, u32[]{:S(2)}, u32[]{:S(2)}) collective-permute-start(f32[136,256]{1,0:T(8,128)S(1)} %shard_map.76), channel_id=1, source_target_pairs={{0,8},{8,0},{16,24},{24,16},{1,9},{9,1},{17,25},{25,17},{2,10},{10... | collective-permute-start | bytes 417800 | tf_op jit(solution)/shard_map/ppermute | solution.py:571

commit v8 on v7

--- a/solution.py
+++ b/solution.py
@@ -558,13 +558,17 @@
     spread = spread_of(*on_chip(offsets, view_index, taps, view_weight))
     count = lax.axis_size("gx")
     route = []
-    for low in range(count):
-        pair = (count + low, (low + 1) % count)
-        route += [pair, pair[::-1]]
-    got_edge = lax.ppermute(near + near_got, ("gy", "gx"), route)
+    angs = lax.axis_size("ang")
+    for ang in range(angs):
+        for low in range(count - 1):
+            pair = ((2 * ang + 1) * count + low, 2 * ang * count + low + 1)
+            route += [pair, pair[::-1]]
+        beside = ang ^ 1 if angs > 1 else ang
+        route.append((2 * ang * count, 2 * beside * count))
+        route.append(((2 * ang + 2) * count - 1, (2 * beside + 2) * count - 1))
+    got_edge = lax.ppermute(near + near_got, ("ang", "gy", "gx"), route)
     gridded, vm = grid(*on_chip(data, own, got, spread))
     wave, gridded, vm, got_edge = on_chip(wave, gridded, vm, got_edge)
-    angs = lax.axis_size("ang")
     parts = []
     for apart in range(angs - 1, 0, -1):
         part = block_of(apart, wave, gridded, vm, got_edge)
@@ -604,7 +608,8 @@
         parts = [lax.all_to_all(parts, ("gy", "ang"), split_axis=0, concat_axis=0)]
     done = smooth(on_chip(*parts), planes, local_lines, columns)
     done = lax.all_to_all(done, ("gy", "ang"), split_axis=0, concat_axis=0)
-    return jnp.transpose(done, (1, 0, 2)).reshape(local_planes, rows, columns)
+    done = done.reshape(done.shape[0], local_planes, rows, done.shape[2])
+    return jnp.transpose(done, (1, 2, 0, 3)).reshape(local_planes, rows, columns)
 
 
 def solution(mesh):

time: 29.1 us -> 28.6 us (0.983)
  starting transfers between devices: 9.02 us -> 7.24 us
  waiting for transfers between devices: 5.74 us -> 6.57 us
  blocking collectives: 7.91 us -> 8.5 us
    ppermute x1, starting transfers between devices: 4.7 us -> 2.85 us  [project_paired(): got_edge = lax.ppermute(near + near_got, ('ang', 'gy', 'gx'), route)]
    all_to_all x1, blocking collectives: 7.91 us -> 8.5 us  [per_device(): done = lax.all_to_all(done, ('gy', 'ang'), split_axis=0, concat_axis=0)]
    ppermute x3, waiting for transfers between devices: 4.35 us -> 4.92 us  [project_paired(): lax.ppermute(part, 'ang', [(ang, ang ^ apart) for ang in range(angs)])]
  transfers between devices with their start and end apart: 6 -> 6, of which waited for: 5 -> 4; matrix products, arithmetic and copies ran while one was open for 0% -> 0% of each run, Pallas kernels for 9% -> 9%
where the time goes in v8:
time: 28.6 us; the launch traced here: 28.4 us
  blocking collectives  8.5 us (30%)
  starting transfers between devices  7.24 us (25%)
  waiting for transfers between devices  6.57 us (23%)
  Pallas kernels  5.42 us (19%)
  local copies, waits for them, and re-layouts  0.66 us (2%)
    all_to_all x1, blocking collectives, per_device(): done = lax.all_to_all(done, ('gy', 'ang'), split_axis=0, concat_axis=0)  8.5 us
    ppermute x3, waiting for transfers between devices, project_paired(): lax.ppermute(part, 'ang', [(ang, ang ^ apart) for ang in range(angs)])  4.92 us
    ppermute x3, starting transfers between devices, project_paired(): lax.ppermute(part, 'ang', [(ang, ang ^ apart) for ang in range(angs)])  3.76 us
    ppermute x1, starting transfers between devices, project_paired(): got_edge = lax.ppermute(near + near_got, ('ang', 'gy', 'gx'), route)  2.85 us
    pallas_call x1, Pallas kernels, pack(): pl.pallas_call(pack_kernel, out_shape=[pltpu.VMEM((rows + 2 * local_lines...  1.38 us
    pallas_call x4, Pallas kernels, block_of(): pl.pallas_call(functools.partial(block_kernel, apart), out_shape=pltpu.VM...  1.33 us
    pallas_call x1, Pallas kernels, smooth(): pl.pallas_call(functools.partial(smooth_kernel, planes, columns), out_sha...  1.09 us
    pallas_call x1, Pallas kernels, spread_of(): pl.pallas_call(make_spread, out_shape=pltpu.VMEM((block_size, taps.shape[...  0.84 us
  transfers between devices with their start and end apart: 6, of which 4 were waited for; matrix products, arithmetic and copies ran while one was open for 0% of the time, Pallas kernels for 9%

profile of v8, /device:TPU:0, one launch (start us, length us, event | category | flops | bytes accessed | tf_op | source)
XLA Modules:
  0.0 28.4 jit_solution(14642905820499181868)
XLA Ops:
  0.0 1.4 %pack.1 = (f32[320,512]{1,0:T(8,128)S(1)}, bf16[256,512]{1,0:T(8,128)(2,1)S(1)}, s32[4,128]{1,0:T(4,128)S(1)}, s32[4,128]{1,0:T(4,128)S(1)}, f32[4,512]{1,0:T(4,...) custom-call(bf16[256,512]{1,0:T(8,128)(2,1)} %bitcast.12, ...), custom_call_target="tpu_custom_call" | custom-call | tf_op jit(solution)/shard_map/pack/pallas_call | solution.py:412
  1.4 0.6 %collective-permute-start = (f32[320,512]{1,0:T(8,128)S(1)}, f32[320,512]{1,0:T(8,128)S(1)}, u32[]{:S(2)}, u32[]{:S(2)}) collective-permute-start(f32[320,512]{1,0:T(8,128)S(1)} %get-tuple-element.20), channel_id=1, source_target_pairs={{0,4},{4,0},{1,5},{5,1},{2,6},{6,2},{3,7},{7,3},{8,12},{12,8},{9,1... | collective-permute-start | bytes 1966088 | tf_op jit(solution)/shard_map/ppermute | solution.py:557
  1.9 0.1 collective-permute-start.1
  2.0 0.8 %spread.1.spread_ref = bf16[1024,512]{1,0:T(8,128)(2,1)S(1)} custom-call(s32[4,128]{1,0:T(4,128)S(1)} %get-tuple-element.21.offsets_ref, s32[4,128]{1,0:T(4,128)S(1)} %get-tuple-element.22.view_ref, f32[4,512]{1,0:T(4,128)S(1)} %get-tuple-element.23.taps_ref, f32[1500]{0:T(1024)S(1)} %get-tuple-element.24.weight_ref), custom_call_target="tpu_custom_call" | custom-call | flops 2000000000 | bytes 1000000 | tf_op jit(solution)/shard_map/spread/pallas_call | solution.py:451
  2.9 0.8 %collective-permute-done.1 = f32[8,256]{1,0:T(8,128)S(1)} collective-permute-done((f32[8,256]{1,0:T(8,128)S(1)}, f32[8,256]{1,0:T(8,128)S(1)}, u32[]{:S(2)}, u32[]{:S(2)}) %collective-permute-start.1) | collective-permute-done | bytes 8224 | tf_op jit(solution)/shard_map/ppermute | solution.py:556
  3.7 2.8 %collective-permute-start.2 = (f32[8,256]{1,0:T(8,128)S(1)}, f32[8,256]{1,0:T(8,128)S(1)}, u32[]{:S(2)}, u32[]{:S(2)}) collective-permute-start(f32[8,256]{1,0:T(8,128)S(1)} %add.3), channel_id=1, source_target_pairs={{4,1},{1,4},{5,2},{2,5},{6,3},{3,6},{0,8},{7,15},{12,9},{9,12},{13... | collective-permute-start | bytes 24584 | tf_op jit(solution)/shard_map/ppermute | solution.py:569
  6.5 0.0 collective-permute-done.got_ref
  6.5 0.8 %grid.1 = (bf16[2048,256]{1,0:T(8,128)(2,1)S(1)}, f32[520,256]{1,0:T(8,128)S(1)}) custom-call(bf16[256,512]{1,0:T(8,128)(2,1)S(1)} %get-tuple-element.18.data_ref, f32[32,640]{1,0:T(8,128)S(1)} %get-tuple-element.19.own_ref, f32[320,512]{1,0:T(8,128)S(1)} %collective-permute-done.got_ref, bf16[1024,512]{1,0:T(8,128)(2,1)S(1)} %spread.1.spread_ref), custom_call_target="tpu_custom_call" | custom-call | flops 1000000000 | bytes 1000000 | tf_op jit(solution)/shard_map/grid/pallas_call | solution.py:500
  7.3 0.8 %collective-permute-done.2.edge_ref = f32[8,256]{1,0:T(8,128)S(1)} collective-permute-done((f32[8,256]{1,0:T(8,128)S(1)}, f32[8,256]{1,0:T(8,128)S(1)}, u32[]{:S(2)}, u32[]{:S(2)}) %collective-permute-start.2) | collective-permute-done | bytes 8224 | tf_op jit(solution)/shard_map/ppermute | solution.py:569
  8.2 0.3 %shard_map.74 = f32[136,256]{1,0:T(8,128)S(1)} custom-call(bf16[528,2048]{1,0:T(8,128)(2,1)S(1)} %get-tuple-element.17.wave_ref, bf16[2048,256]{1,0:T(8,128)(2,1)S(1)} %get-tuple-element.25.grid_ref, f32[520,256]{1,0:T(8,128)S(1)} %get-tuple-element.26.vm_ref, f32[8,256]{1,0:T(8,128)S(1)} %collective-permute-done.2.edge_ref), custom_call_target="tpu_custom_call" | custom-call | flops 1000000000 | bytes 1000000 | tf_op jit(solution)/shard_map/pallas_call | solution.py:538
  8.5 3.0 %collective-permute-start.3 = (f32[136,256]{1,0:T(8,128)S(1)}, f32[136,256]{1,0:T(8,128)S(1)}, u32[]{:S(2)}, u32[]{:S(2)}) collective-permute-start(f32[136,256]{1,0:T(8,128)S(1)} %shard_map.74), channel_id=1, source_target_pairs={{0,24},{8,16},{16,8},{24,0},{1,25},{9,17},{17,9},{25,1},{2,26},{10... | collective-permute-start | bytes 417800 | tf_op jit(solution)/shard_map/ppermute | solution.py:575
  11.5 0.3 %shard_map.75 = f32[136,256]{1,0:T(8,128)S(1)} custom-call(bf16[528,2048]{1,0:T(8,128)(2,1)S(1)} %get-tuple-element.17.wave_ref, bf16[2048,256]{1,0:T(8,128)(2,1)S(1)} %get-tuple-element.25.grid_ref, f32[520,256]{1,0:T(8,128)S(1)} %get-tuple-element.26.vm_ref, f32[8,256]{1,0:T(8,128)S(1)} %collective-permute-done.2.edge_ref), custom_call_target="tpu_custom_call" | custom-call | flops 1000000000 | bytes 1000000 | tf_op jit(solution)/shard_map/pallas_call | solution.py:538
  11.9 0.6 %collective-permute-start.4 = (f32[136,256]{1,0:T(8,128)S(1)}, f32[136,256]{1,0:T(8,128)S(1)}, u32[]{:S(2)}, u32[]{:S(2)}) collective-permute-start(f32[136,256]{1,0:T(8,128)S(1)} %shard_map.75), channel_id=1, source_target_pairs={{0,16},{8,24},{16,0},{24,8},{1,17},{9,25},{17,1},{25,9},{2,18},{10... | collective-permute-start | bytes 417800 | tf_op jit(solution)/shard_map/ppermute | solution.py:575
  12.5 0.3 %shard_map.76 = f32[136,256]{1,0:T(8,128)S(1)} custom-call(bf16[528,2048]{1,0:T(8,128)(2,1)S(1)} %get-tuple-element.17.wave_ref, bf16[2048,256]{1,0:T(8,128)(2,1)S(1)} %get-tuple-element.25.grid_ref, f32[520,256]{1,0:T(8,128)S(1)} %get-tuple-element.26.vm_ref, f32[8,256]{1,0:T(8,128)S(1)} %collective-permute-done.2.edge_ref), custom_call_target="tpu_custom_call" | custom-call | flops 1000000000 | bytes 1000000 | tf_op jit(solution)/shard_map/pallas_call | solution.py:538
  12.8 0.1 collective-permute-start.5
  12.9 0.3 %shard_map.73.refs_0_ = f32[136,256]{1,0:T(8,128)S(1)} custom-call(bf16[528,2048]{1,0:T(8,128)(2,1)S(1)} %get-tuple-element.17.wave_ref, bf16[2048,256]{1,0:T(8,128)(2,1)S(1)} %get-tuple-element.25.grid_ref, f32[520,256]{1,0:T(8,128)S(1)} %get-tuple-element.26.vm_ref, f32[8,256]{1,0:T(8,128)S(1)} %collective-permute-done.2.edge_ref), custom_call_target="tpu_custom_call" | custom-call | flops 1000000000 | bytes 1000000 | tf_op jit(solution)/shard_map/pallas_call | solution.py:538
  13.3 2.3 %collective-permute-done.3.refs_1_ = f32[136,256]{1,0:T(8,128)S(1)} collective-permute-done((f32[136,256]{1,0:T(8,128)S(1)}, f32[136,256]{1,0:T(8,128)S(1)}, u32[]{:S(2)}, u32[]{:S(2)}) %collective-permute-start.3) | collective-permute-done | bytes 139296 | tf_op jit(solution)/shard_map/ppermute | solution.py:575
  15.6 2.5 %collective-permute-done.4.refs_2_ = f32[136,256]{1,0:T(8,128)S(1)} collective-permute-done((f32[136,256]{1,0:T(8,128)S(1)}, f32[136,256]{1,0:T(8,128)S(1)}, u32[]{:S(2)}, u32[]{:S(2)}) %collective-permute-start.4) | collective-permute-done | bytes 139296 | tf_op jit(solution)/shard_map/ppermute | solution.py:575
  18.1 0.0 collective-permute-done.5.refs_3_
  18.2 1.1 %smooth.1 = f32[8,32,128]{2,1,0:T(8,128)S(1)} custom-call(f32[136,256]{1,0:T(8,128)S(1)} %shard_map.73.refs_0_, f32[136,256]{1,0:T(8,128)S(1)} %collective-permute-done.3.refs_1_, f32[136,256]{1,0:T(8,128)S(1)} %collective-permute-done.4.refs_2_, f32[136,256]{1,0:T(8,128)S(1)} %collective-permute-done.5.refs_3_), custom_call_target="tpu_custom_call" | custom-call | tf_op jit(solution)/shard_map/smooth/pallas_call | solution.py:315
  19.3 8.5 %all_to_all.5 = f32[8,32,128]{2,1,0:T(8,128)S(1)} all-to-all(f32[8,32,128]{2,1,0:T(8,128)S(1)} %smooth.1), channel_id=1, replica_groups=mesh['ang'=4,'gy'=2,'gx'=4] {'gy','ang'}, dimensions={0} | all-to-all | bytes 262144 | tf_op jit(solution)/shard_map/all_to_all | solution.py:610
  27.8 0.7 %copy_bitcast_fusion = f32[4,8,1024]{2,1,0:T(8,128)} fusion(f32[8,32,128]{2,1,0:T(8,128)S(1)} %all_to_all.5), kind=kLoop, calls=%fused_computation | loop fusion | bytes 262144 | tf_op jit(solution)/shard_map/reshape | solution.py:612
  (1 shorter events, 0.0 us)
Async XLA Ops:
  1.4 5.1 %collective-permute-start = (f32[320,512]{1,0:T(8,128)S(1)}, f32[320,512]{1,0:T(8,128)S(1)}, u32[]{:S(2)}, u32[]{:S(2)}) collective-permute-start(f32[320,512]{1,0:T(8,128)S(1)} %get-tuple-element.20), channel_id=1, source_target_pairs={{0,4},{4,0},{1,5},{5,1},{2,6},{6,2},{3,7},{7,3},{8,12},{12,8},{9,1... | collective-permute-start | bytes 1966088 | tf_op jit(solution)/shard_map/ppermute | solution.py:557
  1.9 1.7 %collective-permute-start.1 = (f32[8,256]{1,0:T(8,128)S(1)}, f32[8,256]{1,0:T(8,128)S(1)}, u32[]{:S(2)}, u32[]{:S(2)}) collective-permute-start(f32[8,256]{1,0:T(8,128)S(1)} %get-tuple-element.28), channel_id=1, source_target_pairs={{0,4},{4,0},{1,5},{5,1},{2,6},{6,2},{3,7},{7,3},{8,12},{12,8},{9,1... | collective-permute-start | bytes 24584 | tf_op jit(solution)/shard_map/ppermute | solution.py:556
  3.7 4.5 %collective-permute-start.2 = (f32[8,256]{1,0:T(8,128)S(1)}, f32[8,256]{1,0:T(8,128)S(1)}, u32[]{:S(2)}, u32[]{:S(2)}) collective-permute-start(f32[8,256]{1,0:T(8,128)S(1)} %add.3), channel_id=1, source_target_pairs={{4,1},{1,4},{5,2},{2,5},{6,3},{3,6},{0,8},{7,15},{12,9},{9,12},{13... | collective-permute-start | bytes 24584 | tf_op jit(solution)/shard_map/ppermute | solution.py:569
  8.5 7.1 %collective-permute-start.3 = (f32[136,256]{1,0:T(8,128)S(1)}, f32[136,256]{1,0:T(8,128)S(1)}, u32[]{:S(2)}, u32[]{:S(2)}) collective-permute-start(f32[136,256]{1,0:T(8,128)S(1)} %shard_map.74), channel_id=1, source_target_pairs={{0,24},{8,16},{16,8},{24,0},{1,25},{9,17},{17,9},{25,1},{2,26},{10... | collective-permute-start | bytes 417800 | tf_op jit(solution)/shard_map/ppermute | solution.py:575
  11.9 6.3 %collective-permute-start.4 = (f32[136,256]{1,0:T(8,128)S(1)}, f32[136,256]{1,0:T(8,128)S(1)}, u32[]{:S(2)}, u32[]{:S(2)}) collective-permute-start(f32[136,256]{1,0:T(8,128)S(1)} %shard_map.75), channel_id=1, source_target_pairs={{0,16},{8,24},{16,0},{24,8},{1,17},{9,25},{17,1},{25,9},{2,18},{10... | collective-permute-start | bytes 417800 | tf_op jit(solution)/shard_map/ppermute | solution.py:575
  12.8 5.4 %collective-permute-start.5 = (f32[136,256]{1,0:T(8,128)S(1)}, f32[136,256]{1,0:T(8,128)S(1)}, u32[]{:S(2)}, u32[]{:S(2)}) collective-permute-start(f32[136,256]{1,0:T(8,128)S(1)} %shard_map.76), channel_id=1, source_target_pairs={{0,8},{8,0},{16,24},{24,16},{1,9},{9,1},{17,25},{25,17},{2,10},{10... | collective-permute-start | bytes 417800 | tf_op jit(solution)/shard_map/ppermute | solution.py:575

commit v9 on v8

--- a/solution.py
+++ b/solution.py
@@ -515,34 +515,55 @@
     )(data, own, got, spread)
 
 
-def block_kernel(apart, wave_ref, grid_ref, vm_ref, edge_ref, out_ref):
+def block_kernel(apart, wave_ref, grid_ref, vm_ref, *refs):
+    *edge_refs, out_ref = refs
     window = out_ref.shape[0]
-    block = window - 2 * HALO
-    angs = lax.axis_size("ang")
     dest = lax.axis_index("ang") ^ apart
-    gy = lax.axis_index("gy")
-    first = pl.multiple_of(dest * block, 16)
+    first = pl.multiple_of(dest * (window - 2 * HALO), 16)
     made = 16 * pl.cdiv(window, 16)
     total = jnp.dot(wave_ref[pl.ds(first, made), :], grid_ref[...], preferred_element_type=jnp.float32)
     out_ref[...] = vm_ref[pl.ds(first, window), :] - total[:window] * NX ** (-0.5)
+    if edge_refs:
+        add_edge(apart, edge_refs[0], out_ref, out_ref)
+
+
+def add_edge(apart, edge_ref, in_ref, out_ref):
+    window = out_ref.shape[0]
+    dest, gy = lax.axis_index("ang") ^ apart, lax.axis_index("gy")
     edge = edge_ref[...][:HALO]
     opens = jnp.logical_and(dest == 0, gy == 0)
-    out_ref[pl.ds(0, HALO), :] += jnp.where(opens, edge, 0.0)
-    closes = jnp.logical_and(dest == angs - 1, gy == 1)
-    out_ref[pl.ds(window - HALO, HALO), :] += jnp.where(closes, edge, 0.0)
-
-
-def block_of(apart, wave, grid, vm, got_edge):
+    closes = jnp.logical_and(dest == lax.axis_size("ang") - 1, gy == 1)
+    for at, here in ((pl.ds(0, HALO), opens), (pl.ds(window - HALO, HALO), closes)):
+        out_ref[at, :] = in_ref[at, :] + jnp.where(here, edge, 0.0)
+
+
+def join_kernel(apart, part_ref, edge_ref, out_ref):
+    add_edge(apart, edge_ref, part_ref, out_ref)
+
+
+def join(apart, part, got_edge):
+    vmem = pl.BlockSpec(memory_space=pltpu.VMEM)
+    return pl.pallas_call(
+        functools.partial(join_kernel, apart),
+        out_shape=pltpu.VMEM(part.shape, part.dtype),
+        in_specs=[vmem] * 2,
+        out_specs=vmem,
+        input_output_aliases={0: 0},
+        compiler_params=pltpu.CompilerParams(vmem_limit_bytes=VMEM_LIMIT),
+    )(part, got_edge)
+
+
+def block_of(apart, wave, grid, vm, *got_edge):
     window = (vm.shape[0] - 2 * HALO) // lax.axis_size("ang") + 2 * HALO
     vmem = pl.BlockSpec(memory_space=pltpu.VMEM)
     return pl.pallas_call(
         functools.partial(block_kernel, apart),
         out_shape=pltpu.VMEM((window, vm.shape[1]), jnp.float32),
-        in_specs=[vmem] * 4,
+        in_specs=[vmem] * (3 + len(got_edge)),
         out_specs=vmem,
         cost_estimate=pl.CostEstimate(flops=10**9, transcendentals=0, bytes_accessed=10**6),
         compiler_params=pltpu.CompilerParams(vmem_limit_bytes=VMEM_LIMIT),
-    )(wave, grid, vm, got_edge)
+    )(wave, grid, vm, *got_edge)
 
 
 def on_chip(*arrays):
@@ -571,7 +592,10 @@
     wave, gridded, vm, got_edge = on_chip(wave, gridded, vm, got_edge)
     parts = []
     for apart in range(angs - 1, 0, -1):
-        part = block_of(apart, wave, gridded, vm, got_edge)
+        if apart == angs - 1:
+            part = join(apart, *on_chip(block_of(apart, wave, gridded, vm), got_edge))
+        else:
+            part = block_of(apart, wave, gridded, vm, got_edge)
         parts.append(lax.ppermute(part, "ang", [(ang, ang ^ apart) for ang in range(angs)]))
     return [block_of(0, wave, gridded, vm, got_edge)] + parts
 

time: 28.6 us -> 28.2 us (0.986)
  waiting for transfers between devices: 6.57 us -> 6.24 us
    ppermute x1, waiting for transfers between devices: 0.83 us -> 0.5 us  [project_paired(): got_edge = lax.ppermute(near + near_got, ('ang', 'gy', 'gx'), route)]
  transfers between devices with their start and end apart: 6 -> 6, of which waited for: 4 -> 4; matrix products, arithmetic and copies ran while one was open for 0% -> 0% of each run, Pallas kernels for 9% -> 11%
where the time goes in v9:
time: 28.2 us; the launch traced here: 28 us
  blocking collectives  8.5 us (30%)
  starting transfers between devices  7.16 us (25%)
  waiting for transfers between devices  6.24 us (22%)
  Pallas kernels  5.42 us (19%)
  local copies, waits for them, and re-layouts  0.66 us (2%)
    all_to_all x1, blocking collectives, per_device(): done = lax.all_to_all(done, ('gy', 'ang'), split_axis=0, concat_axis=0)  8.5 us
    ppermute x3, waiting for transfers between devices, project_paired(): lax.ppermute(part, 'ang', [(ang, ang ^ apart) for ang in range(angs)])  4.93 us
    ppermute x3, starting transfers between devices, project_paired(): lax.ppermute(part, 'ang', [(ang, ang ^ apart) for ang in range(angs)])  3.68 us
    ppermute x1, starting transfers between devices, project_paired(): got_edge = lax.ppermute(near + near_got, ('ang', 'gy', 'gx'), route)  2.85 us
    pallas_call x1, Pallas kernels, pack(): pl.pallas_call(pack_kernel, out_shape=[pltpu.VMEM((rows + 2 * local_lines...  1.38 us
    pallas_call x4, Pallas kernels, block_of(): pl.pallas_call(functools.partial(block_kernel, apart), out_shape=pltpu.VM...  1.33 us
    pallas_call x1, Pallas kernels, smooth(): pl.pallas_call(functools.partial(smooth_kernel, planes, columns), out_sha...  1.08 us
    pallas_call x1, Pallas kernels, spread_of(): pl.pallas_call(make_spread, out_shape=pltpu.VMEM((block_size, taps.shape[...  0.84 us
  transfers between devices with their start and end apart: 6, of which 4 were waited for; matrix products, arithmetic and copies ran while one was open for 0% of the time, Pallas kernels for 11%

profile of v9, /device:TPU:0, one launch (start us, length us, event | category | flops | bytes accessed | tf_op | source)
XLA Modules:
  0.0 28.0 jit_solution(3918368715476232819)
XLA Ops:
  0.0 1.4 %pack.1 = (f32[320,512]{1,0:T(8,128)S(1)}, bf16[256,512]{1,0:T(8,128)(2,1)S(1)}, s32[4,128]{1,0:T(4,128)S(1)}, s32[4,128]{1,0:T(4,128)S(1)}, f32[4,512]{1,0:T(4,...) custom-call(bf16[256,512]{1,0:T(8,128)(2,1)} %bitcast.12, ...), custom_call_target="tpu_custom_call" | custom-call | tf_op jit(solution)/shard_map/pack/pallas_call | solution.py:412
  1.4 0.6 %collective-permute-start = (f32[320,512]{1,0:T(8,128)S(1)}, f32[320,512]{1,0:T(8,128)S(1)}, u32[]{:S(2)}, u32[]{:S(2)}) collective-permute-start(f32[320,512]{1,0:T(8,128)S(1)} %get-tuple-element.20), channel_id=1, source_target_pairs={{0,4},{4,0},{1,5},{5,1},{2,6},{6,2},{3,7},{7,3},{8,12},{12,8},{9,1... | collective-permute-start | bytes 1966088 | tf_op jit(solution)/shard_map/ppermute | solution.py:578
  1.9 0.1 collective-permute-start.1
  2.0 0.8 %spread.1.spread_ref = bf16[1024,512]{1,0:T(8,128)(2,1)S(1)} custom-call(s32[4,128]{1,0:T(4,128)S(1)} %get-tuple-element.21.offsets_ref, s32[4,128]{1,0:T(4,128)S(1)} %get-tuple-element.22.view_ref, f32[4,512]{1,0:T(4,128)S(1)} %get-tuple-element.23.taps_ref, f32[1500]{0:T(1024)S(1)} %get-tuple-element.24.weight_ref), custom_call_target="tpu_custom_call" | custom-call | flops 2000000000 | bytes 1000000 | tf_op jit(solution)/shard_map/spread/pallas_call | solution.py:451
  2.9 0.8 %collective-permute-done.1 = f32[8,256]{1,0:T(8,128)S(1)} collective-permute-done((f32[8,256]{1,0:T(8,128)S(1)}, f32[8,256]{1,0:T(8,128)S(1)}, u32[]{:S(2)}, u32[]{:S(2)}) %collective-permute-start.1) | collective-permute-done | bytes 8224 | tf_op jit(solution)/shard_map/ppermute | solution.py:577
  3.7 2.8 %collective-permute-start.2 = (f32[8,256]{1,0:T(8,128)S(1)}, f32[8,256]{1,0:T(8,128)S(1)}, u32[]{:S(2)}, u32[]{:S(2)}) collective-permute-start(f32[8,256]{1,0:T(8,128)S(1)} %add.3), channel_id=1, source_target_pairs={{4,1},{1,4},{5,2},{2,5},{6,3},{3,6},{0,8},{7,15},{12,9},{9,12},{13... | collective-permute-start | bytes 24584 | tf_op jit(solution)/shard_map/ppermute | solution.py:590
  6.5 0.0 collective-permute-done.got_ref
  6.5 0.8 %grid.1 = (bf16[2048,256]{1,0:T(8,128)(2,1)S(1)}, f32[520,256]{1,0:T(8,128)S(1)}) custom-call(bf16[256,512]{1,0:T(8,128)(2,1)S(1)} %get-tuple-element.18.data_ref, f32[32,640]{1,0:T(8,128)S(1)} %get-tuple-element.19.own_ref, f32[320,512]{1,0:T(8,128)S(1)} %collective-permute-done.got_ref, bf16[1024,512]{1,0:T(8,128)(2,1)S(1)} %spread.1.spread_ref), custom_call_target="tpu_custom_call" | custom-call | flops 1000000000 | bytes 1000000 | tf_op jit(solution)/shard_map/grid/pallas_call | solution.py:500
  7.3 0.3 %shard_map.74.part_ref = f32[136,256]{1,0:T(8,128)S(1)} custom-call(bf16[528,2048]{1,0:T(8,128)(2,1)S(1)} %get-tuple-element.17.wave_ref, bf16[2048,256]{1,0:T(8,128)(2,1)S(1)} %get-tuple-element.25.grid_ref, f32[520,256]{1,0:T(8,128)S(1)} %get-tuple-element.26.vm_ref), custom_call_target="tpu_custom_call" | custom-call | flops 1000000000 | bytes 1000000 | tf_op jit(solution)/shard_map/pallas_call | solution.py:559
  7.7 0.5 %collective-permute-done.2.refs_0_.edge_ref = f32[8,256]{1,0:T(8,128)S(1)} collective-permute-done((f32[8,256]{1,0:T(8,128)S(1)}, f32[8,256]{1,0:T(8,128)S(1)}, u32[]{:S(2)}, u32[]{:S(2)}) %collective-permute-start.2) | collective-permute-done | bytes 8224 | tf_op jit(solution)/shard_map/ppermute | solution.py:590
  8.2 3.0 %collective-permute-start.3 = (f32[136,256]{1,0:T(8,128)S(1)}, f32[136,256]{1,0:T(8,128)S(1)}, u32[]{:S(2)}, u32[]{:S(2)}) collective-permute-start(f32[136,256]{1,0:T(8,128)S(1)} %shard_map.75), channel_id=1, source_target_pairs={{0,24},{8,16},{16,8},{24,0},{1,25},{9,17},{17,9},{25,1},{2,26},{10... | collective-permute-start | bytes 417800 | tf_op jit(solution)/shard_map/ppermute | solution.py:599
  11.1 0.3 %shard_map.76 = f32[136,256]{1,0:T(8,128)S(1)} custom-call(bf16[528,2048]{1,0:T(8,128)(2,1)S(1)} %get-tuple-element.17.wave_ref, bf16[2048,256]{1,0:T(8,128)(2,1)S(1)} %get-tuple-element.25.grid_ref, f32[520,256]{1,0:T(8,128)S(1)} %get-tuple-element.26.vm_ref, f32[8,256]{1,0:T(8,128)S(1)} %collective-permute-done.2.refs_0_.edge_ref), custom_call_target="tpu_custom_call" | custom-call | flops 1000000000 | bytes 1000000 | tf_op jit(solution)/shard_map/pallas_call | solution.py:559
  11.5 0.6 %collective-permute-start.4 = (f32[136,256]{1,0:T(8,128)S(1)}, f32[136,256]{1,0:T(8,128)S(1)}, u32[]{:S(2)}, u32[]{:S(2)}) collective-permute-start(f32[136,256]{1,0:T(8,128)S(1)} %shard_map.76), channel_id=1, source_target_pairs={{0,16},{8,24},{16,0},{24,8},{1,17},{9,25},{17,1},{25,9},{2,18},{10... | collective-permute-start | bytes 417800 | tf_op jit(solution)/shard_map/ppermute | solution.py:599
  12.1 0.3 %shard_map.77 = f32[136,256]{1,0:T(8,128)S(1)} custom-call(bf16[528,2048]{1,0:T(8,128)(2,1)S(1)} %get-tuple-element.17.wave_ref, bf16[2048,256]{1,0:T(8,128)(2,1)S(1)} %get-tuple-element.25.grid_ref, f32[520,256]{1,0:T(8,128)S(1)} %get-tuple-element.26.vm_ref, f32[8,256]{1,0:T(8,128)S(1)} %collective-permute-done.2.refs_0_.edge_ref), custom_call_target="tpu_custom_call" | custom-call | flops 1000000000 | bytes 1000000 | tf_op jit(solution)/shard_map/pallas_call | solution.py:559
  12.4 0.1 collective-permute-start.5
  12.5 0.3 %shard_map.73.refs_0_ = f32[136,256]{1,0:T(8,128)S(1)} custom-call(bf16[528,2048]{1,0:T(8,128)(2,1)S(1)} %get-tuple-element.17.wave_ref, bf16[2048,256]{1,0:T(8,128)(2,1)S(1)} %get-tuple-element.25.grid_ref, f32[520,256]{1,0:T(8,128)S(1)} %get-tuple-element.26.vm_ref, f32[8,256]{1,0:T(8,128)S(1)} %collective-permute-done.2.refs_0_.edge_ref), custom_call_target="tpu_custom_call" | custom-call | flops 1000000000 | bytes 1000000 | tf_op jit(solution)/shard_map/pallas_call | solution.py:559
  12.9 2.3 %collective-permute-done.3.refs_1_ = f32[136,256]{1,0:T(8,128)S(1)} collective-permute-done((f32[136,256]{1,0:T(8,128)S(1)}, f32[136,256]{1,0:T(8,128)S(1)}, u32[]{:S(2)}, u32[]{:S(2)}) %collective-permute-start.3) | collective-permute-done | bytes 139296 | tf_op jit(solution)/shard_map/ppermute | solution.py:599
  15.2 2.5 %collective-permute-done.4.refs_2_ = f32[136,256]{1,0:T(8,128)S(1)} collective-permute-done((f32[136,256]{1,0:T(8,128)S(1)}, f32[136,256]{1,0:T(8,128)S(1)}, u32[]{:S(2)}, u32[]{:S(2)}) %collective-permute-start.4) | collective-permute-done | bytes 139296 | tf_op jit(solution)/shard_map/ppermute | solution.py:599
  17.7 0.0 collective-permute-done.5.refs_3_
  17.8 1.1 %smooth.1 = f32[8,32,128]{2,1,0:T(8,128)S(1)} custom-call(f32[136,256]{1,0:T(8,128)S(1)} %shard_map.73.refs_0_, f32[136,256]{1,0:T(8,128)S(1)} %collective-permute-done.3.refs_1_, f32[136,256]{1,0:T(8,128)S(1)} %collective-permute-done.4.refs_2_, f32[136,256]{1,0:T(8,128)S(1)} %collective-permute-done.5.refs_3_), custom_call_target="tpu_custom_call" | custom-call | tf_op jit(solution)/shard_map/smooth/pallas_call | solution.py:315
  18.9 8.5 %all_to_all.5 = f32[8,32,128]{2,1,0:T(8,128)S(1)} all-to-all(f32[8,32,128]{2,1,0:T(8,128)S(1)} %smooth.1), channel_id=1, replica_groups=mesh['ang'=4,'gy'=2,'gx'=4] {'gy','ang'}, dimensions={0} | all-to-all | bytes 262144 | tf_op jit(solution)/shard_map/all_to_all | solution.py:634
  27.4 0.7 %copy_bitcast_fusion = f32[4,8,1024]{2,1,0:T(8,128)} fusion(f32[8,32,128]{2,1,0:T(8,128)S(1)} %all_to_all.5), kind=kLoop, calls=%fused_computation | loop fusion | bytes 262144 | tf_op jit(solution)/shard_map/reshape | solution.py:636
  (2 shorter events, 0.0 us)
Async XLA Ops:
  1.4 5.1 %collective-permute-start = (f32[320,512]{1,0:T(8,128)S(1)}, f32[320,512]{1,0:T(8,128)S(1)}, u32[]{:S(2)}, u32[]{:S(2)}) collective-permute-start(f32[320,512]{1,0:T(8,128)S(1)} %get-tuple-element.20), channel_id=1, source_target_pairs={{0,4},{4,0},{1,5},{5,1},{2,6},{6,2},{3,7},{7,3},{8,12},{12,8},{9,1... | collective-permute-start | bytes 1966088 | tf_op jit(solution)/shard_map/ppermute | solution.py:578
  1.9 1.7 %collective-permute-start.1 = (f32[8,256]{1,0:T(8,128)S(1)}, f32[8,256]{1,0:T(8,128)S(1)}, u32[]{:S(2)}, u32[]{:S(2)}) collective-permute-start(f32[8,256]{1,0:T(8,128)S(1)} %get-tuple-element.28), channel_id=1, source_target_pairs={{0,4},{4,0},{1,5},{5,1},{2,6},{6,2},{3,7},{7,3},{8,12},{12,8},{9,1... | collective-permute-start | bytes 24584 | tf_op jit(solution)/shard_map/ppermute | solution.py:577
  3.7 4.5 %collective-permute-start.2 = (f32[8,256]{1,0:T(8,128)S(1)}, f32[8,256]{1,0:T(8,128)S(1)}, u32[]{:S(2)}, u32[]{:S(2)}) collective-permute-start(f32[8,256]{1,0:T(8,128)S(1)} %add.3), channel_id=1, source_target_pairs={{4,1},{1,4},{5,2},{2,5},{6,3},{3,6},{0,8},{7,15},{12,9},{9,12},{13... | collective-permute-start | bytes 24584 | tf_op jit(solution)/shard_map/ppermute | solution.py:590
  8.2 7.0 %collective-permute-start.3 = (f32[136,256]{1,0:T(8,128)S(1)}, f32[136,256]{1,0:T(8,128)S(1)}, u32[]{:S(2)}, u32[]{:S(2)}) collective-permute-start(f32[136,256]{1,0:T(8,128)S(1)} %shard_map.75), channel_id=1, source_target_pairs={{0,24},{8,16},{16,8},{24,0},{1,25},{9,17},{17,9},{25,1},{2,26},{10... | collective-permute-start | bytes 417800 | tf_op jit(solution)/shard_map/ppermute | solution.py:599
  11.5 6.3 %collective-permute-start.4 = (f32[136,256]{1,0:T(8,128)S(1)}, f32[136,256]{1,0:T(8,128)S(1)}, u32[]{:S(2)}, u32[]{:S(2)}) collective-permute-start(f32[136,256]{1,0:T(8,128)S(1)} %shard_map.76), channel_id=1, source_target_pairs={{0,16},{8,24},{16,0},{24,8},{1,17},{9,25},{17,1},{25,9},{2,18},{10... | collective-permute-start | bytes 417800 | tf_op jit(solution)/shard_map/ppermute | solution.py:599
  12.4 5.4 %collective-permute-start.5 = (f32[136,256]{1,0:T(8,128)S(1)}, f32[136,256]{1,0:T(8,128)S(1)}, u32[]{:S(2)}, u32[]{:S(2)}) collective-permute-start(f32[136,256]{1,0:T(8,128)S(1)} %shard_map.77), channel_id=1, source_target_pairs={{0,8},{8,0},{16,24},{24,16},{1,9},{9,1},{17,25},{25,17},{2,10},{10... | collective-permute-start | bytes 417800 | tf_op jit(solution)/shard_map/ppermute | solution.py:599

commit v10 on v9

--- a/solution.py
+++ b/solution.py
@@ -354,9 +354,9 @@
     gx, gy = lax.axis_index("gx"), lax.axis_index("gy")
     first_core = gy == 0
     pairs = (
+        (data_ref, data_out),
         (volume_ref, volume_here),
         (multiplier_ref, multiplier_here),
-        (data_ref, data_out),
         (offsets_ref, offsets_out),
         (view_ref, view_out),
         (taps_ref, taps_out),
@@ -377,8 +377,9 @@
 
         make_waves(base, part, count, *angles, put)
 
-    copies[0].wait()
-    copies[1].wait()
+    for copy in copies:
+        copy.wait()
+    sent_ref[pl.ds(0, rows), :] = data_out[...].astype(jnp.float32)
     low = volume_here[:, pl.ds(0, half)] + multiplier_here[:, pl.ds(0, half)]
     high = volume_here[:, pl.ds(half, half)] + multiplier_here[:, pl.ds(half, half)]
     outer = (low[:, :HALO], high[:, half - HALO :])
@@ -396,10 +397,6 @@
     own_ref[:, pl.ds(half, HALO)] = jnp.where(first_core, above, below)
     sent_ref[pl.ds(rows, local_lines), :] = jnp.where(first_core, high, low)
     sent_ref[pl.ds(rows + local_lines, local_lines), pl.ds(0, HALO)] = jnp.where(first_core, below, above)
-    copies[2].wait()
-    sent_ref[pl.ds(0, rows), :] = data_out[...].astype(jnp.float32)
-    for copy in copies[3:]:
-        copy.wait()
 
 
 def pack(data, offsets, view_index, taps, view_weight, volume, multiplier):

time: 28.2 us -> 28.3 us (level)
  transfers between devices with their start and end apart: 6 -> 6, of which waited for: 4 -> 4; matrix products, arithmetic and copies ran while one was open for 0% -> 0% of each run, Pallas kernels for 11% -> 10%
where the time goes in v10:
time: 28.3 us; the launch traced here: 28.1 us
  blocking collectives  8.5 us (30%)
  starting transfers between devices  7.17 us (25%)
  waiting for transfers between devices  6.24 us (22%)
  Pallas kernels  5.45 us (19%)
  local copies, waits for them, and re-layouts  0.66 us (2%)
    all_to_all x1, blocking collectives, per_device(): done = lax.all_to_all(done, ('gy', 'ang'), split_axis=0, concat_axis=0)  8.5 us
    ppermute x3, waiting for transfers between devices, project_paired(): lax.ppermute(part, 'ang', [(ang, ang ^ apart) for ang in range(angs)])  4.92 us
    ppermute x3, starting transfers between devices, project_paired(): lax.ppermute(part, 'ang', [(ang, ang ^ apart) for ang in range(angs)])  3.69 us
    ppermute x1, starting transfers between devices, project_paired(): got_edge = lax.ppermute(near + near_got, ('ang', 'gy', 'gx'), route)  2.85 us
    pallas_call x1, Pallas kernels, pack(): pl.pallas_call(pack_kernel, out_shape=[pltpu.VMEM((rows + 2 * local_lines...  1.42 us
    pallas_call x4, Pallas kernels, block_of(): pl.pallas_call(functools.partial(block_kernel, apart), out_shape=pltpu.VM...  1.32 us
    pallas_call x1, Pallas kernels, smooth(): pl.pallas_call(functools.partial(smooth_kernel, planes, columns), out_sha...  1.08 us
    pallas_call x1, Pallas kernels, spread_of(): pl.pallas_call(make_spread, out_shape=pltpu.VMEM((block_size, taps.shape[...  0.84 us
  transfers between devices with their start and end apart: 6, of which 4 were waited for; matrix products, arithmetic and copies ran while one was open for 0% of the time, Pallas kernels for 10%

profile of v10, /device:TPU:0, one launch (start us, length us, event | category | flops | bytes accessed | tf_op | source)
XLA Modules:
  0.0 28.1 jit_solution(6956354708214954563)
XLA Ops:
  0.0 1.4 %pack.1 = (f32[320,512]{1,0:T(8,128)S(1)}, bf16[256,512]{1,0:T(8,128)(2,1)S(1)}, s32[4,128]{1,0:T(4,128)S(1)}, s32[4,128]{1,0:T(4,128)S(1)}, f32[4,512]{1,0:T(4,...) custom-call(bf16[256,512]{1,0:T(8,128)(2,1)} %bitcast.12, ...), custom_call_target="tpu_custom_call" | custom-call | tf_op jit(solution)/shard_map/pack/pallas_call | solution.py:409
  1.4 0.6 %collective-permute-start = (f32[320,512]{1,0:T(8,128)S(1)}, f32[320,512]{1,0:T(8,128)S(1)}, u32[]{:S(2)}, u32[]{:S(2)}) collective-permute-start(f32[320,512]{1,0:T(8,128)S(1)} %get-tuple-element.20), channel_id=1, source_target_pairs={{0,4},{4,0},{1,5},{5,1},{2,6},{6,2},{3,7},{7,3},{8,12},{12,8},{9,1... | collective-permute-start | bytes 1966088 | tf_op jit(solution)/shard_map/ppermute | solution.py:575
  2.0 0.1 collective-permute-start.1
  2.1 0.8 %spread.1.spread_ref = bf16[1024,512]{1,0:T(8,128)(2,1)S(1)} custom-call(s32[4,128]{1,0:T(4,128)S(1)} %get-tuple-element.21.offsets_ref, s32[4,128]{1,0:T(4,128)S(1)} %get-tuple-element.22.view_ref, f32[4,512]{1,0:T(4,128)S(1)} %get-tuple-element.23.taps_ref, f32[1500]{0:T(1024)S(1)} %get-tuple-element.24.weight_ref), custom_call_target="tpu_custom_call" | custom-call | flops 2000000000 | bytes 1000000 | tf_op jit(solution)/shard_map/spread/pallas_call | solution.py:448
  2.9 0.8 %collective-permute-done.1 = f32[8,256]{1,0:T(8,128)S(1)} collective-permute-done((f32[8,256]{1,0:T(8,128)S(1)}, f32[8,256]{1,0:T(8,128)S(1)}, u32[]{:S(2)}, u32[]{:S(2)}) %collective-permute-start.1) | collective-permute-done | bytes 8224 | tf_op jit(solution)/shard_map/ppermute | solution.py:574
  3.7 2.8 %collective-permute-start.2 = (f32[8,256]{1,0:T(8,128)S(1)}, f32[8,256]{1,0:T(8,128)S(1)}, u32[]{:S(2)}, u32[]{:S(2)}) collective-permute-start(f32[8,256]{1,0:T(8,128)S(1)} %add.3), channel_id=1, source_target_pairs={{4,1},{1,4},{5,2},{2,5},{6,3},{3,6},{0,8},{7,15},{12,9},{9,12},{13... | collective-permute-start | bytes 24584 | tf_op jit(solution)/shard_map/ppermute | solution.py:587
  6.6 0.0 collective-permute-done.got_ref
  6.6 0.8 %grid.1 = (bf16[2048,256]{1,0:T(8,128)(2,1)S(1)}, f32[520,256]{1,0:T(8,128)S(1)}) custom-call(bf16[256,512]{1,0:T(8,128)(2,1)S(1)} %get-tuple-element.18.data_ref, f32[32,640]{1,0:T(8,128)S(1)} %get-tuple-element.19.own_ref, f32[320,512]{1,0:T(8,128)S(1)} %collective-permute-done.got_ref, bf16[1024,512]{1,0:T(8,128)(2,1)S(1)} %spread.1.spread_ref), custom_call_target="tpu_custom_call" | custom-call | flops 1000000000 | bytes 1000000 | tf_op jit(solution)/shard_map/grid/pallas_call | solution.py:497
  7.4 0.3 %shard_map.74.part_ref = f32[136,256]{1,0:T(8,128)S(1)} custom-call(bf16[528,2048]{1,0:T(8,128)(2,1)S(1)} %get-tuple-element.17.wave_ref, bf16[2048,256]{1,0:T(8,128)(2,1)S(1)} %get-tuple-element.25.grid_ref, f32[520,256]{1,0:T(8,128)S(1)} %get-tuple-element.26.vm_ref), custom_call_target="tpu_custom_call" | custom-call | flops 1000000000 | bytes 1000000 | tf_op jit(solution)/shard_map/pallas_call | solution.py:556
  7.7 0.5 %collective-permute-done.2.refs_0_.edge_ref = f32[8,256]{1,0:T(8,128)S(1)} collective-permute-done((f32[8,256]{1,0:T(8,128)S(1)}, f32[8,256]{1,0:T(8,128)S(1)}, u32[]{:S(2)}, u32[]{:S(2)}) %collective-permute-start.2) | collective-permute-done | bytes 8224 | tf_op jit(solution)/shard_map/ppermute | solution.py:587
  8.2 3.0 %collective-permute-start.3 = (f32[136,256]{1,0:T(8,128)S(1)}, f32[136,256]{1,0:T(8,128)S(1)}, u32[]{:S(2)}, u32[]{:S(2)}) collective-permute-start(f32[136,256]{1,0:T(8,128)S(1)} %shard_map.75), channel_id=1, source_target_pairs={{0,24},{8,16},{16,8},{24,0},{1,25},{9,17},{17,9},{25,1},{2,26},{10... | collective-permute-start | bytes 417800 | tf_op jit(solution)/shard_map/ppermute | solution.py:596
  11.2 0.3 %shard_map.76 = f32[136,256]{1,0:T(8,128)S(1)} custom-call(bf16[528,2048]{1,0:T(8,128)(2,1)S(1)} %get-tuple-element.17.wave_ref, bf16[2048,256]{1,0:T(8,128)(2,1)S(1)} %get-tuple-element.25.grid_ref, f32[520,256]{1,0:T(8,128)S(1)} %get-tuple-element.26.vm_ref, f32[8,256]{1,0:T(8,128)S(1)} %collective-permute-done.2.refs_0_.edge_ref), custom_call_target="tpu_custom_call" | custom-call | flops 1000000000 | bytes 1000000 | tf_op jit(solution)/shard_map/pallas_call | solution.py:556
  11.5 0.6 %collective-permute-start.4 = (f32[136,256]{1,0:T(8,128)S(1)}, f32[136,256]{1,0:T(8,128)S(1)}, u32[]{:S(2)}, u32[]{:S(2)}) collective-permute-start(f32[136,256]{1,0:T(8,128)S(1)} %shard_map.76), channel_id=1, source_target_pairs={{0,16},{8,24},{16,0},{24,8},{1,17},{9,25},{17,1},{25,9},{2,18},{10... | collective-permute-start | bytes 417800 | tf_op jit(solution)/shard_map/ppermute | solution.py:596
  12.1 0.3 %shard_map.77 = f32[136,256]{1,0:T(8,128)S(1)} custom-call(bf16[528,2048]{1,0:T(8,128)(2,1)S(1)} %get-tuple-element.17.wave_ref, bf16[2048,256]{1,0:T(8,128)(2,1)S(1)} %get-tuple-element.25.grid_ref, f32[520,256]{1,0:T(8,128)S(1)} %get-tuple-element.26.vm_ref, f32[8,256]{1,0:T(8,128)S(1)} %collective-permute-done.2.refs_0_.edge_ref), custom_call_target="tpu_custom_call" | custom-call | flops 1000000000 | bytes 1000000 | tf_op jit(solution)/shard_map/pallas_call | solution.py:556
  12.4 0.1 collective-permute-start.5
  12.6 0.3 %shard_map.73.refs_0_ = f32[136,256]{1,0:T(8,128)S(1)} custom-call(bf16[528,2048]{1,0:T(8,128)(2,1)S(1)} %get-tuple-element.17.wave_ref, bf16[2048,256]{1,0:T(8,128)(2,1)S(1)} %get-tuple-element.25.grid_ref, f32[520,256]{1,0:T(8,128)S(1)} %get-tuple-element.26.vm_ref, f32[8,256]{1,0:T(8,128)S(1)} %collective-permute-done.2.refs_0_.edge_ref), custom_call_target="tpu_custom_call" | custom-call | flops 1000000000 | bytes 1000000 | tf_op jit(solution)/shard_map/pallas_call | solution.py:556
  12.9 2.3 %collective-permute-done.3.refs_1_ = f32[136,256]{1,0:T(8,128)S(1)} collective-permute-done((f32[136,256]{1,0:T(8,128)S(1)}, f32[136,256]{1,0:T(8,128)S(1)}, u32[]{:S(2)}, u32[]{:S(2)}) %collective-permute-start.3) | collective-permute-done | bytes 139296 | tf_op jit(solution)/shard_map/ppermute | solution.py:596
  15.2 2.5 %collective-permute-done.4.refs_2_ = f32[136,256]{1,0:T(8,128)S(1)} collective-permute-done((f32[136,256]{1,0:T(8,128)S(1)}, f32[136,256]{1,0:T(8,128)S(1)}, u32[]{:S(2)}, u32[]{:S(2)}) %collective-permute-start.4) | collective-permute-done | bytes 139296 | tf_op jit(solution)/shard_map/ppermute | solution.py:596
  17.8 0.0 collective-permute-done.5.refs_3_
  17.8 1.1 %smooth.1 = f32[8,32,128]{2,1,0:T(8,128)S(1)} custom-call(f32[136,256]{1,0:T(8,128)S(1)} %shard_map.73.refs_0_, f32[136,256]{1,0:T(8,128)S(1)} %collective-permute-done.3.refs_1_, f32[136,256]{1,0:T(8,128)S(1)} %collective-permute-done.4.refs_2_, f32[136,256]{1,0:T(8,128)S(1)} %collective-permute-done.5.refs_3_), custom_call_target="tpu_custom_call" | custom-call | tf_op jit(solution)/shard_map/smooth/pallas_call | solution.py:315
  18.9 8.5 %all_to_all.5 = f32[8,32,128]{2,1,0:T(8,128)S(1)} all-to-all(f32[8,32,128]{2,1,0:T(8,128)S(1)} %smooth.1), channel_id=1, replica_groups=mesh['ang'=4,'gy'=2,'gx'=4] {'gy','ang'}, dimensions={0} | all-to-all | bytes 262144 | tf_op jit(solution)/shard_map/all_to_all | solution.py:631
  27.4 0.7 %copy_bitcast_fusion = f32[4,8,1024]{2,1,0:T(8,128)} fusion(f32[8,32,128]{2,1,0:T(8,128)S(1)} %all_to_all.5), kind=kLoop, calls=%fused_computation | loop fusion | bytes 262144 | tf_op jit(solution)/shard_map/reshape | solution.py:633
  (2 shorter events, 0.0 us)
Async XLA Ops:
  1.4 5.1 %collective-permute-start = (f32[320,512]{1,0:T(8,128)S(1)}, f32[320,512]{1,0:T(8,128)S(1)}, u32[]{:S(2)}, u32[]{:S(2)}) collective-permute-start(f32[320,512]{1,0:T(8,128)S(1)} %get-tuple-element.20), channel_id=1, source_target_pairs={{0,4},{4,0},{1,5},{5,1},{2,6},{6,2},{3,7},{7,3},{8,12},{12,8},{9,1... | collective-permute-start | bytes 1966088 | tf_op jit(solution)/shard_map/ppermute | solution.py:575
  2.0 1.7 %collective-permute-start.1 = (f32[8,256]{1,0:T(8,128)S(1)}, f32[8,256]{1,0:T(8,128)S(1)}, u32[]{:S(2)}, u32[]{:S(2)}) collective-permute-start(f32[8,256]{1,0:T(8,128)S(1)} %get-tuple-element.28), channel_id=1, source_target_pairs={{0,4},{4,0},{1,5},{5,1},{2,6},{6,2},{3,7},{7,3},{8,12},{12,8},{9,1... | collective-permute-start | bytes 24584 | tf_op jit(solution)/shard_map/ppermute | solution.py:574
  3.7 4.5 %collective-permute-start.2 = (f32[8,256]{1,0:T(8,128)S(1)}, f32[8,256]{1,0:T(8,128)S(1)}, u32[]{:S(2)}, u32[]{:S(2)}) collective-permute-start(f32[8,256]{1,0:T(8,128)S(1)} %add.3), channel_id=1, source_target_pairs={{4,1},{1,4},{5,2},{2,5},{6,3},{3,6},{0,8},{7,15},{12,9},{9,12},{13... | collective-permute-start | bytes 24584 | tf_op jit(solution)/shard_map/ppermute | solution.py:587
  8.2 7.0 %collective-permute-start.3 = (f32[136,256]{1,0:T(8,128)S(1)}, f32[136,256]{1,0:T(8,128)S(1)}, u32[]{:S(2)}, u32[]{:S(2)}) collective-permute-start(f32[136,256]{1,0:T(8,128)S(1)} %shard_map.75), channel_id=1, source_target_pairs={{0,24},{8,16},{16,8},{24,0},{1,25},{9,17},{17,9},{25,1},{2,26},{10... | collective-permute-start | bytes 417800 | tf_op jit(solution)/shard_map/ppermute | solution.py:596
  11.5 6.3 %collective-permute-start.4 = (f32[136,256]{1,0:T(8,128)S(1)}, f32[136,256]{1,0:T(8,128)S(1)}, u32[]{:S(2)}, u32[]{:S(2)}) collective-permute-start(f32[136,256]{1,0:T(8,128)S(1)} %shard_map.76), channel_id=1, source_target_pairs={{0,16},{8,24},{16,0},{24,8},{1,17},{9,25},{17,1},{25,9},{2,18},{10... | collective-permute-start | bytes 417800 | tf_op jit(solution)/shard_map/ppermute | solution.py:596
  12.4 5.4 %collective-permute-start.5 = (f32[136,256]{1,0:T(8,128)S(1)}, f32[136,256]{1,0:T(8,128)S(1)}, u32[]{:S(2)}, u32[]{:S(2)}) collective-permute-start(f32[136,256]{1,0:T(8,128)S(1)} %shard_map.77), channel_id=1, source_target_pairs={{0,8},{8,0},{16,24},{24,16},{1,9},{9,1},{17,25},{25,17},{2,10},{10... | collective-permute-start | bytes 417800 | tf_op jit(solution)/shard_map/ppermute | solution.py:596
